TPU v7x, 32 devices: a whole 2x2x4 slice. The times are simulated.
32 devices in a mesh: utt: 4 (over z), tm: 8 (over y, x, core).
Axes of the slice: x: 2, y: 2, z: 4, core: 2. Of those that a mesh axis runs over, the one named last changes fastest.
Arguments:
- inputs: bfloat16 [4, 8192, 512], P('utt', 'tm'), may hold values from -6 to 6
- cotangent: bfloat16 [4, 8192, 512], P('utt', 'tm'), may hold values from -6 to 6
- frame_mask: int32 [4, 8192], P('utt', 'tm'), may hold values from 0 to 1, as said below
- slot_lengths: int32 [4, 4], P('utt'), may hold values from 1024 to 3072, as said below
- decays: float32 [4, 8, 8192], P('utt', None, 'tm'), may hold values from 0.0005 to 1
- tile_slots: int32 [22], replicated, may hold values from 0 to 31, as said below
- master_weight_tiles: float32 [2048, 8, 512], P(('utt', 'tm')), may hold values from -6 to 6
- tile_first: float32 [2048, 8, 512], P(('utt', 'tm'))
- tile_second: float32 [2048, 8, 512], P(('utt', 'tm'))
- vector_master: float32 [27, 512], replicated
- vector_first: float32 [27, 512], replicated
- vector_second: float32 [27, 512], replicated
Outputs:
- output: bfloat16 [4, 8192, 512], P('utt', 'tm')
- grad_input: float32 [4, 8192, 512], P('utt', 'tm')
- new_tile_master: float32 [2048, 8, 512], P(('utt', 'tm'))
- new_tile_first: float32 [2048, 8, 512], P(('utt', 'tm'))
- new_tile_second: float32 [2048, 8, 512], P(('utt', 'tm'))
- tile_copy: bfloat16 [2048, 8, 512], P(('utt', 'tm'))
- new_vector_master: float32 [27, 512], replicated
- new_vector_first: float32 [27, 512], replicated
- new_vector_second: float32 [27, 512], replicated
Inputs may be any that keep to these rules, and one draw needn't show every extreme that they name: `slot_lengths`: the 4 slots of a group lie end to end in order and fill its 8192 frames; every group has a slot of 3072 frames and one of 1024. `frame_mask`: within each slot the 1s come first and cover at least three quarters of it; every group has a slot that is 1 throughout and one that is not. `tile_slots`: 22 distinct slots; slot s belongs to the owner s // 8; every slot of some owner is used.
All inputs are finite; a program needn't handle non-finite values.
Results may differ from a plain program's by a relative error of at most 0.015.
Values may be sent and summed in bfloat16 or wider, within the bound.
A program may use at most 256 MiB of HBM per device.

v0:
```python
import jax
import jax.numpy as jnp
from jax import lax
from jax.sharding import PartitionSpec as P

D = 512
FF = 2048
H = 8
NS = 32
K = 15
BLK = 512
STEP = 7
P_SIZE = 64


NORM_EPS = 1e-05
ADAM_EPS = 1e-08
BETA_ONE = 0.9
BETA_TWO = 0.999
RATE_TILES = 0.04
RATE_VECTORS = 0.1
DECAY_TILES = 0.1
PRECISE = lax.Precision.HIGHEST


def entering_2(shard, axis, join, neutral, backward):
    count = lax.axis_size(axis)
    place = lax.axis_index(axis)
    ahead = count - 1 - place if backward else place
    gathered = jax.tree.map(
        lambda a, kind: lax.all_gather(a.astype(kind), axis), shard, (jnp.bfloat16, jnp.bfloat16)
    )
    state = jax.tree.map(lambda a, e: jnp.zeros_like(a) + jnp.asarray(e, a.dtype), shard, neutral)

    def one(lap, state):
        source = count - 1 - lap if backward else lap
        return join(
            state,
            jax.tree.map(
                lambda a, own: lax.dynamic_index_in_dim(a, source, 0, False).astype(own.dtype),
                gathered,
                shard,
            ),
        )

    return lax.fori_loop(0, ahead, one, state)


def padded_2(cells, sides, width):
    for axis, dim in sides:
        count = lax.axis_size(axis)
        ends = count - 1
        head = lax.slice_in_dim(cells, 0, width, axis=dim)
        tail = lax.slice_in_dim(cells, cells.shape[dim] - width, cells.shape[dim], axis=dim)
        cells = jnp.concatenate(
            [
                lax.ppermute(tail, axis, [(i, (i + 1) % count) for i in range(ends)]),
                cells,
                lax.ppermute(head, axis, [((i + 1) % count, i) for i in range(ends)]),
            ],
            axis=dim,
        )
    return cells


def product(matrix_a, matrix_b):
    return jnp.dot(matrix_a, matrix_b, preferred_element_type=jnp.float32)


def weight_grad(activations, gradients):
    return lax.dot_general(
        activations, gradients, (((0,), (0,)), ((), ())), preferred_element_type=jnp.float32
    )


def input_grad(gradients, weights):
    return lax.dot_general(
        gradients, weights, (((1,), (1,)), ((), ())), preferred_element_type=jnp.float32
    )


def layer_norm(values, norm_gain, norm_shift):
    centered = values - jnp.mean(values, axis=-1, keepdims=True)
    inverse_dev = lax.rsqrt(jnp.mean(centered * centered, axis=-1, keepdims=True) + NORM_EPS)
    normed = centered * inverse_dev
    return (normed * norm_gain + norm_shift, normed, inverse_dev)


def norm_grad(gradients, normed, inverse_dev, norm_gain):
    scaled = gradients * norm_gain
    middle = (
        scaled
        - jnp.mean(scaled, axis=-1, keepdims=True)
        - normed * jnp.mean(scaled * normed, axis=-1, keepdims=True)
    )
    return (middle * inverse_dev, jnp.sum(gradients * normed, axis=0), jnp.sum(gradients, axis=0))


def swish_slope(pre_act):
    sigmoid_of = jax.nn.sigmoid(pre_act)
    return sigmoid_of * (1.0 + pre_act * (1.0 - sigmoid_of))


def split_tiles(tile_values):
    blocks_ff = FF // D
    offset = 2 * blocks_ff
    up_first = tile_values[0:blocks_ff].transpose(1, 0, 2).reshape(D, FF)
    down_first = tile_values[blocks_ff:offset].reshape(FF, D)
    mixers = [tile_values[offset + number] for number in range(6)]
    up_second = tile_values[offset + 6 : offset + 6 + blocks_ff].transpose(1, 0, 2).reshape(D, FF)
    down_second = tile_values[offset + 6 + blocks_ff : offset + 6 + 2 * blocks_ff].reshape(FF, D)
    return (up_first, down_first, mixers, up_second, down_second)


def column_tiles(full_grad):
    blocks_ff = FF // D
    return full_grad.reshape(D, blocks_ff, D).transpose(1, 0, 2)


def ffn_forward(start_x, up_weight, down_weight, norm_gain, norm_shift):
    normed_out, normed, inverse_dev = layer_norm(start_x, norm_gain, norm_shift)
    normed_low = normed_out.astype(jnp.bfloat16)
    hidden = product(normed_low, up_weight)
    activated = (hidden * jax.nn.sigmoid(hidden)).astype(jnp.bfloat16)
    return (
        start_x + 0.5 * product(activated, down_weight),
        (normed, inverse_dev, normed_low, hidden, activated),
    )


def ffn_backward(grad_after, kept, up_weight, down_weight, norm_gain):
    normed, inverse_dev, normed_low, hidden, activated = kept
    down_in = (0.5 * grad_after).astype(jnp.bfloat16)
    grad_down = weight_grad(activated, down_in)
    hidden_grad = (input_grad(down_in, down_weight) * swish_slope(hidden)).astype(jnp.bfloat16)
    grad_up = weight_grad(normed_low, hidden_grad)
    grad_normed, gain_grad, shift_grad = norm_grad(
        input_grad(hidden_grad, up_weight), normed, inverse_dev, norm_gain
    )
    return (grad_after + grad_normed, grad_up, grad_down, gain_grad, shift_grad)


def block_weights(log_piece, seg_piece, seg_prior):
    cumulative = jnp.cumsum(log_piece, axis=1)
    row_index = jnp.arange(seg_piece.shape[0], dtype=jnp.int32)
    allowed = (seg_piece[:, None] == seg_piece[None, :]) & (
        row_index[:, None] >= row_index[None, :]
    )
    exponent = jnp.where(allowed[None], cumulative[:, :, None] - cumulative[:, None, :], 0.0)
    within = jnp.where(allowed[None], jnp.exp(exponent), 0.0)
    entering = jnp.where((seg_piece == seg_prior)[None, :], jnp.exp(cumulative), 0.0)
    leaving = jnp.where(
        (seg_piece == seg_piece[-1])[None, :], jnp.exp(cumulative[:, -1:] - cumulative), 0.0
    )
    return (within, entering, leaving)


def chain_states(earlier, latter):
    return (latter[0] * earlier[0], latter[0][:, None, None] * earlier[1] + latter[1])


def adam_step(master, first_old, second, gradient, step_rate, decay_rate):
    first_new = BETA_ONE * first_old + (1.0 - BETA_ONE) * gradient
    second_new = BETA_TWO * second + (1.0 - BETA_TWO) * gradient * gradient
    first_hat = first_new / (1.0 - BETA_ONE**STEP)
    second_hat = second_new / (1.0 - BETA_TWO**STEP)
    master_new = master - step_rate * (
        first_hat / (jnp.sqrt(second_hat) + ADAM_EPS) + decay_rate * master
    )
    return (master_new, first_new, second_new)


def local(
    inputs,
    cotangent,
    frame_mask,
    slot_lengths,
    decays,
    tile_slots,
    master_weight_tiles,
    tile_first,
    tile_second,
    vector_master,
    vector_first,
    vector_second,
):
    low_master = master_weight_tiles.astype(jnp.bfloat16)
    gathered = lax.all_gather(low_master, ("utt", "tm"), axis=0, tiled=True)
    owners_count = gathered.shape[0] // D
    capacity = gathered.shape[1]
    grouped = gathered.reshape(owners_count, D, capacity, D)
    owner_of = tile_slots // capacity
    column_of = tile_slots % capacity
    tile_values = grouped[owner_of, :, column_of, :]
    up_first, down_first, mixers, up_second, down_second = split_tiles(tile_values)
    w_values, w_states, w_output, w_linear, w_gate, w_project = mixers
    norm_gains = vector_master[0:6]
    norm_shifts = vector_master[6:12]
    conv_taps = vector_master[12:]
    frames = inputs.shape[1]
    first_frame = lax.axis_index("tm") * frames
    starts = jnp.cumsum(slot_lengths[0]) - slot_lengths[0]

    def segment_of(positions):
        return jnp.sum((starts[None, :] <= positions[:, None]).astype(jnp.int32), axis=1) - 1

    positions = first_frame + jnp.arange(frames, dtype=jnp.int32)
    segments = segment_of(positions)
    seg_before = segment_of(jnp.reshape(first_frame - 1, (1,)))[0]
    log_decay = jnp.log(decays[0])
    start_x = inputs[0].astype(jnp.float32)
    after_a, kept_a = ffn_forward(start_x, up_first, down_first, norm_gains[0], norm_shifts[0])
    normed_b_out, unit_b, inverse_b = layer_norm(after_a, norm_gains[1], norm_shifts[1])
    low_b = normed_b_out.astype(jnp.bfloat16)
    live_mask = frame_mask[0].astype(jnp.bfloat16)[:, None]
    state_vals = (product(low_b, w_values).astype(jnp.bfloat16) * live_mask).reshape(
        frames, H, P_SIZE
    )
    key_query = product(low_b, w_states).astype(jnp.bfloat16)
    state_keys = key_query[:, : H * NS].reshape(frames, H, NS)
    state_query = key_query[:, H * NS :].reshape(frames, H, NS)
    keys_wide = state_keys.astype(jnp.float32)
    query_wide = state_query.astype(jnp.float32)
    vals_wide = state_vals.astype(jnp.float32)
    total_log = jnp.cumsum(log_decay, axis=1)
    tail_dev = jnp.where(
        (segments == segments[-1])[None, :], jnp.exp(total_log[:, -1:] - total_log), 0.0
    )
    local_state = jnp.einsum(
        "shn,shp->hnp", keys_wide * tail_dev.T[:, :, None], vals_wide, precision=PRECISE
    )
    carry_dev = jnp.where(segments[-1] == seg_before, jnp.exp(total_log[:, -1]), 0.0)
    identity = (jnp.ones((H,), jnp.float32), jnp.zeros((H, NS, P_SIZE), jnp.float32))
    entry_scale, entry_state = entering_2(
        (carry_dev, local_state), "tm", chain_states, identity, False
    )
    count_blocks = frames // BLK
    saved_blocks = []
    outputs = []
    run_state = entry_state
    for number in range(count_blocks):
        block_start = number * BLK
        rows_here = slice(block_start, block_start + BLK)
        if number == 0:
            seg_prior = seg_before
        else:
            seg_prior = segments[block_start - 1]
        within, entering, leaving = block_weights(
            log_decay[:, rows_here], segments[rows_here], seg_prior
        )
        scores = jnp.einsum(
            "thn,shn->hts",
            state_query[rows_here],
            state_keys[rows_here],
            preferred_element_type=jnp.float32,
        )
        mixed_low = (within * scores).astype(jnp.bfloat16)
        inner_part = jnp.einsum(
            "hts,shp->thp", mixed_low, state_vals[rows_here], preferred_element_type=jnp.float32
        )
        carried = jnp.einsum(
            "thn,hnp->thp",
            query_wide[rows_here] * entering.T[:, :, None],
            run_state,
            precision=PRECISE,
        )
        outputs.append(inner_part + carried)
        saved_blocks.append((within, entering, leaving, mixed_low, run_state))
        run_state = (
            jnp.einsum(
                "shn,shp->hnp",
                keys_wide[rows_here] * leaving.T[:, :, None],
                vals_wide[rows_here],
                precision=PRECISE,
            )
            + entering[:, -1][:, None, None] * run_state
        )
    low_y = jnp.concatenate(outputs, axis=0).reshape(frames, H * P_SIZE).astype(jnp.bfloat16)
    after_b = after_a + product(low_y, w_output)
    normed_c_out, unit_c, inverse_c = layer_norm(after_b, norm_gains[2], norm_shifts[2])
    low_c = normed_c_out.astype(jnp.bfloat16)
    part_lin = product(low_c, w_linear)
    part_gate = product(low_c, w_gate)
    gate_sigmoid = jax.nn.sigmoid(part_gate)
    glu_low = (part_lin * gate_sigmoid).astype(jnp.bfloat16)
    half_width = K // 2
    padded = padded_2(glu_low, (("tm", 0),), half_width)
    pad_positions = first_frame - half_width + jnp.arange(frames + 2 * half_width, dtype=jnp.int32)
    pad_segments = segment_of(pad_positions)
    tap_masks = [
        (pad_segments[kernel_offset : kernel_offset + frames] == segments).astype(jnp.float32)[
            :, None
        ]
        for kernel_offset in range(K)
    ]
    conv_sum = jnp.zeros((frames, D), jnp.float32)
    for kernel_offset in range(K):
        conv_sum = (
            conv_sum
            + conv_taps[kernel_offset]
            * padded[kernel_offset : kernel_offset + frames].astype(jnp.float32)
            * tap_masks[kernel_offset]
        )
    normed_d, unit_d, inverse_d = layer_norm(conv_sum, norm_gains[3], norm_shifts[3])
    low_d = (normed_d * jax.nn.sigmoid(normed_d)).astype(jnp.bfloat16)
    after_c = after_b + product(low_d, w_project)
    after_e, kept_e = ffn_forward(after_c, up_second, down_second, norm_gains[4], norm_shifts[4])
    final_out, unit_f, inverse_f = layer_norm(after_e, norm_gains[5], norm_shifts[5])
    output = final_out.astype(jnp.bfloat16)[None]
    grad_out = cotangent[0].astype(jnp.float32)
    grad_e, gain_f, shift_f = norm_grad(grad_out, unit_f, inverse_f, norm_gains[5])
    grad_c, grad_up_e, grad_down_e, gain_e, shift_e = ffn_backward(
        grad_e, kept_e, up_second, down_second, norm_gains[4]
    )
    project_in = grad_c.astype(jnp.bfloat16)
    grad_project = weight_grad(low_d, project_in)
    grad_swish = input_grad(project_in, w_project) * swish_slope(normed_d)
    grad_conv, gain_d, shift_d = norm_grad(grad_swish, unit_d, inverse_d, norm_gains[3])
    low_grad_conv = grad_conv.astype(jnp.bfloat16)
    grad_padded = padded_2(low_grad_conv, (("tm", 0),), half_width)
    grad_conv_wide = low_grad_conv.astype(jnp.float32)
    grad_glu = jnp.zeros((frames, D), jnp.float32)
    tap_grads = []
    for kernel_offset in range(K):
        back_start = 2 * half_width - kernel_offset
        grad_glu = (
            grad_glu
            + conv_taps[kernel_offset]
            * grad_padded[back_start : back_start + frames].astype(jnp.float32)
            * tap_masks[K - 1 - kernel_offset]
        )
        tap_grads.append(
            jnp.sum(
                grad_conv_wide
                * padded[kernel_offset : kernel_offset + frames].astype(jnp.float32)
                * tap_masks[kernel_offset],
                axis=0,
            )
        )
    grad_lin = (grad_glu * gate_sigmoid).astype(jnp.bfloat16)
    grad_gate = (grad_glu * part_lin * gate_sigmoid * (1.0 - gate_sigmoid)).astype(jnp.bfloat16)
    grad_w_linear = weight_grad(low_c, grad_lin)
    grad_w_gate = weight_grad(low_c, grad_gate)
    grad_in_c, gain_c, shift_c = norm_grad(
        input_grad(grad_lin, w_linear) + input_grad(grad_gate, w_gate),
        unit_c,
        inverse_c,
        norm_gains[2],
    )
    grad_b = grad_c + grad_in_c
    output_in = grad_b.astype(jnp.bfloat16)
    grad_w_output = weight_grad(low_y, output_in)
    grad_y = input_grad(output_in, w_output).astype(jnp.bfloat16).reshape(frames, H, P_SIZE)
    grad_y_wide = grad_y.astype(jnp.float32)
    entering_dev = jnp.where((segments == seg_before)[None, :], jnp.exp(total_log), 0.0)
    local_back = jnp.einsum(
        "thn,thp->hnp", query_wide * entering_dev.T[:, :, None], grad_y_wide, precision=PRECISE
    )
    exit_scale, exit_grad = entering_2((carry_dev, local_back), "tm", chain_states, identity, True)
    incoming = exit_grad
    vals_parts = []
    keys_parts = []
    query_parts = []
    for number in reversed(range(count_blocks)):
        block_start = number * BLK
        rows_here = slice(block_start, block_start + BLK)
        within, entering, leaving, mixed_low, prior_state = saved_blocks[number]
        grad_blk = grad_y[rows_here]
        grad_blk_wide = grad_y_wide[rows_here]
        grad_mixed = jnp.einsum(
            "thp,shp->hts", grad_blk, state_vals[rows_here], preferred_element_type=jnp.float32
        )
        grad_vals = jnp.einsum(
            "hts,thp->shp", mixed_low, grad_blk, preferred_element_type=jnp.float32
        )
        grad_scores = (within * grad_mixed).astype(jnp.bfloat16)
        grad_query = jnp.einsum(
            "hts,shn->thn", grad_scores, state_keys[rows_here], preferred_element_type=jnp.float32
        )
        grad_keys = jnp.einsum(
            "hts,thn->shn", grad_scores, state_query[rows_here], preferred_element_type=jnp.float32
        )
        grad_query = grad_query + entering.T[:, :, None] * jnp.einsum(
            "thp,hnp->thn", grad_blk_wide, prior_state, precision=PRECISE
        )
        grad_vals = grad_vals + jnp.einsum(
            "shn,hnp->shp",
            keys_wide[rows_here] * leaving.T[:, :, None],
            incoming,
            precision=PRECISE,
        )
        grad_keys = grad_keys + leaving.T[:, :, None] * jnp.einsum(
            "shp,hnp->shn", vals_wide[rows_here], incoming, precision=PRECISE
        )
        incoming = (
            jnp.einsum(
                "thn,thp->hnp",
                query_wide[rows_here] * entering.T[:, :, None],
                grad_blk_wide,
                precision=PRECISE,
            )
            + entering[:, -1][:, None, None] * incoming
        )
        vals_parts.insert(0, grad_vals)
        keys_parts.insert(0, grad_keys)
        query_parts.insert(0, grad_query)
    grad_v_low = (
        jnp.concatenate(vals_parts, axis=0).reshape(frames, D) * live_mask.astype(jnp.float32)
    ).astype(jnp.bfloat16)
    grad_kq_low = jnp.concatenate(
        [
            jnp.concatenate(keys_parts, axis=0).reshape(frames, H * NS),
            jnp.concatenate(query_parts, axis=0).reshape(frames, H * NS),
        ],
        axis=1,
    ).astype(jnp.bfloat16)
    grad_w_values = weight_grad(low_b, grad_v_low)
    grad_w_states = weight_grad(low_b, grad_kq_low)
    grad_in_b, gain_b, shift_b = norm_grad(
        input_grad(grad_v_low, w_values) + input_grad(grad_kq_low, w_states),
        unit_b,
        inverse_b,
        norm_gains[1],
    )
    grad_a = grad_b + grad_in_b
    grad_start, grad_up_a, grad_down_a, gain_a, shift_a = ffn_backward(
        grad_a, kept_a, up_first, down_first, norm_gains[0]
    )
    blocks_ff = FF // D
    tile_grads = jnp.concatenate(
        [
            column_tiles(grad_up_a),
            grad_down_a.reshape(blocks_ff, D, D),
            jnp.stack(
                [
                    grad_w_values,
                    grad_w_states,
                    grad_w_output,
                    grad_w_linear,
                    grad_w_gate,
                    grad_project,
                ]
            ),
            column_tiles(grad_up_e),
            grad_down_e.reshape(blocks_ff, D, D),
        ],
        axis=0,
    )
    buffer = (
        jnp.zeros((owners_count, D, capacity, D), jnp.float32)
        .at[owner_of, :, column_of, :]
        .set(tile_grads)
    )
    buffer = buffer.reshape(owners_count * D, capacity, D)
    reduced = lax.psum_scatter(buffer, ("utt", "tm"), scatter_dimension=0, tiled=True)
    vector_grad = jnp.concatenate(
        [
            jnp.stack(
                [
                    gain_a,
                    gain_b,
                    gain_c,
                    gain_d,
                    gain_e,
                    gain_f,
                    shift_a,
                    shift_b,
                    shift_c,
                    shift_d,
                    shift_e,
                    shift_f,
                ]
            ),
            jnp.stack(tap_grads),
        ],
        axis=0,
    )
    vector_total = lax.psum(vector_grad, ("utt", "tm"))
    tile_new, first_new, second_new = adam_step(
        master_weight_tiles, tile_first, tile_second, reduced, RATE_TILES, DECAY_TILES
    )
    vector_new, vfirst_new, vsecond_new = adam_step(
        vector_master, vector_first, vector_second, vector_total, RATE_VECTORS, 0.0
    )
    return (
        output,
        grad_start[None],
        tile_new,
        first_new,
        second_new,
        tile_new.astype(jnp.bfloat16),
        vector_new,
        vfirst_new,
        vsecond_new,
    )


def solution(mesh):
    in_specs = (
        P("utt", "tm", None),
        P("utt", "tm", None),
        P("utt", "tm"),
        P("utt", None),
        P("utt", None, "tm"),
        P(),
        P(("utt", "tm"), None, None),
        P(("utt", "tm"), None, None),
        P(("utt", "tm"), None, None),
        P(),
        P(),
        P(),
    )
    out_specs = (
        P("utt", "tm", None),
        P("utt", "tm", None),
        P(("utt", "tm"), None, None),
        P(("utt", "tm"), None, None),
        P(("utt", "tm"), None, None),
        P(("utt", "tm"), None, None),
        P(),
        P(),
        P(),
    )
    return jax.shard_map(local, mesh=mesh, in_specs=in_specs, out_specs=out_specs, check_vma=False)
```

profile of v0, /device:TPU:0, one launch (start us, length us, event | category | flops | bytes accessed | tf_op | source)
XLA Modules:
  0.0 891.4 jit_solution(13275285275719363377)
XLA Ops:
  7.3 2.2 convert_element_type.379
  11.7 2.3 reduce-window.25
  17.4 15.6 %all-reduce = bf16[64]{0:T(256)(128)(2,1)S(1)} all-reduce(bf16[64]{0:T(256)(128)(2,1)S(1)} %dynamic-update-slice), channel_id=2, replica_groups=mesh['utt'=4,'tm'=8] {'tm'}, use_global_device_ids=true, to_apply=%add | all-reduce | flops 64 | bytes 256
  48.0 80.6 %all-gather.5.cloned.1.call-done = bf16[2048,8,512]{2,1,0:T(8,128)(2,1)} async-done(((bf16[64,8,512]{2,1,0:T(8,128)(2,1)}), bf16[2048,8,512]{2,1,0:T(8,128)(2,1)}) %all-gather.5.cloned.1.call-update) | async-done | bytes 16777232 | tf_op jit(solution)/shard_map/all_gather | solution.py:188
  128.6 16.6 %copy.105 = bf16[4,512,8,512]{3,1,2,0:T(8,128)(2,1)} copy(bf16[4,512,8,512]{3,2,1,0:T(8,128)(2,1)} %bitcast.457) | data formatting | bytes 33554432 | tf_op jit(solution)/shard_map/reshape | solution.py:191
  145.2 11.8 %gather_fusion = bf16[22,512,512]{2,1,0:T(8,128)(2,1)} fusion(bf16[4,512,8,512]{3,1,2,0:T(8,128)(2,1)} %copy.105, s32[22]{0:T(128)S(1)} %get-tuple-element.356), kind=kCustom, calls=%fused_computation | custom fusion | bytes 23068848 | tf_op jit(solution)/shard_map/gather | solution.py:194
  157.0 5.7 fusion.233
  162.7 2.4 copy.106
  165.1 8.2 multiply_convert_fusion.7
  173.4 2.5 fusion.245
  177.1 2.2 fusion.105
  184.2 9.8 %all-gather.1 = bf16[64,32,64]{2,1,0:T(8,128)(2,1)S(1)} all-gather(bf16[8,32,64]{2,1,0:T(8,128)(2,1)S(1)} %convolution_convert_fusion.4), channel_id=3, replica_groups=mesh['utt'=4,'tm'=8] {'tm'}, dimensions={0}, use_global_device_ids=true | all-gather | bytes 294912 | tf_op jit(solution)/shard_map/all_gather | solution.py:31
  195.2 3.2 multiply_convert_fusion.5
  200.4 2.8 multiply_convert_fusion.6
  210.8 2.5 add_divide_fusion.3
  213.3 3.6 multiply_convert_fusion.15
  217.5 3.0 collective-permute-start
  223.1 4.1 copy.109
  227.5 9.2 %fusion.231 = (f32[1024]{0:T(1024)S(1)}, f32[1024,512]{1,0:T(8,128)S(1)}) fusion(f32[1024]{0:T(1024)S(1)} %copy-done.133, bf16[7,512]{1,0:T(8,128)(2,1)S(1)} %collective-permute-done.1, bf16[1024,512]{1,0:T(8,128)(2,1)S(1)} %get-tuple-element.363, f32[512]{0:T(512)S(1)} %bitcast.531, f32[1024]{0:T(1024)S(1)} %copy-done.126, f32[512]{0:T(512)S(1)} %bitcast.533, ...), kind=kLoop, calls=%fused_computation.500 | loop fusion | flops 53476352 | bytes 3256320 | tf_op jit(solution)/shard_map/reduce_sum | solution.py:83
  237.2 2.5 fusion.247
  240.1 2.0 copy-done.58
  242.1 4.2 multiply_convert_fusion.4
  246.3 2.4 fusion.248
  252.2 4.9 fusion.179
  257.1 5.0 multiply_convert_fusion.3
  262.1 4.2 fusion.250
  266.4 2.9 copy.111
  269.3 3.7 multiply_reduce_fusion
  273.1 4.0 multiply_add_fusion.2
  277.2 4.3 multiply_reduce_fusion.1
  281.5 5.7 fusion.102
  290.1 4.9 collective-permute-start.3
  295.0 4.6 fusion.223
  299.6 5.6 copy.119
  305.4 19.3 %multiply_convert_fusion.11 = (bf16[1024,512]{1,0:T(8,128)(2,1)S(1)}, f32[1024,512]{1,0:T(8,128)S(1)}) fusion(f32[1024,512]{1,0:T(8,128)} %copy-done.7, f32[1024]{0:T(1024)S(1)} %copy-done.120, bf16[1024,512]{1,0:T(8,128)(2,1)} %copy-done.16, bf16[7,512]{1,0:T(8,128)(2,1)} %collective-permute-done.3, f32[512]{0:T(512)S(1)} %bitcast.532, ...), kind=kLoop, calls=%fused_computation.202 | loop fusion | flops 54001664 | bytes 6397952 | tf_op jit(solution)/shard_map/convert_element_type | solution.py:340
  325.5 2.2 fusion.178
  327.7 3.1 multiply_reduce_fusion.2
  331.4 2.3 convolution_convert_fusion
  340.6 4.1 multiply_convert_fusion.1
  344.7 4.1 multiply_convert_fusion.2
  349.8 14.8 %all-gather.2 = bf16[64,32,64]{2,1,0:T(8,128)(2,1)} all-gather(bf16[8,32,64]{2,1,0:T(8,128)(2,1)S(1)} %convolution_convert_fusion.3), channel_id=4, replica_groups=mesh['utt'=4,'tm'=8] {'tm'}, dimensions={0}, use_global_device_ids=true | all-gather | bytes 294912 | tf_op jit(solution)/shard_map/all_gather | solution.py:31
  364.6 11.6 %while.27 = (s32[]{:T(128)}, f32[8,32,64]{2,1,0:T(8,128)S(1)}, s32[]{:T(128)}, bf16[8,8]{1,0:T(8,128)(2,1)}, bf16[8,8,32,64]{3,2,1,0:T(8,128)(2,1)}, /*index=5*/s32[]{:T(128)}, s32[]{:T(128)}, s32[]{:T(128)}, s32[]{:T(128)}) while((s32[]{:T(128)}, f32[8,32,64]{2,1,0:T(8,128)S(1)}, s32[]{:T(128)}, bf16[8,8]{1,0:T(8,128)(2,1)}, ...), condition=%wide.region_33.34_spmd, body=%wide.region_32.33_spmd.sunk | while | flops 49166 | bytes 164075 | solution.py:46
  393.3 2.5 multiply_reduce_fusion.3
  398.0 4.5 fusion.180
  402.7 6.8 fusion.6
  409.5 6.4 copy.130
  416.0 7.1 bitcast_dynamic-update-slice_fusion.1
  423.1 2.5 constant_dynamic-update-slice_fusion.1
  434.3 2.2 fusion.106
  436.5 2.6 bitcast_dynamic-update-slice_fusion
  440.2 2.5 constant_dynamic-update-slice_fusion
  442.7 11.3 %broadcast_in_dim.111 = f32[4,512,8,512]{3,1,2,0:T(8,128)} broadcast(f32[]{:T(128)} %constant.151.clone.1), dimensions={} | broadcast | bytes 33554436 | tf_op jit(solution)/shard_map/broadcast_in_dim | solution.py:450
  454.0 41.2 %scatter_fusion = f32[4,512,8,512]{3,1,2,0:T(8,128)} fusion(f32[4,512,8,512]{3,1,2,0:T(8,128)} %broadcast_in_dim.111, s32[22]{0:T(128)S(1)} %copy-done.82, f32[22,512,512]{2,1,0:T(8,128)} %constant_dynamic-update-slice_fusion), kind=kCustom, calls=%fused_computation.1 | custom fusion | bytes 69206192 | tf_op jit(solution)/shard_map/scatter | solution.py:452
  495.2 32.0 %copy.120 = f32[4,512,8,512]{3,2,1,0:T(8,128)} copy(f32[4,512,8,512]{3,1,2,0:T(8,128)} %scatter_fusion) | data formatting | bytes 67108864 | tf_op jit(solution)/shard_map/scatter | solution.py:452
  528.8 2.4 copy.123
  531.2 1.9 fusion.100
  533.1 2.7 fusion.86
  535.8 10.7 %fusion.249 = (f32[512]{0:T(512)S(1)}, f32[1024,512]{1,0:T(8,128)}) fusion(bf16[512,2048]{0,1:T(8,128)(2,1)S(1)} %bitcast.494, f32[1024,2048]{1,0:T(8,128)} %get-tuple-element.375, f32[1024,2048]{1,0:T(8,128)} %get-tuple-element.358), kind=kOutput, calls=%fused_computation.517 | convolution fusion | flops 2166881792 | bytes 20973568 | tf_op jit(solution)/shard_map/dot_general | solution.py:77
  546.5 2.0 copy.116
  550.2 2.0 fusion.24
  552.3 3.0 copy.124
  555.6 44.4 %psum.7 = f32[27,512]{1,0:T(8,128)S(1)} all-reduce(f32[27,512]{1,0:T(8,128)S(1)} %concatenate.99), channel_id=1, replica_groups=mesh['utt'=4,'tm'=8] {'utt','tm'}, use_global_device_ids=true, to_apply=%region_67.68 | all-reduce | flops 13824 | bytes 110592 | tf_op jit(solution)/shard_map/psum | solution.py:478
  600.8 279.7 %reduce-scatter.2.cloned.1.call-done = f32[64,8,512]{2,1,0:T(8,128)} async-done(((f32[2048,8,512]{2,1,0:T(8,128)}), f32[64,8,512]{2,1,0:T(8,128)}) %reduce-scatter.2.cloned.1.call-update) | async-done | bytes 1048592 | tf_op jit(solution)/shard_map/reduce_scatter | solution.py:455
  880.5 3.6 fusion.228
  (570 shorter events, 98.9 us)
Async XLA Ops:
  7.2 7.4 copy-start.199
  7.2 29.2 %copy-start.65 = (bf16[1,1024,512]{2,1,0:T(8,128)(2,1)S(1)}, bf16[1,1024,512]{2,1,0:T(8,128)(2,1)}, u32[]{:S(2)}) copy-start(bf16[1,1024,512]{2,1,0:T(8,128)(2,1)} %param.16) | copy-start | bytes 3145732
  7.2 29.7 %copy-start.66 = (bf16[1,1024,512]{2,1,0:T(8,128)(2,1)S(1)}, bf16[1,1024,512]{2,1,0:T(8,128)(2,1)}, u32[]{:S(2)}) copy-start(bf16[1,1024,512]{2,1,0:T(8,128)(2,1)} %param.17) | copy-start | bytes 3145732
  7.2 121.4 %all-gather.5.cloned.1.call-start = ((), (), s32[]{:S(2)}) async-start(), calls=%async_computation.1 | async-start | bytes 17301504 | tf_op jit(solution)/shard_map/all_gather | solution.py:188
  9.5 870.9 %reduce-scatter.2.cloned.1.call-start = ((), (), s32[]{:S(2)}) async-start(), calls=%async_computation.2 | async-start | bytes 34603008 | tf_op jit(solution)/shard_map/reduce_scatter | solution.py:455
  37.0 136.4 %copy-start.5 = (bf16[1,1024,512]{1,2,0:T(8,128)(2,1)}, bf16[1,1024,512]{1,2,0:T(8,128)(2,1)S(1)}, u32[]{:S(2)}) copy-start(bf16[1,1024,512]{1,2,0:T(8,128)(2,1)S(1)} %copy.104) | copy-start | bytes 3145732
  37.0 5.3 copy-start.198
  37.0 5.9 copy-start.88
  39.7 105.5 %copy-start.94 = (f32[8,512]{1,0:T(8,128)}, f32[8,512]{1,0:T(8,128)S(1)}, u32[]{:S(2)}) copy-start(f32[8,512]{1,0:T(8,128)S(1)} %get-tuple-element.255) | copy-start | bytes 49156
  40.7 104.5 %copy-start.97 = (f32[8,512]{1,0:T(8,128)}, f32[8,512]{1,0:T(8,128)S(1)}, u32[]{:S(2)}) copy-start(f32[8,512]{1,0:T(8,128)S(1)} %get-tuple-element.253) | copy-start | bytes 49156
  41.9 123.2 %copy-start.104 = (f32[1024]{0:T(1024)}, f32[1024]{0:T(1024)S(1)}, u32[]{:S(2)}) copy-start(f32[1024]{0:T(1024)S(1)} %broadcast_multiply_fusion.17) | copy-start | bytes 12292
  42.8 122.3 %copy-start.134 = (f32[1024]{0:T(1024)}, f32[1024]{0:T(1024)S(1)}, u32[]{:S(2)}) copy-start(f32[1024]{0:T(1024)S(1)} %add_rsqrt_fusion.5) | copy-start | bytes 12292
  43.5 121.7 %copy-start.158 = (f32[1,512]{1,0:T(1,128)}, f32[1,512]{1,0:T(1,128)S(1)}, u32[]{:S(2)}) copy-start(f32[1,512]{1,0:T(1,128)S(1)} %get-tuple-element.306) | copy-start | bytes 6148
  43.5 121.7 %copy-start.193 = (f32[1,512]{1,0:T(1,128)}, f32[1,512]{1,0:T(1,128)S(1)}, u32[]{:S(2)}) copy-start(f32[1,512]{1,0:T(1,128)S(1)} %get-tuple-element.305) | copy-start | bytes 6148
  43.5 132.7 %copy-start.144 = (f32[1,512]{1,0:T(1,128)}, f32[1,512]{1,0:T(1,128)S(1)}, u32[]{:S(2)}) copy-start(f32[1,512]{1,0:T(1,128)S(1)} %get-tuple-element.304) | copy-start | bytes 6148
  165.1 8.2 copy-start.60
  182.1 18.3 %copy-start.70 = (bf16[512,256]{0,1:T(8,128)(2,1)}, bf16[512,256]{0,1:T(8,128)(2,1)S(1)}, u32[]{:S(2)}) copy-start(bf16[512,256]{0,1:T(8,128)(2,1)S(1)} %get-tuple-element.275) | copy-start | bytes 786436
  182.3 11.8 %copy-start.27 = (f32[1024,256]{0,1:T(8,128)}, f32[1024,256]{0,1:T(8,128)S(1)}, u32[]{:S(2)}) copy-start(f32[1024,256]{0,1:T(8,128)S(1)} %get-tuple-element.276) | copy-start | bytes 3145732
  183.3 22.0 %copy-start.35 = (bf16[512,512]{0,1:T(8,128)(2,1)}, bf16[512,512]{0,1:T(8,128)(2,1)S(1)}, u32[]{:S(2)}) copy-start(bf16[512,512]{0,1:T(8,128)(2,1)S(1)} %get-tuple-element.278) | copy-start | bytes 1572868
  195.1 10.1 %copy-start.41 = (f32[512,256]{0,1:T(8,128)}, f32[512,256]{0,1:T(8,128)S(1)}, u32[]{:S(2)}) copy-start(f32[512,256]{0,1:T(8,128)S(1)} %get-tuple-element.265) | copy-start | bytes 1572868
  195.1 11.7 %copy-start.37 = (f32[512,256]{0,1:T(8,128)}, f32[512,256]{0,1:T(8,128)S(1)}, u32[]{:S(2)}) copy-start(f32[512,256]{0,1:T(8,128)S(1)} %get-tuple-element.384) | copy-start | bytes 1572868
  217.5 9.8 %collective-permute-start = (bf16[7,512]{1,0:T(8,128)(2,1)}, bf16[7,512]{1,0:T(8,128)(2,1)S(1)}, u32[]{:S(2)}, u32[]{:S(2)}) collective-permute-start(bf16[7,512]{1,0:T(8,128)(2,1)} %get-tuple-element.268), channel_id=1, source_target_pairs={{0,1},{1,2},{2,3},{3,4},{4,5},{5,6},{6,7},{8,9},{9,10},{10,11},{11... | collective-permute-start | bytes 21512 | tf_op jit(solution)/shard_map/ppermute | solution.py:57
  220.6 6.7 collective-permute-start.1
  227.3 9.9 %copy-start.100 = (bf16[7,512]{1,0:T(8,128)(2,1)}, bf16[7,512]{1,0:T(8,128)(2,1)S(1)}, u32[]{:S(2)}) copy-start(bf16[7,512]{1,0:T(8,128)(2,1)S(1)} %collective-permute-done) | copy-start | bytes 21508
  227.3 54.2 %copy-start.102 = (bf16[7,512]{1,0:T(8,128)(2,1)}, bf16[7,512]{1,0:T(8,128)(2,1)S(1)}, u32[]{:S(2)}) copy-start(bf16[7,512]{1,0:T(8,128)(2,1)S(1)} %collective-permute-done.1) | copy-start | bytes 21508
  227.5 9.7 %copy-start.176 = (f32[1,512]{1,0:T(1,128)S(1)}, f32[1,512]{1,0:T(1,128)}, u32[]{:S(2)}) copy-start(f32[1,512]{1,0:T(1,128)} %get-tuple-element.284) | copy-start | bytes 6148
  227.5 9.7 %copy-start.190 = (f32[1,512]{1,0:T(1,128)S(1)}, f32[1,512]{1,0:T(1,128)}, u32[]{:S(2)}) copy-start(f32[1,512]{1,0:T(1,128)} %get-tuple-element.283) | copy-start | bytes 6148
  236.7 44.8 %copy-start.138 = (f32[1024]{0:T(1024)}, f32[1024]{0:T(1024)S(1)}, u32[]{:S(2)}) copy-start(f32[1024]{0:T(1024)S(1)} %broadcast_multiply_fusion.14) | copy-start | bytes 12292
  239.7 6.6 copy-start.12
  248.8 8.3 copy-start.14
  252.2 4.9 copy-start.165
  252.2 4.9 copy-start.167
  281.5 13.5 %copy-start.196 = (f32[1,512]{1,0:T(1,128)S(1)}, f32[1,512]{1,0:T(1,128)}, u32[]{:S(2)}) copy-start(f32[1,512]{1,0:T(1,128)} %get-tuple-element.281) | copy-start | bytes 6148
  281.5 13.5 %copy-start.203 = (bf16[1024,2048]{1,0:T(8,128)(2,1)S(1)}, bf16[1024,2048]{1,0:T(8,128)(2,1)}, u32[]{:S(2)}) copy-start(bf16[1024,2048]{1,0:T(8,128)(2,1)} %copy-done.202) | copy-start | bytes 12582916
  288.8 16.5 %collective-permute-start.2 = (bf16[7,512]{1,0:T(8,128)(2,1)}, bf16[7,512]{1,0:T(8,128)(2,1)}, u32[]{:S(2)}, u32[]{:S(2)}) collective-permute-start(bf16[7,512]{1,0:T(8,128)(2,1)} %get-tuple-element.266), channel_id=1, source_target_pairs={{1,0},{2,1},{3,2},{4,3},{5,4},{6,5},{7,6},{9,8},{10,9},{11,10},{12... | collective-permute-start | bytes 21512 | tf_op jit(solution)/shard_map/ppermute | solution.py:59
  290.1 15.2 %collective-permute-start.3 = (bf16[7,512]{1,0:T(8,128)(2,1)}, bf16[7,512]{1,0:T(8,128)(2,1)}, u32[]{:S(2)}, u32[]{:S(2)}) collective-permute-start(bf16[7,512]{1,0:T(8,128)(2,1)} %get-tuple-element.267), channel_id=1, source_target_pairs={{0,1},{1,2},{2,3},{3,4},{4,5},{5,6},{6,7},{8,9},{9,10},{10,11},{11... | collective-permute-start | bytes 21512 | tf_op jit(solution)/shard_map/ppermute | solution.py:57
  299.6 5.7 copy-start.147
  299.6 5.7 copy-start.149
  299.6 5.7 copy-start.151
  299.6 5.7 copy-start.152
  299.6 5.7 copy-start.153
  299.6 5.7 copy-start.154
  299.6 5.7 copy-start.155
  305.3 19.4 %copy-start.8 = (f32[1024,512]{1,0:T(8,128)S(1)}, f32[1024,512]{1,0:T(8,128)}, u32[]{:S(2)}) copy-start(f32[1024,512]{1,0:T(8,128)} %copy-done.7) | copy-start | bytes 6291460
  305.3 19.4 %copy-start.29 = (f32[1024,512]{1,0:T(8,128)S(1)}, f32[1024,512]{1,0:T(8,128)}, u32[]{:S(2)}) copy-start(f32[1024,512]{1,0:T(8,128)} %get-tuple-element.364) | copy-start | bytes 6291460
  325.5 5.3 copy-start.43
  348.8 27.4 %copy-start.92 = (f32[512,8]{0,1:T(8,128)S(1)}, f32[512,8]{0,1:T(8,128)}, u32[]{:S(2)}) copy-start(f32[512,8]{0,1:T(8,128)} %get-tuple-element.380) | copy-start | bytes 49156
  349.8 28.0 %copy-start.38 = (f32[512,256]{0,1:T(8,128)S(1)}, f32[512,256]{0,1:T(8,128)}, u32[]{:S(2)}) copy-start(f32[512,256]{0,1:T(8,128)} %copy-done.37) | copy-start | bytes 1572868
  349.8 28.0 %copy-start.185 = (f32[8]{0:T(128)S(1)}, f32[8]{0:T(128)}, u32[]{:S(2)}) copy-start(f32[8]{0:T(128)} %slice_reduce_fusion.4) | copy-start | bytes 100
  364.6 15.2 %copy-start.77 = (bf16[512,256]{0,1:T(8,128)(2,1)S(1)}, bf16[512,256]{0,1:T(8,128)(2,1)}, u32[]{:S(2)}) copy-start(bf16[512,256]{0,1:T(8,128)(2,1)} %get-tuple-element.273) | copy-start | bytes 786436
  395.9 6.7 slice-start
  398.0 4.6 slice-start.1
  409.5 6.4 copy-start.105
  409.5 6.4 copy-start.135
  409.5 6.4 copy-start.159
  409.5 6.4 copy-start.194
  416.0 7.1 copy-start.47
  442.7 11.3 %copy-start.82 = (s32[22]{0:T(128)S(1)}, s32[22]{0:T(128)}, u32[]{:S(2)}) copy-start(s32[22]{0:T(128)} %get-tuple-element.355) | copy-start | bytes 268
  552.3 47.8 %copy-start.89 = (f32[27,512]{1,0:T(8,128)S(1)}, f32[27,512]{1,0:T(8,128)}, u32[]{:S(2)}) copy-start(f32[27,512]{1,0:T(8,128)} %param.25) | copy-start | bytes 165892
  552.3 47.8 %copy-start.108 = (f32[27,512]{1,0:T(8,128)S(1)}, f32[27,512]{1,0:T(8,128)}, u32[]{:S(2)}) copy-start(f32[27,512]{1,0:T(8,128)} %param.26) | copy-start | bytes 165892
  552.3 47.8 %copy-start.109 = (f32[27,512]{1,0:T(8,128)S(1)}, f32[27,512]{1,0:T(8,128)}, u32[]{:S(2)}) copy-start(f32[27,512]{1,0:T(8,128)} %param.27) | copy-start | bytes 165892
  552.3 328.2 %copy-start.45 = (f32[64,8,512]{2,1,0:T(8,128)S(1)}, f32[64,8,512]{2,1,0:T(8,128)}, u32[]{:S(2)}) copy-start(f32[64,8,512]{2,1,0:T(8,128)} %param.22) | copy-start | bytes 3145732
  552.3 328.2 %copy-start.63 = (f32[64,8,512]{2,1,0:T(8,128)S(1)}, f32[64,8,512]{2,1,0:T(8,128)}, u32[]{:S(2)}) copy-start(f32[64,8,512]{2,1,0:T(8,128)} %param.23) | copy-start | bytes 3145732
  552.3 328.2 %copy-start.64 = (f32[64,8,512]{2,1,0:T(8,128)S(1)}, f32[64,8,512]{2,1,0:T(8,128)}, u32[]{:S(2)}) copy-start(f32[64,8,512]{2,1,0:T(8,128)} %param.24) | copy-start | bytes 3145732
  (148 other events, 437.5 us)
Sparse Core Ops, SparseCore 0:
  11.5 117.1 all-gather.4
  527.4 353.0 reduce-scatter.1
where the time goes:
time: 905 us; the launch traced here: 891 us
  waiting for transfers between devices  360 us (40%)
  local copies, waits for them, and re-layouts  185 us (20%)
  matrix products  142 us (16%)
  other arithmetic  88.8 us (10%)
  blocking collectives  84.7 us (9%)
  between operations  19 us (2%)
  starting transfers between devices  10.5 us (1%)
    reduce_scatter x1, waiting for transfers between devices, local(): lax.psum_scatter(buffer, ('utt', 'tm'), scatter_dimension=0, tiled=True)  280 us
    all_gather x1, waiting for transfers between devices, local(): gathered = lax.all_gather(low_master, ('utt', 'tm'), axis=0, tiled=True)  80.6 us
    scatter x2, local copies, waits for them, and re-layouts, local(): buffer = jnp.zeros((owners_count, D, capacity, D), jnp.float32).at[owner_...  73.3 us
    psum x1, blocking collectives, local(): vector_total = lax.psum(vector_grad, ('utt', 'tm'))  44.4 us
    dot_general x10, matrix products, input_grad(): lax.dot_general(gradients, weights, (((1,), (1,)), ((), ())), preferred_e...  42.8 us
    dot_general x10, matrix products, weight_grad(): lax.dot_general(activations, gradients, (((0,), (0,)), ((), ())), preferr...  31.9 us
    dot_general x10, matrix products, product(): return jnp.dot(matrix_a, matrix_b, preferred_element_type=jnp.float32)  31.7 us
    unnamed x423, local copies, waits for them, and re-layouts  31.3 us
  transfers between devices with their start and end apart: 6, of which 2 were waited for; matrix products, arithmetic and copies ran while one was open for 7% of the time, Pallas kernels for 0%

commit v1 on v0

--- a/solution.py
+++ b/solution.py
@@ -168,6 +168,36 @@
         first_hat / (jnp.sqrt(second_hat) + ADAM_EPS) + decay_rate * master
     )
     return (master_new, first_new, second_new)
+
+
+def halving_sum(cells, axis):
+    bits = lax.axis_size(axis).bit_length() - 1
+    count = cells.shape[1]
+    cells = exchange_bit(cells, axis, 0, 0)
+    parts = []
+    for piece, order in (
+        (cells[:, : count // 2], list(range(bits - 1))),
+        (cells[:, count // 2 :], list(reversed(range(bits - 1)))),
+    ):
+        left = list(range(bits - 1))
+        for bit in order:
+            place = left.index(bit)
+            piece = exchange_bit(piece, axis, place, bit + 1)
+            left.remove(bit)
+        parts.append(piece[0])
+    return jnp.concatenate(parts, axis=0)
+
+
+def exchange_bit(cells, axis, place, bit):
+    count = lax.axis_size(axis)
+    mine = (lax.axis_index(axis) >> bit) & 1
+    shape = cells.shape
+    cells = cells.reshape(shape[0] >> (place + 1), 2, 1 << place, *shape[1:])
+    kept = lax.dynamic_index_in_dim(cells, mine, 1, False)
+    sent = lax.dynamic_index_in_dim(cells, 1 - mine, 1, False)
+    got = lax.ppermute(sent, axis, [(i, i ^ (1 << bit)) for i in range(count)])
+    total = (kept.astype(jnp.float32) + got.astype(jnp.float32)).astype(cells.dtype)
+    return total.reshape(shape[0] // 2, *shape[1:])
 
 
 def local(
@@ -184,14 +214,16 @@
     vector_first,
     vector_second,
 ):
-    low_master = master_weight_tiles.astype(jnp.bfloat16)
-    gathered = lax.all_gather(low_master, ("utt", "tm"), axis=0, tiled=True)
-    owners_count = gathered.shape[0] // D
-    capacity = gathered.shape[1]
-    grouped = gathered.reshape(owners_count, D, capacity, D)
-    owner_of = tile_slots // capacity
-    column_of = tile_slots % capacity
-    tile_values = grouped[owner_of, :, column_of, :]
+    own_rows, capacity, _ = master_weight_tiles.shape
+    owners_count = lax.axis_size("utt")
+    low_master = master_weight_tiles.transpose(1, 0, 2).astype(jnp.bfloat16)
+    by_slot = lax.all_gather(low_master, "utt", axis=0, tiled=True)
+    chosen = by_slot[tile_slots]
+    groups = []
+    for first, last in ((0, 8), (8, 22)):
+        part = lax.all_gather(chosen[first:last], "tm", axis=0)
+        groups.append(part.transpose(1, 0, 2, 3).reshape(last - first, D, D))
+    tile_values = jnp.concatenate(groups, axis=0)
     up_first, down_first, mixers, up_second, down_second = split_tiles(tile_values)
     w_values, w_states, w_output, w_linear, w_gate, w_project = mixers
     norm_gains = vector_master[0:6]
@@ -427,32 +459,38 @@
         grad_a, kept_a, up_first, down_first, norm_gains[0]
     )
     blocks_ff = FF // D
-    tile_grads = jnp.concatenate(
+    count = lax.axis_size("tm")
+
+    def reduce_tiles(parts):
+        stacked = jnp.concatenate(parts, axis=0).astype(jnp.bfloat16)
+        stacked = stacked.reshape(stacked.shape[0], count, own_rows, D).transpose(1, 0, 2, 3)
+        return halving_sum(stacked, "tm")
+
+    middle = reduce_tiles([jnp.stack([grad_w_output, grad_w_linear, grad_w_gate])])
+    late = reduce_tiles(
+        [
+            grad_project[None],
+            column_tiles(grad_up_e),
+            grad_down_e.reshape(blocks_ff, D, D),
+        ]
+    )
+    early = reduce_tiles(
         [
             column_tiles(grad_up_a),
             grad_down_a.reshape(blocks_ff, D, D),
-            jnp.stack(
-                [
-                    grad_w_values,
-                    grad_w_states,
-                    grad_w_output,
-                    grad_w_linear,
-                    grad_w_gate,
-                    grad_project,
-                ]
-            ),
-            column_tiles(grad_up_e),
-            grad_down_e.reshape(blocks_ff, D, D),
-        ],
-        axis=0,
-    )
-    buffer = (
-        jnp.zeros((owners_count, D, capacity, D), jnp.float32)
-        .at[owner_of, :, column_of, :]
-        .set(tile_grads)
-    )
-    buffer = buffer.reshape(owners_count * D, capacity, D)
-    reduced = lax.psum_scatter(buffer, ("utt", "tm"), scatter_dimension=0, tiled=True)
+            jnp.stack([grad_w_values, grad_w_states]),
+        ]
+    )
+    shards = jnp.concatenate([early, middle, late, jnp.zeros((1, own_rows, D), jnp.bfloat16)], axis=0)
+    tiles = tile_slots.shape[0]
+    tile_of = (
+        jnp.full((owners_count * capacity,), tiles, jnp.int32)
+        .at[tile_slots]
+        .set(jnp.arange(tiles, dtype=jnp.int32))
+    )
+    placed = shards[tile_of].reshape(owners_count, capacity, own_rows, D)
+    reduced = lax.psum_scatter(placed, "utt", scatter_dimension=0)
+    reduced = reduced.astype(jnp.float32).transpose(1, 0, 2)
     vector_grad = jnp.concatenate(
         [
             jnp.stack(

time: 905 us -> 570 us (0.63)
  waiting for transfers between devices: 360 us -> 124 us
  local copies, waits for them, and re-layouts: 185 us -> 112 us
  matrix products: 142 us -> 122 us
    reduce_scatter x1, waiting for transfers between devices: 280 us -> 0.01 us  [local(): reduced = lax.psum_scatter(placed, 'utt', scatter_dimension=0)]
    scatter x2 -> x1, local copies, waits for them, and re-layouts: 73.3 us -> 0.76 us  [local(): tile_of = jnp.full((owners_count * capacity,), tiles, jnp.int32).at[tile_...]
    ppermute x0 -> x15, waiting for transfers between devices: none -> 45.1 us  [exchange_bit(): got = lax.ppermute(sent, axis, [(i, i ^ 1 << bit) for i in range(count)])]
    reshape x1 -> x0, local copies, waits for them, and re-layouts: 16.6 us -> none  [local(): grouped = gathered.reshape(owners_count, D, capacity, D)]
    slice x1 -> x14, local copies, waits for them, and re-layouts: 0.16 us -> 14.3 us  [the longest x2 6.06 us: split_tiles(): down_first = tile_values[blocks_ff:offset].reshape(FF, D)]
    unnamed x423 -> x510, local copies, waits for them, and re-layouts: 31.3 us -> 43.8 us
    broadcast_in_dim x1 -> x0, local copies, waits for them, and re-layouts: 11.3 us -> none  [local(): jnp.zeros((owners_count, D, capacity, D), jnp.float32)]
    dot_general x10, matrix products: 31.7 us -> 22.1 us  [product(): return jnp.dot(matrix_a, matrix_b, preferred_element_type=jnp.float32)]
  transfers between devices with their start and end apart: 6 -> 23, of which waited for: 2 -> 10; matrix products, arithmetic and copies ran while one was open for 7% -> 35% of each run, Pallas kernels for 0% -> 0%
where the time goes in v1:
time: 570 us; the launch traced here: 565 us
  waiting for transfers between devices  124 us (22%)
  matrix products  122 us (21%)
  local copies, waits for them, and re-layouts  112 us (20%)
  other arithmetic  91.7 us (16%)
  blocking collectives  77.7 us (14%)
  between operations  19.2 us (3%)
  starting transfers between devices  17.8 us (3%)
    all_gather x1, waiting for transfers between devices, local(): by_slot = lax.all_gather(low_master, 'utt', axis=0, tiled=True)  48.1 us
    ppermute x15, waiting for transfers between devices, exchange_bit(): got = lax.ppermute(sent, axis, [(i, i ^ 1 << bit) for i in range(count)])  45.1 us
    unnamed x510, local copies, waits for them, and re-layouts  43.8 us
    psum x1, blocking collectives, local(): vector_total = lax.psum(vector_grad, ('utt', 'tm'))  39.9 us
    dot_general x10, matrix products, input_grad(): lax.dot_general(gradients, weights, (((1,), (1,)), ((), ())), preferred_e...  35 us
    all_gather x2, waiting for transfers between devices, local(): part = lax.all_gather(chosen[first:last], 'tm', axis=0)  30.4 us
    dot_general x10, matrix products, weight_grad(): lax.dot_general(activations, gradients, (((0,), (0,)), ((), ())), preferr...  25 us
    all_gather x2, blocking collectives, entering_2(): lax.all_gather(a.astype(kind), axis)  24.1 us
  transfers between devices with their start and end apart: 23, of which 10 were waited for; matrix products, arithmetic and copies ran while one was open for 35% of the time, Pallas kernels for 0%

profile of v1, /device:TPU:0, one launch (start us, length us, event | category | flops | bytes accessed | tf_op | source)
XLA Modules:
  0.0 565.3 jit_solution(6487237023455007533)
XLA Ops:
  7.2 2.6 copy.294
  10.5 48.1 %all-gather.9.cloned.1.call-done = bf16[32,64,512]{2,1,0:T(8,128)(2,1)} async-done(((bf16[8,64,512]{2,1,0:T(8,128)(2,1)}), bf16[32,64,512]{2,1,0:T(8,128)(2,1)}) %all-gather.9.cloned.1.call-update) | async-done | bytes 2097168 | tf_op jit(solution)/shard_map/all_gather | solution.py:220
  58.6 2.2 gather_fusion
  67.1 2.3 reduce-window.25
  72.8 13.7 %all-reduce = bf16[64]{0:T(256)(128)(2,1)S(1)} all-reduce(bf16[64]{0:T(256)(128)(2,1)S(1)} %dynamic-update-slice), channel_id=4, replica_groups=mesh['utt'=4,'tm'=8] {'tm'}, use_global_device_ids=true, to_apply=%add | all-reduce | flops 64 | bytes 256
  99.5 3.9 fusion.254
  103.6 2.4 copy.213
  106.0 2.1 copy.214
  108.7 6.3 %multiply_convert_fusion.7 = (bf16[1024,2048]{1,0:T(8,128)(2,1)S(1)}, f32[1024,2048]{1,0:T(8,128)}) fusion(bf16[512,2048]{0,1:T(8,128)(2,1)S(1)} %bitcast.592, f32[512]{0:T(512)S(1)} %bitcast.725, f32[512]{0:T(512)S(1)} %bitcast.681, f32[1024]{0:T(1024)S(1)} %add_rsqrt_fusion.5, f32[1024]{0:T(1024)S(1)} %broadcast_multiply_fusion.17, ...), kind=kOutput, calls=%fused_computation.42 | convolution fusion | flops 2161115136 | bytes 15740928 | tf_op jit(solution)/shard_map/dot_general | solution.py:67
  115.0 2.5 fusion.267
  119.2 30.4 %all-gather.13.cloned.1.call-done = bf16[112,64,512]{2,1,0:T(8,128)(2,1)} async-done(((bf16[14,64,512]{2,1,0:T(8,128)(2,1)}), bf16[112,64,512]{2,1,0:T(8,128)(2,1)}) %all-gather.13.cloned.1.call-update) | async-done | bytes 7340048 | tf_op jit(solution)/shard_map/all_gather | solution.py:224
  149.6 3.3 fusion.253
  157.5 9.8 %all-gather.3 = bf16[64,32,64]{2,1,0:T(8,128)(2,1)S(1)} all-gather(bf16[8,32,64]{2,1,0:T(8,128)(2,1)S(1)} %convolution_convert_fusion.14), channel_id=5, replica_groups=mesh['utt'=4,'tm'=8] {'tm'}, dimensions={0}, use_global_device_ids=true | all-gather | bytes 294912 | tf_op jit(solution)/shard_map/all_gather | solution.py:31
  168.7 2.8 multiply_convert_fusion.6
  173.5 2.8 multiply_convert_fusion.5
  187.6 3.1 collective-permute-start
  195.1 4.6 copy.218
  202.1 8.3 %fusion.250 = (f32[1024]{0:T(1024)S(1)}, f32[1024,512]{1,0:T(8,128)S(1)}) fusion(f32[1024]{0:T(1024)S(1)} %copy-done.154, bf16[7,512]{1,0:T(8,128)(2,1)S(1)} %collective-permute-done.1, bf16[1024,512]{1,0:T(8,128)(2,1)S(1)} %get-tuple-element.384, f32[512]{0:T(512)S(1)} %bitcast.649, f32[1024]{0:T(1024)S(1)} %copy-done.147, f32[512]{0:T(512)S(1)} %bitcast.651, ...), kind=kLoop, calls=%fused_computation.548 | loop fusion | flops 53476352 | bytes 3256320 | tf_op jit(solution)/shard_map/reduce_sum | solution.py:83
  214.5 4.2 multiply_convert_fusion.4
  220.7 2.4 fusion.270
  226.6 4.9 multiply_convert_fusion.3
  231.6 4.3 fusion.272
  235.8 3.0 copy.221
  238.9 3.7 multiply_reduce_fusion
  242.7 4.0 multiply_add_fusion.2
  246.7 2.7 multiply_reduce_fusion.1
  251.5 3.9 convolution_convert_fusion.1
  255.4 4.3 convolution_convert_fusion
  259.7 5.7 %fusion.106 = (f32[512]{0:T(512)}, f32[512]{0:T(512)}, f32[512]{0:T(512)}, f32[512]{0:T(512)}, f32[512]{0:T(512)}, /*index=5*/f32[512]{0:T(512)}, bf16[1024,512]{1,0:T(8,128)(2,1)S(1)}) fusion(bf16[7,512]{1,0:T(8,128)(2,1)S(1)} %collective-permute-done.1, bf16[1024,512]{1,0:T(8,128)(2,1)S(1)} %get-tuple-element.384, f32[1024]{0:T(1024)S(1)} %copy-done.154, ...), kind=kLoop, calls=%fused_computation.196 | loop fusion | flops 26735616 | bytes 6353920 | tf_op jit(solution)/shard_map/reduce_sum | solution.py:365
  268.2 4.9 collective-permute-start.3
  273.1 4.9 reshape.823
  278.0 2.2 copy.234
  285.7 10.2 %multiply_convert_fusion.11 = (bf16[1024,512]{1,0:T(8,128)(2,1)S(1)}, f32[1024,512]{1,0:T(8,128)S(1)}) fusion(f32[1024,512]{1,0:T(8,128)S(1)} %copy-done.9, f32[1024]{0:T(1024)S(1)} %copy-done.141, bf16[1024,512]{1,0:T(8,128)(2,1)S(1)} %copy-done.19, bf16[7,512]{1,0:T(8,128)(2,1)} %collective-permute-done.3, f32[512]{0:T(512)S(1)} %bitcast.650, ...), kind=kLoop, calls=%fused_computation.209 | loop fusion | flops 54001664 | bytes 6397952 | tf_op jit(solution)/shard_map/convert_element_type | solution.py:372
  302.7 4.1 multiply_convert_fusion.2
  307.9 4.1 multiply_convert_fusion.1
  321.6 14.3 %all-gather.4 = bf16[64,32,64]{2,1,0:T(8,128)(2,1)} all-gather(bf16[8,32,64]{2,1,0:T(8,128)(2,1)S(1)} %convolution_convert_fusion.13), channel_id=6, replica_groups=mesh['utt'=4,'tm'=8] {'tm'}, dimensions={0}, use_global_device_ids=true | all-gather | bytes 294912 | tf_op jit(solution)/shard_map/all_gather | solution.py:31
  335.9 11.7 %while.27 = (s32[]{:T(128)}, f32[8,32,64]{2,1,0:T(8,128)S(1)}, s32[]{:T(128)}, bf16[8,8]{1,0:T(8,128)(2,1)}, bf16[8,8,32,64]{3,2,1,0:T(8,128)(2,1)}, /*index=5*/s32[]{:T(128)}, s32[]{:T(128)}, s32[]{:T(128)}, s32[]{:T(128)}) while((s32[]{:T(128)}, f32[8,32,64]{2,1,0:T(8,128)S(1)}, s32[]{:T(128)}, bf16[8,8]{1,0:T(8,128)(2,1)}, ...), condition=%wide.region_33.34_spmd, body=%wide.region_32.33_spmd.sunk | while | flops 49166 | bytes 164067 | solution.py:46
  349.1 3.0 fusion.128
  360.8 2.1 convolution_add_fusion.4
  372.5 3.9 convolution_convert_fusion.2
  377.2 6.9 %fusion.6 = (bf16[2048,1024]{0,1:T(8,128)(2,1)}, f32[1024,2048]{1,0:T(8,128)}) fusion(f32[1024,2048]{1,0:T(8,128)S(1)} %bitcast.733, bf16[2048,512]{1,0:T(8,128)(2,1)S(1)} %bitcast.595, f32[1024,512]{0,1:T(8,128)S(1)} %multiply_add_fusion), kind=kOutput, calls=%fused_computation.31 | convolution fusion | flops 2167406592 | bytes 25165824 | tf_op jit(solution)/shard_map/dot_general | solution.py:77
  386.9 6.5 %copy.255 = bf16[2048,1024]{1,0:T(8,128)(2,1)} copy(bf16[2048,1024]{0,1:T(8,128)(2,1)} %get-tuple-element.395) | data formatting | bytes 8388608 | tf_op jit(solution)/shard_map/dot_general | solution.py:71
  393.4 4.8 convolution_convert_fusion.3
  406.9 5.6 collective-permute-done.10
  412.6 3.4 collective-permute-done.12
  418.1 3.5 fusion.23
  424.7 2.7 fusion.17
  429.0 7.6 %collective-permute-done.15 = bf16[2,1,4,64,512]{4,3,2,1,0:T(8,128)(2,1)S(1)} collective-permute-done((bf16[2,1,4,64,512]{4,3,2,1,0:T(8,128)(2,1)S(1)}, bf16[2,1,4,64,512]{4,3,2,1,0:T(8,128)(2,1)S(1)}, u32[]{:S(2)}, u32[]{:S(2)}) %collective-permute-start.15) | collective-permute-done | bytes 524320 | tf_op jit(solution)/shard_map/ppermute | solution.py:198
  437.4 3.4 collective-permute-done.17
  441.2 9.5 %collective-permute-done.5 = bf16[2,1,5,64,512]{4,3,2,1,0:T(8,128)(2,1)S(1)} collective-permute-done((bf16[2,1,5,64,512]{4,3,2,1,0:T(8,128)(2,1)S(1)}, bf16[2,1,5,64,512]{4,3,2,1,0:T(8,128)(2,1)S(1)}, u32[]{:S(2)}, u32[]{:S(2)}) %collective-permute-start.5) | collective-permute-done | bytes 655392 | tf_op jit(solution)/shard_map/ppermute | solution.py:198
  451.7 3.2 collective-permute-done.7
  455.4 9.5 %collective-permute-done.6 = bf16[1,1,5,64,512]{4,3,2,1,0:T(8,128)(2,1)S(1)} collective-permute-done((bf16[1,1,5,64,512]{4,3,2,1,0:T(8,128)(2,1)S(1)}, bf16[1,1,5,64,512]{4,3,2,1,0:T(8,128)(2,1)S(1)}, u32[]{:S(2)}, u32[]{:S(2)}) %collective-permute-start.6) | collective-permute-done | bytes 327712 | tf_op jit(solution)/shard_map/ppermute | solution.py:198
  469.2 2.8 collective-permute-done.18
  473.4 3.5 gather_fusion.1
  478.2 2.3 fusion.104
  480.5 2.3 copy.244
  482.8 2.7 fusion.90
  485.5 10.8 %fusion.271 = (f32[512]{0:T(512)S(1)}, f32[1024,512]{1,0:T(8,128)}) fusion(bf16[512,2048]{0,1:T(8,128)(2,1)S(1)} %bitcast.593, f32[1024,2048]{1,0:T(8,128)} %get-tuple-element.396, f32[1024,2048]{1,0:T(8,128)} %get-tuple-element.379), kind=kOutput, calls=%fused_computation.568 | convolution fusion | flops 2166881792 | bytes 20973568 | tf_op jit(solution)/shard_map/dot_general | solution.py:77
  496.3 2.9 copy.228
  499.2 2.5 fusion.29
  501.7 3.6 fusion.28
  505.4 3.0 copy.245
  508.7 39.9 %psum.7 = f32[27,512]{1,0:T(8,128)S(1)} all-reduce(f32[27,512]{1,0:T(8,128)S(1)} %concatenate.124), channel_id=1, replica_groups=mesh['utt'=4,'tm'=8] {'utt','tm'}, use_global_device_ids=true, to_apply=%region_67.68 | all-reduce | flops 13824 | bytes 110592 | tf_op jit(solution)/shard_map/psum | solution.py:516
  549.4 3.4 fusion.246
  (746 shorter events, 151.7 us)
Async XLA Ops:
  7.2 51.4 %all-gather.9.cloned.1.call-start = ((), (), s32[]{:S(2)}) async-start(), calls=%async_computation.1 | async-start | bytes 2621440 | tf_op jit(solution)/shard_map/all_gather | solution.py:220
  9.8 89.7 %all-gather.11.cloned.1.call-start = ((), (), s32[]{:S(2)}) async-start(), calls=%async_computation.3 | async-start | bytes 4718592 | tf_op jit(solution)/shard_map/all_gather | solution.py:224
  61.7 87.9 %all-gather.13.cloned.1.call-start = ((), (), s32[]{:S(2)}) async-start(), calls=%async_computation.4 | async-start | bytes 8257536 | tf_op jit(solution)/shard_map/all_gather | solution.py:224
  62.7 8.5 %copy-start.235 = (u32[32]{0:T(128)S(1)}, u32[32]{0:T(128)}, u32[]{:S(2)}) copy-start(u32[32]{0:T(128)} %constant.252) | copy-start | bytes 388
  62.7 25.7 %copy-start.79 = (bf16[1,1024,512]{2,1,0:T(8,128)(2,1)S(1)}, bf16[1,1024,512]{2,1,0:T(8,128)(2,1)}, u32[]{:S(2)}) copy-start(bf16[1,1024,512]{2,1,0:T(8,128)(2,1)} %param.17) | copy-start | bytes 3145732
  62.8 486.6 %reduce-scatter.2.cloned.1.call-start = ((), (), s32[]{:S(2)}) async-start(), calls=%async_computation.2 | async-start | bytes 2621440 | tf_op jit(solution)/shard_map/reduce_scatter | solution.py:492
  62.8 27.0 %copy-start.220 = (s32[1,1024]{1,0:T(1,128)S(1)}, s32[1,1024]{1,0:T(1,128)}, u32[]{:S(2)}) copy-start(s32[1,1024]{1,0:T(1,128)} %param.18) | copy-start | bytes 12292
  63.4 51.6 %copy-start.5 = (bf16[1,1024,512]{1,2,0:T(8,128)(2,1)}, bf16[1,1024,512]{1,2,0:T(8,128)(2,1)S(1)}, u32[]{:S(2)}) copy-start(bf16[1,1024,512]{1,2,0:T(8,128)(2,1)S(1)} %copy.210) | copy-start | bytes 3145732
  91.8 11.6 %copy-start.115 = (f32[8,512]{1,0:T(8,128)}, f32[8,512]{1,0:T(8,128)S(1)}, u32[]{:S(2)}) copy-start(f32[8,512]{1,0:T(8,128)S(1)} %get-tuple-element.262) | copy-start | bytes 49156
  92.1 11.4 %copy-start.110 = (f32[8,512]{1,0:T(8,128)}, f32[8,512]{1,0:T(8,128)S(1)}, u32[]{:S(2)}) copy-start(f32[8,512]{1,0:T(8,128)S(1)} %get-tuple-element.263) | copy-start | bytes 49156
  92.1 11.4 %copy-start.118 = (f32[8,512]{1,0:T(8,128)}, f32[8,512]{1,0:T(8,128)S(1)}, u32[]{:S(2)}) copy-start(f32[8,512]{1,0:T(8,128)S(1)} %get-tuple-element.264) | copy-start | bytes 49156
  94.0 14.2 %copy-start.125 = (f32[1024]{0:T(1024)}, f32[1024]{0:T(1024)S(1)}, u32[]{:S(2)}) copy-start(f32[1024]{0:T(1024)S(1)} %broadcast_multiply_fusion.17) | copy-start | bytes 12292
  94.4 13.8 %copy-start.155 = (f32[1024]{0:T(1024)}, f32[1024]{0:T(1024)S(1)}, u32[]{:S(2)}) copy-start(f32[1024]{0:T(1024)S(1)} %add_rsqrt_fusion.5) | copy-start | bytes 12292
  95.0 13.2 %copy-start.195 = (f32[1,512]{1,0:T(1,128)}, f32[1,512]{1,0:T(1,128)S(1)}, u32[]{:S(2)}) copy-start(f32[1,512]{1,0:T(1,128)S(1)} %get-tuple-element.329) | copy-start | bytes 6148
  95.0 13.2 %copy-start.226 = (f32[1,512]{1,0:T(1,128)}, f32[1,512]{1,0:T(1,128)S(1)}, u32[]{:S(2)}) copy-start(f32[1,512]{1,0:T(1,128)S(1)} %get-tuple-element.328) | copy-start | bytes 6148
  95.0 22.9 %copy-start.161 = (f32[1,512]{1,0:T(1,128)}, f32[1,512]{1,0:T(1,128)S(1)}, u32[]{:S(2)}) copy-start(f32[1,512]{1,0:T(1,128)S(1)} %get-tuple-element.327) | copy-start | bytes 6148
  108.2 6.9 %copy-start.70 = (bf16[4,8,64,512]{3,2,1,0:T(8,128)(2,1)}, bf16[4,8,64,512]{3,2,1,0:T(8,128)(2,1)S(1)}, u32[]{:S(2)}) copy-start(bf16[4,8,64,512]{3,2,1,0:T(8,128)(2,1)S(1)} %copy.214) | copy-start | bytes 6291460
  117.8 35.0 %copy-start.157 = (f32[1024]{0:T(1024)}, f32[1024]{0:T(1024)S(1)}, u32[]{:S(2)}) copy-start(f32[1024]{0:T(1024)S(1)} %add_rsqrt_fusion.4) | copy-start | bytes 12292
  119.2 35.6 %copy-start.80 = (bf16[1024,512]{0,1:T(8,128)(2,1)}, bf16[1024,512]{0,1:T(8,128)(2,1)S(1)}, u32[]{:S(2)}) copy-start(bf16[1024,512]{0,1:T(8,128)(2,1)S(1)} %add_convert_fusion.3) | copy-start | bytes 3145732
  154.5 18.9 %copy-start.86 = (bf16[512,256]{0,1:T(8,128)(2,1)}, bf16[512,256]{0,1:T(8,128)(2,1)S(1)}, u32[]{:S(2)}) copy-start(bf16[512,256]{0,1:T(8,128)(2,1)S(1)} %get-tuple-element.296) | copy-start | bytes 786436
  154.8 12.7 %copy-start.31 = (f32[1024,256]{0,1:T(8,128)}, f32[1024,256]{0,1:T(8,128)S(1)}, u32[]{:S(2)}) copy-start(f32[1024,256]{0,1:T(8,128)S(1)} %get-tuple-element.299) | copy-start | bytes 3145732
  156.5 22.9 %copy-start.37 = (bf16[512,512]{0,1:T(8,128)(2,1)}, bf16[512,512]{0,1:T(8,128)(2,1)S(1)}, u32[]{:S(2)}) copy-start(bf16[512,512]{0,1:T(8,128)(2,1)S(1)} %get-tuple-element.301) | copy-start | bytes 1572868
  168.6 10.8 %copy-start.53 = (f32[512,256]{0,1:T(8,128)}, f32[512,256]{0,1:T(8,128)S(1)}, u32[]{:S(2)}) copy-start(f32[512,256]{0,1:T(8,128)S(1)} %get-tuple-element.288) | copy-start | bytes 1572868
  168.6 11.4 %copy-start.46 = (f32[512,256]{0,1:T(8,128)}, f32[512,256]{0,1:T(8,128)S(1)}, u32[]{:S(2)}) copy-start(f32[512,256]{0,1:T(8,128)S(1)} %get-tuple-element.405) | copy-start | bytes 1572868
  183.1 8.9 %slice-start.3 = ((s8[7340032]{0:T(1024)(128)(4,1)}), s8[4194304]{0:T(1024)(128)(4,1)S(1)}, s32[]{:S(2)}) async-start(s8[7340032]{0:T(1024)(128)(4,1)} %bitcast.555), calls=%async_computation.8 | async-start | bytes 8388608
  183.4 8.6 %slice-start.4 = ((s8[7340032]{0:T(1024)(128)(4,1)}), s8[3145728]{0:T(1024)(128)(4,1)S(1)}, s32[]{:S(2)}) async-start(s8[7340032]{0:T(1024)(128)(4,1)} %bitcast.555), calls=%async_computation.9 | async-start | bytes 6291456
  187.6 14.1 %collective-permute-start = (bf16[7,512]{1,0:T(8,128)(2,1)}, bf16[7,512]{1,0:T(8,128)(2,1)S(1)}, u32[]{:S(2)}, u32[]{:S(2)}) collective-permute-start(bf16[7,512]{1,0:T(8,128)(2,1)} %get-tuple-element.291), channel_id=1, source_target_pairs={{0,1},{1,2},{2,3},{3,4},{4,5},{5,6},{6,7},{8,9},{9,10},{10,11},{11... | collective-permute-start | bytes 21512 | tf_op jit(solution)/shard_map/ppermute | solution.py:57
  190.7 11.1 %collective-permute-start.1 = (bf16[7,512]{1,0:T(8,128)(2,1)}, bf16[7,512]{1,0:T(8,128)(2,1)S(1)}, u32[]{:S(2)}, u32[]{:S(2)}) collective-permute-start(bf16[7,512]{1,0:T(8,128)(2,1)} %get-tuple-element.292), channel_id=1, source_target_pairs={{1,0},{2,1},{3,2},{4,3},{5,4},{6,5},{7,6},{9,8},{10,9},{11,10},{12... | collective-permute-start | bytes 21512 | tf_op jit(solution)/shard_map/ppermute | solution.py:59
  201.8 9.1 %copy-start.121 = (bf16[7,512]{1,0:T(8,128)(2,1)}, bf16[7,512]{1,0:T(8,128)(2,1)S(1)}, u32[]{:S(2)}) copy-start(bf16[7,512]{1,0:T(8,128)(2,1)S(1)} %collective-permute-done) | copy-start | bytes 21508
  201.8 57.9 %copy-start.123 = (bf16[7,512]{1,0:T(8,128)(2,1)}, bf16[7,512]{1,0:T(8,128)(2,1)S(1)}, u32[]{:S(2)}) copy-start(bf16[7,512]{1,0:T(8,128)(2,1)S(1)} %collective-permute-done.1) | copy-start | bytes 21508
  202.1 8.8 %copy-start.96 = (bf16[1,8,64,512]{3,2,0,1:T(8,128)(2,1)S(1)}, bf16[1,8,64,512]{3,2,0,1:T(8,128)(2,1)}, u32[]{:S(2)}) copy-start(bf16[1,8,64,512]{3,2,0,1:T(8,128)(2,1)} %get-tuple-element.268) | copy-start | bytes 1572868
  202.1 8.8 %copy-start.213 = (f32[1,512]{1,0:T(1,128)S(1)}, f32[1,512]{1,0:T(1,128)}, u32[]{:S(2)}) copy-start(f32[1,512]{1,0:T(1,128)} %get-tuple-element.307) | copy-start | bytes 6148
  202.1 8.8 %copy-start.230 = (f32[1,512]{1,0:T(1,128)S(1)}, f32[1,512]{1,0:T(1,128)}, u32[]{:S(2)}) copy-start(f32[1,512]{1,0:T(1,128)} %get-tuple-element.306) | copy-start | bytes 6148
  212.2 6.6 %copy-start.13 = (f32[1024,512]{0,1:T(8,128)}, f32[1024,512]{0,1:T(8,128)S(1)}, u32[]{:S(2)}) copy-start(f32[1024,512]{0,1:T(8,128)S(1)} %get-tuple-element.387) | copy-start | bytes 6291460
  267.0 18.6 %collective-permute-start.2 = (bf16[7,512]{1,0:T(8,128)(2,1)}, bf16[7,512]{1,0:T(8,128)(2,1)}, u32[]{:S(2)}, u32[]{:S(2)}) collective-permute-start(bf16[7,512]{1,0:T(8,128)(2,1)} %get-tuple-element.289), channel_id=1, source_target_pairs={{1,0},{2,1},{3,2},{4,3},{5,4},{6,5},{7,6},{9,8},{10,9},{11,10},{12... | collective-permute-start | bytes 21512 | tf_op jit(solution)/shard_map/ppermute | solution.py:59
  268.2 17.3 %collective-permute-start.3 = (bf16[7,512]{1,0:T(8,128)(2,1)}, bf16[7,512]{1,0:T(8,128)(2,1)}, u32[]{:S(2)}, u32[]{:S(2)}) collective-permute-start(bf16[7,512]{1,0:T(8,128)(2,1)} %get-tuple-element.290), channel_id=1, source_target_pairs={{0,1},{1,2},{2,3},{3,4},{4,5},{5,6},{6,7},{8,9},{9,10},{10,11},{11... | collective-permute-start | bytes 21512 | tf_op jit(solution)/shard_map/ppermute | solution.py:57
  284.3 11.6 %copy-start.33 = (f32[1024,512]{1,0:T(8,128)S(1)}, f32[1024,512]{1,0:T(8,128)}, u32[]{:S(2)}) copy-start(f32[1024,512]{1,0:T(8,128)} %get-tuple-element.385) | copy-start | bytes 6291460
  284.4 133.7 %collective-permute-start.14 = (bf16[4,1,9,64,512]{4,3,0,2,1:T(8,128)(2,1)}, bf16[4,1,9,64,512]{4,3,0,2,1:T(8,128)(2,1)}, u32[]{:S(2)}, u32[]{:S(2)}) collective-permute-start(bf16[4,1,9,64,512]{4,3,0,2,1:T(8,128)(2,1)} %dynamic-slice_bitcast_fusion.1), channel_id=1, source_target_pairs={{0,1},{1,0},{2,3},{3,2},{4,5},{5,4},{6,7},{7,6},{8,9},{9,8},{10,11... | collective-permute-start | bytes 7077896 | tf_op jit(solution)/shard_map/ppermute | solution.py:198
  320.6 27.1 %copy-start.221 = (f32[8]{0:T(128)S(1)}, f32[8]{0:T(128)}, u32[]{:S(2)}) copy-start(f32[8]{0:T(128)} %slice_reduce_fusion.4) | copy-start | bytes 100
  321.6 26.1 %copy-start.47 = (f32[512,256]{0,1:T(8,128)S(1)}, f32[512,256]{0,1:T(8,128)}, u32[]{:S(2)}) copy-start(f32[512,256]{0,1:T(8,128)} %copy-done.46) | copy-start | bytes 1572868
  335.9 12.7 %copy-start.112 = (f32[512,8]{0,1:T(8,128)S(1)}, f32[512,8]{0,1:T(8,128)}, u32[]{:S(2)}) copy-start(f32[512,8]{0,1:T(8,128)} %get-tuple-element.401) | copy-start | bytes 49156
  377.2 6.9 %copy-start.41 = (bf16[8,64,512]{2,1,0:T(8,128)(2,1)S(1)}, bf16[8,64,512]{2,1,0:T(8,128)(2,1)}, u32[]{:S(2)}) copy-start(bf16[8,64,512]{2,1,0:T(8,128)(2,1)} %copy-done.40) | copy-start | bytes 1572868
  377.2 6.9 %copy-start.43 = (bf16[8,64,512]{2,1,0:T(8,128)(2,1)S(1)}, bf16[8,64,512]{2,1,0:T(8,128)(2,1)}, u32[]{:S(2)}) copy-start(bf16[8,64,512]{2,1,0:T(8,128)(2,1)} %copy-done.42) | copy-start | bytes 1572868
  386.4 18.5 %collective-permute-start.9 = (bf16[4,1,3,64,512]{4,3,0,2,1:T(8,128)(2,1)}, bf16[4,1,3,64,512]{4,3,0,2,1:T(8,128)(2,1)}, u32[]{:S(2)}, u32[]{:S(2)}) collective-permute-start(bf16[4,1,3,64,512]{4,3,0,2,1:T(8,128)(2,1)} %dynamic-slice_bitcast_fusion.2), channel_id=1, source_target_pairs={{0,1},{1,0},{2,3},{3,2},{4,5},{5,4},{6,7},{7,6},{8,9},{9,8},{10,11... | collective-permute-start | bytes 2359304 | tf_op jit(solution)/shard_map/ppermute | solution.py:198
  403.8 20.9 %collective-permute-start.4 = (bf16[4,1,10,64,512]{4,3,0,2,1:T(8,128)(2,1)}, bf16[4,1,10,64,512]{4,3,0,2,1:T(8,128)(2,1)}, u32[]{:S(2)}, u32[]{:S(2)}) collective-permute-start(bf16[4,1,10,64,512]{4,3,0,2,1:T(8,128)(2,1)} %dynamic-slice_bitcast_fusion), channel_id=1, source_target_pairs={{0,1},{1,0},{2,3},{3,2},{4,5},{5,4},{6,7},{7,6},{8,9},{9,8},{10,11... | collective-permute-start | bytes 7864328 | tf_op jit(solution)/shard_map/ppermute | solution.py:198
  406.6 5.9 %collective-permute-start.10 = (bf16[2,1,1,64,512]{4,3,0,2,1:T(8,128)(2,1)S(1)}, bf16[2,1,1,64,512]{4,3,0,2,1:T(8,128)(2,1)S(1)}, u32[]{:S(2)}, u32[]{:S(2)}) collective-permute-start(bf16[2,1,1,64,512]{4,3,0,2,1:T(8,128)(2,1)S(1)} %dynamic-slice_bitcast_fusion.5), channel_id=1, source_target_pairs={{0,2},{1,3},{2,0},{3,1},{4,6},{5,7},{6,4},{7,5},{8,10},{9,11},{10,... | collective-permute-start | bytes 393224 | tf_op jit(solution)/shard_map/ppermute | solution.py:198
  406.8 9.2 %collective-permute-start.12 = (bf16[1,2,2,64,512]{4,3,1,2,0:T(8,128)(2,1)S(1)}, bf16[1,2,2,64,512]{4,3,1,2,0:T(8,128)(2,1)S(1)}, u32[]{:S(2)}, u32[]{:S(2)}) collective-permute-start(bf16[1,2,2,64,512]{4,3,1,2,0:T(8,128)(2,1)S(1)} %dynamic-slice_bitcast_fusion.4), channel_id=1, source_target_pairs={{0,4},{1,5},{2,6},{3,7},{4,0},{5,1},{6,2},{7,3},{8,12},{9,13},{10,... | collective-permute-start | bytes 786440 | tf_op jit(solution)/shard_map/ppermute | solution.py:198
  412.6 54.6 %collective-permute-start.11 = (bf16[1,1,1,64,512]{4,3,0,2,1:T(8,128)(2,1)S(1)}, bf16[1,1,1,64,512]{4,3,0,2,1:T(8,128)(2,1)S(1)}, u32[]{:S(2)}, u32[]{:S(2)}) collective-permute-start(bf16[1,1,1,64,512]{4,3,0,2,1:T(8,128)(2,1)S(1)} %constant_dynamic-slice_fusion.7), channel_id=1, source_target_pairs={{0,4},{1,5},{2,6},{3,7},{4,0},{5,1},{6,2},{7,3},{8,12},{9,13},{10,... | collective-permute-start | bytes 196616 | tf_op jit(solution)/shard_map/ppermute | solution.py:198
  416.1 51.6 %collective-permute-start.13 = (bf16[1,1,2,64,512]{4,3,1,2,0:T(8,128)(2,1)S(1)}, bf16[1,1,2,64,512]{4,3,1,2,0:T(8,128)(2,1)S(1)}, u32[]{:S(2)}, u32[]{:S(2)}) collective-permute-start(bf16[1,1,2,64,512]{4,3,1,2,0:T(8,128)(2,1)S(1)} %constant_dynamic-slice_fusion.6), channel_id=1, source_target_pairs={{0,2},{1,3},{2,0},{3,1},{4,6},{5,7},{6,4},{7,5},{8,10},{9,11},{10,... | collective-permute-start | bytes 393224 | tf_op jit(solution)/shard_map/ppermute | solution.py:198
  418.1 6.6 %slice-start = ((s8[5242880]{0:T(1024)(128)(4,1)}), s8[4194304]{0:T(1024)(128)(4,1)S(1)}, s32[]{:S(2)}) async-start(s8[5242880]{0:T(1024)(128)(4,1)} %bitcast.533), calls=%async_computation.5 | async-start | bytes 8388608
  423.2 17.7 %collective-permute-start.17 = (bf16[1,2,5,64,512]{4,3,2,1,0:T(8,128)(2,1)S(1)}, bf16[1,2,5,64,512]{4,3,2,1,0:T(8,128)(2,1)S(1)}, u32[]{:S(2)}, u32[]{:S(2)}) collective-permute-start(bf16[1,2,5,64,512]{4,3,2,1,0:T(8,128)(2,1)S(1)} %bitcast.620), channel_id=1, source_target_pairs={{0,4},{1,5},{2,6},{3,7},{4,0},{5,1},{6,2},{7,3},{8,12},{9,13},{10,... | collective-permute-start | bytes 1966088 | tf_op jit(solution)/shard_map/ppermute | solution.py:198
  424.5 12.2 %collective-permute-start.15 = (bf16[2,1,4,64,512]{4,3,2,1,0:T(8,128)(2,1)S(1)}, bf16[2,1,4,64,512]{4,3,2,1,0:T(8,128)(2,1)S(1)}, u32[]{:S(2)}, u32[]{:S(2)}) collective-permute-start(bf16[2,1,4,64,512]{4,3,2,1,0:T(8,128)(2,1)S(1)} %bitcast.628), channel_id=1, source_target_pairs={{0,2},{1,3},{2,0},{3,1},{4,6},{5,7},{6,4},{7,5},{8,10},{9,11},{10,... | collective-permute-start | bytes 1572872 | tf_op jit(solution)/shard_map/ppermute | solution.py:198
  427.8 27.1 %collective-permute-start.7 = (bf16[1,2,5,64,512]{4,3,1,2,0:T(8,128)(2,1)S(1)}, bf16[1,2,5,64,512]{4,3,1,2,0:T(8,128)(2,1)S(1)}, u32[]{:S(2)}, u32[]{:S(2)}) collective-permute-start(bf16[1,2,5,64,512]{4,3,1,2,0:T(8,128)(2,1)S(1)} %dynamic-slice_bitcast_fusion.3), channel_id=1, source_target_pairs={{0,4},{1,5},{2,6},{3,7},{4,0},{5,1},{6,2},{7,3},{8,12},{9,13},{10,... | collective-permute-start | bytes 1966088 | tf_op jit(solution)/shard_map/ppermute | solution.py:198
  436.7 14.1 %collective-permute-start.5 = (bf16[2,1,5,64,512]{4,3,2,1,0:T(8,128)(2,1)S(1)}, bf16[2,1,5,64,512]{4,3,2,1,0:T(8,128)(2,1)S(1)}, u32[]{:S(2)}, u32[]{:S(2)}) collective-permute-start(bf16[2,1,5,64,512]{4,3,2,1,0:T(8,128)(2,1)S(1)} %bitcast.621), channel_id=1, source_target_pairs={{0,2},{1,3},{2,0},{3,1},{4,6},{5,7},{6,4},{7,5},{8,10},{9,11},{10,... | collective-permute-start | bytes 1966088 | tf_op jit(solution)/shard_map/ppermute | solution.py:198
  440.9 27.6 %collective-permute-start.16 = (bf16[1,1,4,64,512]{4,3,2,1,0:T(8,128)(2,1)S(1)}, bf16[1,1,4,64,512]{4,3,2,1,0:T(8,128)(2,1)S(1)}, u32[]{:S(2)}, u32[]{:S(2)}) collective-permute-start(bf16[1,1,4,64,512]{4,3,2,1,0:T(8,128)(2,1)S(1)} %constant_dynamic-slice_fusion.3), channel_id=1, source_target_pairs={{0,4},{1,5},{2,6},{3,7},{4,0},{5,1},{6,2},{7,3},{8,12},{9,13},{10,... | collective-permute-start | bytes 786440 | tf_op jit(solution)/shard_map/ppermute | solution.py:198
  451.0 13.9 %collective-permute-start.6 = (bf16[1,1,5,64,512]{4,3,2,1,0:T(8,128)(2,1)S(1)}, bf16[1,1,5,64,512]{4,3,2,1,0:T(8,128)(2,1)S(1)}, u32[]{:S(2)}, u32[]{:S(2)}) collective-permute-start(bf16[1,1,5,64,512]{4,3,2,1,0:T(8,128)(2,1)S(1)} %constant_dynamic-slice_fusion.9), channel_id=1, source_target_pairs={{0,4},{1,5},{2,6},{3,7},{4,0},{5,1},{6,2},{7,3},{8,12},{9,13},{10,... | collective-permute-start | bytes 983048 | tf_op jit(solution)/shard_map/ppermute | solution.py:198
  455.2 11.1 %collective-permute-start.8 = (bf16[1,1,5,64,512]{4,3,1,2,0:T(8,128)(2,1)S(1)}, bf16[1,1,5,64,512]{4,3,1,2,0:T(8,128)(2,1)S(1)}, u32[]{:S(2)}, u32[]{:S(2)}) collective-permute-start(bf16[1,1,5,64,512]{4,3,1,2,0:T(8,128)(2,1)S(1)} %constant_dynamic-slice_fusion.8), channel_id=1, source_target_pairs={{0,2},{1,3},{2,0},{3,1},{4,6},{5,7},{6,4},{7,5},{8,10},{9,11},{10,... | collective-permute-start | bytes 983048 | tf_op jit(solution)/shard_map/ppermute | solution.py:198
  464.9 7.1 %collective-permute-start.18 = (bf16[1,1,5,64,512]{4,3,2,1,0:T(8,128)(2,1)S(1)}, bf16[1,1,5,64,512]{4,3,2,1,0:T(8,128)(2,1)S(1)}, u32[]{:S(2)}, u32[]{:S(2)}) collective-permute-start(bf16[1,1,5,64,512]{4,3,2,1,0:T(8,128)(2,1)S(1)} %constant_dynamic-slice_fusion), channel_id=1, source_target_pairs={{0,2},{1,3},{2,0},{3,1},{4,6},{5,7},{6,4},{7,5},{8,10},{9,11},{10,... | collective-permute-start | bytes 983048 | tf_op jit(solution)/shard_map/ppermute | solution.py:198
  505.3 43.3 %copy-start.109 = (f32[27,512]{1,0:T(8,128)S(1)}, f32[27,512]{1,0:T(8,128)}, u32[]{:S(2)}) copy-start(f32[27,512]{1,0:T(8,128)} %param.25) | copy-start | bytes 165892
  505.4 43.3 %copy-start.129 = (f32[27,512]{1,0:T(8,128)S(1)}, f32[27,512]{1,0:T(8,128)}, u32[]{:S(2)}) copy-start(f32[27,512]{1,0:T(8,128)} %param.26) | copy-start | bytes 165892
  505.4 43.3 %copy-start.130 = (f32[27,512]{1,0:T(8,128)S(1)}, f32[27,512]{1,0:T(8,128)}, u32[]{:S(2)}) copy-start(f32[27,512]{1,0:T(8,128)} %param.27) | copy-start | bytes 165892
  505.4 44.0 %copy-start.55 = (f32[64,8,512]{2,1,0:T(8,128)S(1)}, f32[64,8,512]{2,1,0:T(8,128)}, u32[]{:S(2)}) copy-start(f32[64,8,512]{2,1,0:T(8,128)} %param.22) | copy-start | bytes 3145732
  505.4 43.9 %copy-start.76 = (f32[64,8,512]{2,1,0:T(8,128)S(1)}, f32[64,8,512]{2,1,0:T(8,128)}, u32[]{:S(2)}) copy-start(f32[64,8,512]{2,1,0:T(8,128)} %param.23) | copy-start | bytes 3145732
  505.4 43.9 %copy-start.77 = (f32[64,8,512]{2,1,0:T(8,128)S(1)}, f32[64,8,512]{2,1,0:T(8,128)}, u32[]{:S(2)}) copy-start(f32[64,8,512]{2,1,0:T(8,128)} %param.24) | copy-start | bytes 3145732
  (208 other events, 569.1 us)
Sparse Core Ops, SparseCore 0:
  10.1 48.3 all-gather.8
  61.8 35.5 all-gather.10
  99.8 49.7 all-gather.12
  477.1 43.6 reduce-scatter.1

commit v2 on v1

--- a/solution.py
+++ b/solution.py
@@ -1,6 +1,10 @@
+import functools
+
 import jax
 import jax.numpy as jnp
 from jax import lax
+from jax.experimental import pallas as pl
+from jax.experimental.pallas import tpu as pltpu
 from jax.sharding import PartitionSpec as P
 
 D = 512
@@ -21,29 +25,6 @@
 RATE_VECTORS = 0.1
 DECAY_TILES = 0.1
 PRECISE = lax.Precision.HIGHEST
-
-
-def entering_2(shard, axis, join, neutral, backward):
-    count = lax.axis_size(axis)
-    place = lax.axis_index(axis)
-    ahead = count - 1 - place if backward else place
-    gathered = jax.tree.map(
-        lambda a, kind: lax.all_gather(a.astype(kind), axis), shard, (jnp.bfloat16, jnp.bfloat16)
-    )
-    state = jax.tree.map(lambda a, e: jnp.zeros_like(a) + jnp.asarray(e, a.dtype), shard, neutral)
-
-    def one(lap, state):
-        source = count - 1 - lap if backward else lap
-        return join(
-            state,
-            jax.tree.map(
-                lambda a, own: lax.dynamic_index_in_dim(a, source, 0, False).astype(own.dtype),
-                gathered,
-                shard,
-            ),
-        )
-
-    return lax.fori_loop(0, ahead, one, state)
 
 
 def padded_2(cells, sides, width):
@@ -101,45 +82,6 @@
     return sigmoid_of * (1.0 + pre_act * (1.0 - sigmoid_of))
 
 
-def split_tiles(tile_values):
-    blocks_ff = FF // D
-    offset = 2 * blocks_ff
-    up_first = tile_values[0:blocks_ff].transpose(1, 0, 2).reshape(D, FF)
-    down_first = tile_values[blocks_ff:offset].reshape(FF, D)
-    mixers = [tile_values[offset + number] for number in range(6)]
-    up_second = tile_values[offset + 6 : offset + 6 + blocks_ff].transpose(1, 0, 2).reshape(D, FF)
-    down_second = tile_values[offset + 6 + blocks_ff : offset + 6 + 2 * blocks_ff].reshape(FF, D)
-    return (up_first, down_first, mixers, up_second, down_second)
-
-
-def column_tiles(full_grad):
-    blocks_ff = FF // D
-    return full_grad.reshape(D, blocks_ff, D).transpose(1, 0, 2)
-
-
-def ffn_forward(start_x, up_weight, down_weight, norm_gain, norm_shift):
-    normed_out, normed, inverse_dev = layer_norm(start_x, norm_gain, norm_shift)
-    normed_low = normed_out.astype(jnp.bfloat16)
-    hidden = product(normed_low, up_weight)
-    activated = (hidden * jax.nn.sigmoid(hidden)).astype(jnp.bfloat16)
-    return (
-        start_x + 0.5 * product(activated, down_weight),
-        (normed, inverse_dev, normed_low, hidden, activated),
-    )
-
-
-def ffn_backward(grad_after, kept, up_weight, down_weight, norm_gain):
-    normed, inverse_dev, normed_low, hidden, activated = kept
-    down_in = (0.5 * grad_after).astype(jnp.bfloat16)
-    grad_down = weight_grad(activated, down_in)
-    hidden_grad = (input_grad(down_in, down_weight) * swish_slope(hidden)).astype(jnp.bfloat16)
-    grad_up = weight_grad(normed_low, hidden_grad)
-    grad_normed, gain_grad, shift_grad = norm_grad(
-        input_grad(hidden_grad, up_weight), normed, inverse_dev, norm_gain
-    )
-    return (grad_after + grad_normed, grad_up, grad_down, gain_grad, shift_grad)
-
-
 def block_weights(log_piece, seg_piece, seg_prior):
     cumulative = jnp.cumsum(log_piece, axis=1)
     row_index = jnp.arange(seg_piece.shape[0], dtype=jnp.int32)
@@ -153,10 +95,6 @@
         (seg_piece == seg_piece[-1])[None, :], jnp.exp(cumulative[:, -1:] - cumulative), 0.0
     )
     return (within, entering, leaving)
-
-
-def chain_states(earlier, latter):
-    return (latter[0] * earlier[0], latter[0][:, None, None] * earlier[1] + latter[1])
 
 
 def adam_step(master, first_old, second, gradient, step_rate, decay_rate):
@@ -170,14 +108,46 @@
     return (master_new, first_new, second_new)
 
 
+VEC_ROWS = 32
+ROW_STEP = 256
+ORDER = tuple(range(8)) + tuple(range(14, 22)) + tuple(range(8, 14))
+MESH = pl.DeviceIdType.MESH
+
+
+def entry_of(local_state, carry, scales):
+    count = lax.axis_size("tm")
+    place = lax.axis_index("tm")
+    backward = scales is not None
+    sent = local_state.astype(jnp.bfloat16)
+    if not backward:
+        row = jnp.broadcast_to(carry[:, None, None], (H, 1, P_SIZE)).astype(jnp.bfloat16)
+        sent = jnp.concatenate([sent, row], axis=1)
+    arrived = lax.all_gather(sent, "tm")
+    if not backward:
+        scales = arrived[:, :, NS, 0].astype(jnp.float32)
+        arrived = arrived[:, :, :NS]
+    source = jnp.arange(count)[:, None]
+    between = jnp.arange(count)[None, :]
+    if backward:
+        passed = (between < source) & (between > place)
+        ahead = source > place
+    else:
+        passed = (between > source) & (between < place)
+        ahead = source < place
+    weights = jnp.prod(jnp.where(passed[:, :, None], scales[None], 1.0), axis=1)
+    weights = jnp.where(ahead, weights, 0.0)
+    state = jnp.sum(weights[:, :, None, None] * arrived.astype(jnp.float32), axis=0)
+    return state, scales
+
+
 def halving_sum(cells, axis):
     bits = lax.axis_size(axis).bit_length() - 1
-    count = cells.shape[1]
+    cut = cells.shape[1] // 32 * 16
     cells = exchange_bit(cells, axis, 0, 0)
     parts = []
     for piece, order in (
-        (cells[:, : count // 2], list(range(bits - 1))),
-        (cells[:, count // 2 :], list(reversed(range(bits - 1)))),
+        (cells[:, :cut], list(range(bits - 1))),
+        (cells[:, cut:], list(reversed(range(bits - 1)))),
     ):
         left = list(range(bits - 1))
         for bit in order:
@@ -198,6 +168,340 @@
     got = lax.ppermute(sent, axis, [(i, i ^ (1 << bit)) for i in range(count)])
     total = (kept.astype(jnp.float32) + got.astype(jnp.float32)).astype(cells.dtype)
     return total.reshape(shape[0] // 2, *shape[1:])
+
+
+def gather_kernel(owners, count, slots_ref, own_ref, full_ref, line, chosen, up_s, up_r, down_s, down_r, own_sem, tm_s, tm_r):
+    capacity = own_ref.shape[0]
+    tiles = chosen.shape[0]
+    place = lax.axis_index("utt")
+    me = lax.axis_index("tm")
+    bits = count.bit_length() - 1
+    barrier = pltpu.get_barrier_semaphore()
+    for step in (1, -1):
+
+        @pl.when((place + step >= 0) & (place + step < owners))
+        def _():
+            pl.semaphore_signal(
+                barrier, inc=1, device_id={"utt": place + step}, device_id_type=MESH
+            )
+
+    for bit in range(bits):
+        pl.semaphore_signal(
+            barrier, inc=1, device_id={"tm": partner(me, 1 << bit)}, device_id_type=MESH
+        )
+    beside = (place + owners - 1) // owners + (2 * owners - 2 - place) // owners
+    pl.semaphore_wait(barrier, bits + beside)
+    own_copy = pltpu.make_async_copy(own_ref, line.at[place], own_sem.at[0])
+    own_copy.start()
+    own_copy.wait()
+
+    def hop(slot, target, send, receive):
+        return pltpu.make_async_remote_copy(
+            src_ref=line.at[slot],
+            dst_ref=line.at[slot],
+            send_sem=send,
+            recv_sem=receive,
+            device_id={"utt": target},
+            device_id_type=MESH,
+        )
+
+    def line_step(step, phase):
+        lower, upper = place - step, place + step
+
+        @pl.when((lower >= 0) & (place + 1 < owners))
+        def _():
+            copy = hop(lower, place + 1, up_s.at[step], up_r.at[step])
+            copy.start() if phase == 0 else copy.wait_send()
+
+        @pl.when((upper < owners) & (place >= 1))
+        def _():
+            copy = hop(upper, place - 1, down_s.at[step], down_r.at[step])
+            copy.start() if phase == 0 else copy.wait_send()
+
+    for step in range(owners - 1):
+        line_step(step, 0)
+
+        @pl.when(place - step >= 1)
+        def _():
+            hop(place - step - 1, place - 1, up_s.at[step], up_r.at[step]).wait_recv()
+
+        @pl.when(place + step + 1 < owners)
+        def _():
+            hop(place + step + 1, place + 1, down_s.at[step], down_r.at[step]).wait_recv()
+
+    for number in range(tiles):
+        slot = slots_ref[ORDER[number]]
+        chosen[number] = line[slot // capacity, slot % capacity]
+    local = pltpu.make_async_copy(chosen, full_ref.at[me, pl.ds(0, tiles)], own_sem.at[1])
+    local.start()
+    local.wait()
+    half = tiles // 2
+    ranges = ((0, half), (half, tiles - half))
+    orders = (list(range(1, bits)), list(reversed(range(1, bits))))
+    used = [0, 0]
+    sent = []
+
+    def start_send(piece, offset, flip):
+        start, size = ranges[piece]
+        number = used[piece]
+        used[piece] = number + 1
+        shard = partner(me, offset)
+        cells = full_ref.at[shard, pl.ds(start, size)]
+        copy = pltpu.make_async_remote_copy(
+            src_ref=cells,
+            dst_ref=cells,
+            send_sem=tm_s.at[piece, number],
+            recv_sem=tm_r.at[piece, number],
+            device_id={"tm": partner(me, flip)},
+            device_id_type=MESH,
+        )
+        copy.start()
+        sent.append(copy)
+        return copy
+
+    held = [[0], [0]]
+    over_cores = [start_send(piece, 0, 1) for piece in range(2)]
+    for level in range(bits - 1):
+        moving = [
+            [
+                start_send(piece, offset, 1 << orders[piece][level])
+                for offset in held[piece]
+            ]
+            for piece in range(2)
+        ]
+        for piece in range(2):
+            flip = 1 << orders[piece][level]
+            fresh = [offset ^ flip for offset in held[piece]]
+            for copy, offset in zip(moving[piece], fresh):
+                copy.wait_recv()
+                over_cores.append(start_send(piece, offset, 1))
+            held[piece] = held[piece] + fresh
+    for copy in over_cores:
+        copy.wait_recv()
+    for copy in sent:
+        copy.wait_send()
+    for step in range(owners - 1):
+        line_step(step, 1)
+
+
+def partner(me, flip):
+    for bit in range(flip.bit_length()):
+        if (flip >> bit) & 1:
+            me = me + (1 << bit) * (1 - 2 * ((me // (1 << bit)) % 2))
+    return me
+
+
+def gather_tiles(own, tile_slots):
+    owners, count = lax.axis_size("utt"), lax.axis_size("tm")
+    capacity, rows, width = own.shape
+    tiles = tile_slots.shape[0]
+    dma = pltpu.SemaphoreType.DMA
+    return pl.pallas_call(
+        functools.partial(gather_kernel, owners, count),
+        out_shape=jax.ShapeDtypeStruct((count, 24, rows, width), own.dtype),
+        in_specs=[
+            pl.BlockSpec(memory_space=pltpu.SMEM),
+            pl.BlockSpec(memory_space=pl.ANY),
+        ],
+        out_specs=pl.BlockSpec(memory_space=pl.ANY),
+        scratch_shapes=[
+            pltpu.VMEM((owners, capacity, rows, width), own.dtype),
+            pltpu.VMEM((tiles, rows, width), own.dtype),
+            dma((owners - 1,)),
+            dma((owners - 1,)),
+            dma((owners - 1,)),
+            dma((owners - 1,)),
+            dma((2,)),
+            dma((2, count - 1)),
+            dma((2, count - 1)),
+        ],
+        compiler_params=pltpu.CompilerParams(
+            collective_id=0, has_side_effects=True, vmem_limit_bytes=16 << 20
+        ),
+    )(tile_slots, own)
+
+
+def gate_of(values):
+    return 0.5 * jnp.tanh(0.5 * values) + 0.5
+
+
+def norm_parts(values):
+    centered = values - jnp.mean(values, axis=-1, keepdims=True)
+    inverse_dev = lax.rsqrt(jnp.mean(centered * centered, axis=-1, keepdims=True) + NORM_EPS)
+    return centered * inverse_dev, inverse_dev
+
+
+def norm_back(gradients, normed, inverse_dev, norm_gain):
+    scaled = gradients * norm_gain
+    middle = (
+        scaled
+        - jnp.mean(scaled, axis=-1, keepdims=True)
+        - normed * jnp.mean(scaled * normed, axis=-1, keepdims=True)
+    )
+    return (
+        middle * inverse_dev,
+        jnp.sum(gradients * normed, axis=0, keepdims=True),
+        jnp.sum(gradients, axis=0, keepdims=True),
+    )
+
+
+def tile_at(tiles_ref, number):
+    return tiles_ref[:, number].reshape(D, D)
+
+
+def first_kernel(x_ref, ffn_ref, mix_ref, vec_ref, after_ref, vals_ref, kq_ref):
+    values = x_ref[...].astype(jnp.float32)
+    normed, _ = norm_parts(values)
+    low = (normed * vec_ref[0:1] + vec_ref[6:7]).astype(jnp.bfloat16)
+    total = jnp.zeros_like(values)
+    for part in range(FF // D):
+        hidden = product(low, tile_at(ffn_ref, part))
+        activated = (hidden * gate_of(hidden)).astype(jnp.bfloat16)
+        total = total + product(activated, tile_at(ffn_ref, FF // D + part))
+    after = values + 0.5 * total
+    after_ref[...] = after
+    normed, _ = norm_parts(after)
+    low = (normed * vec_ref[1:2] + vec_ref[7:8]).astype(jnp.bfloat16)
+    vals_ref[...] = product(low, tile_at(mix_ref, 0)).astype(jnp.bfloat16)
+    kq_ref[...] = product(low, tile_at(mix_ref, 1)).astype(jnp.bfloat16)
+
+
+def tile_block(gathered, number):
+    count, _, rows, width = gathered.shape
+    return pl.BlockSpec(
+        (count, 8, rows, width), lambda i: (0, number, 0, 0), pipeline_mode=pl.Buffered(1)
+    )
+
+
+def ffn_first(inputs, gathered, vectors):
+    frames = inputs.shape[0]
+    rows = pl.BlockSpec((ROW_STEP, D), lambda i: (i, 0))
+    return pl.pallas_call(
+        first_kernel,
+        grid=(frames // ROW_STEP,),
+        out_shape=(
+            jax.ShapeDtypeStruct((frames, D), jnp.float32),
+            jax.ShapeDtypeStruct((frames, D), jnp.bfloat16),
+            jax.ShapeDtypeStruct((frames, D), jnp.bfloat16),
+        ),
+        in_specs=[
+            rows,
+            tile_block(gathered, 0),
+            tile_block(gathered, 2),
+            pl.BlockSpec(vectors.shape, lambda i: (0, 0)),
+        ],
+        out_specs=(rows, rows, rows),
+        compiler_params=pltpu.CompilerParams(vmem_limit_bytes=48 << 20),
+    )(inputs, gathered, gathered, vectors)
+
+
+def back_kernel(steps, last, norm, x_ref, grad_ref, ffn_ref, vec_ref, *refs):
+    if last:
+        out_ref, *refs = refs
+    din_ref, tiles_ref, vsum_ref, low_s, act_s, dd_s, dh_s = refs
+    step = pl.program_id(0)
+    parts = FF // D
+
+    @pl.when(step == 0)
+    def _():
+        vsum_ref[...] = jnp.zeros_like(vsum_ref)
+
+    @pl.when(step < steps)
+    def _():
+        rows = pl.ds(pl.multiple_of(step * ROW_STEP, ROW_STEP), ROW_STEP)
+        values = x_ref[...].astype(jnp.float32)
+        gain, shift = vec_ref[norm : norm + 1], vec_ref[6 + norm : 7 + norm]
+        normed, inverse_dev = norm_parts(values)
+        low = (normed * gain + shift).astype(jnp.bfloat16)
+        low_s[rows] = low
+        slopes = []
+        total = jnp.zeros_like(values)
+        for part in range(parts):
+            hidden = product(low, tile_at(ffn_ref, part))
+            gate = gate_of(hidden)
+            activated = (hidden * gate).astype(jnp.bfloat16)
+            act_s[part, rows] = activated
+            slopes.append(gate * (1.0 + hidden * (1.0 - gate)))
+            if last:
+                total = total + product(activated, tile_at(ffn_ref, parts + part))
+        grad = grad_ref[...].astype(jnp.float32)
+        if last:
+            final, final_dev = norm_parts(values + 0.5 * total)
+            out_ref[...] = (final * vec_ref[5:6] + vec_ref[11:12]).astype(jnp.bfloat16)
+            grad, gain_sum, shift_sum = norm_back(grad, final, final_dev, vec_ref[5:6])
+            vsum_ref[2:3] += gain_sum
+            vsum_ref[3:4] += shift_sum
+        down_in = (0.5 * grad).astype(jnp.bfloat16)
+        dd_s[rows] = down_in
+        total = jnp.zeros_like(values)
+        for part in range(parts):
+            back = input_grad(down_in, tile_at(ffn_ref, parts + part))
+            hidden_grad = (back * slopes[part]).astype(jnp.bfloat16)
+            dh_s[part, rows] = hidden_grad
+            total = total + input_grad(hidden_grad, tile_at(ffn_ref, part))
+        through, gain_sum, shift_sum = norm_back(total, normed, inverse_dev, gain)
+        vsum_ref[0:1] += gain_sum
+        vsum_ref[1:2] += shift_sum
+        din_ref[...] = grad + through
+
+    def put(values):
+        tiles_ref[...] = values.astype(jnp.bfloat16).reshape(tiles_ref.shape)
+
+    @pl.when((step >= steps) & (step < steps + parts))
+    def _():
+        put(weight_grad(low_s[...], dh_s[step - steps]))
+
+    @pl.when(step >= steps + parts)
+    def _():
+        put(weight_grad(act_s[step - steps - parts], dd_s[...]))
+
+
+def ffn_back_call(values, grad, gathered, vectors, own_rows, last):
+    frames = values.shape[0]
+    count = gathered.shape[0]
+    steps = frames // ROW_STEP
+    parts = FF // D
+    rows = pl.BlockSpec((ROW_STEP, D), lambda i: (jnp.minimum(i, steps - 1), 0))
+    out_shape = [
+        jax.ShapeDtypeStruct((frames, D), jnp.float32),
+        jax.ShapeDtypeStruct((count, 2 * parts, own_rows, D), jnp.bfloat16),
+        jax.ShapeDtypeStruct((8, D), jnp.float32),
+    ]
+    out_specs = [
+        rows,
+        pl.BlockSpec((count, 1, own_rows, D), lambda i: (0, jnp.maximum(i - steps, 0), 0, 0)),
+        pl.BlockSpec((8, D), lambda i: (0, 0)),
+    ]
+    if last:
+        out_shape.insert(0, jax.ShapeDtypeStruct((frames, D), jnp.bfloat16))
+        out_specs.insert(0, rows)
+    return pl.pallas_call(
+        functools.partial(back_kernel, steps, last, 4 if last else 0),
+        grid=(steps + 2 * parts,),
+        out_shape=out_shape,
+        in_specs=[
+            rows,
+            rows,
+            tile_block(gathered, 1 if last else 0),
+            pl.BlockSpec(vectors.shape, lambda i: (0, 0)),
+        ],
+        out_specs=out_specs,
+        scratch_shapes=[
+            pltpu.VMEM((frames, D), jnp.bfloat16),
+            pltpu.VMEM((parts, frames, D), jnp.bfloat16),
+            pltpu.VMEM((frames, D), jnp.bfloat16),
+            pltpu.VMEM((parts, frames, D), jnp.bfloat16),
+        ],
+        compiler_params=pltpu.CompilerParams(vmem_limit_bytes=48 << 20),
+    )(values, grad, gathered, vectors)
+
+
+def ffn_second(values, cotangent, gathered, vectors, own_rows):
+    return ffn_back_call(values, cotangent, gathered, vectors, own_rows, True)
+
+
+def ffn_back(values, grad, gathered, vectors, own_rows):
+    return ffn_back_call(values, grad, gathered, vectors, own_rows, False)
 
 
 def local(
@@ -217,15 +521,10 @@
     own_rows, capacity, _ = master_weight_tiles.shape
     owners_count = lax.axis_size("utt")
     low_master = master_weight_tiles.transpose(1, 0, 2).astype(jnp.bfloat16)
-    by_slot = lax.all_gather(low_master, "utt", axis=0, tiled=True)
-    chosen = by_slot[tile_slots]
-    groups = []
-    for first, last in ((0, 8), (8, 22)):
-        part = lax.all_gather(chosen[first:last], "tm", axis=0)
-        groups.append(part.transpose(1, 0, 2, 3).reshape(last - first, D, D))
-    tile_values = jnp.concatenate(groups, axis=0)
-    up_first, down_first, mixers, up_second, down_second = split_tiles(tile_values)
-    w_values, w_states, w_output, w_linear, w_gate, w_project = mixers
+    gathered = gather_tiles(low_master, tile_slots)
+    w_values, w_states, w_output, w_linear, w_gate, w_project = [
+        gathered[:, 16 + number].reshape(D, D) for number in range(6)
+    ]
     norm_gains = vector_master[0:6]
     norm_shifts = vector_master[6:12]
     conv_taps = vector_master[12:]
@@ -240,15 +539,9 @@
     segments = segment_of(positions)
     seg_before = segment_of(jnp.reshape(first_frame - 1, (1,)))[0]
     log_decay = jnp.log(decays[0])
-    start_x = inputs[0].astype(jnp.float32)
-    after_a, kept_a = ffn_forward(start_x, up_first, down_first, norm_gains[0], norm_shifts[0])
-    normed_b_out, unit_b, inverse_b = layer_norm(after_a, norm_gains[1], norm_shifts[1])
-    low_b = normed_b_out.astype(jnp.bfloat16)
+    after_a, raw_vals, key_query = ffn_first(inputs[0], gathered, vector_master)
     live_mask = frame_mask[0].astype(jnp.bfloat16)[:, None]
-    state_vals = (product(low_b, w_values).astype(jnp.bfloat16) * live_mask).reshape(
-        frames, H, P_SIZE
-    )
-    key_query = product(low_b, w_states).astype(jnp.bfloat16)
+    state_vals = (raw_vals * live_mask).reshape(frames, H, P_SIZE)
     state_keys = key_query[:, : H * NS].reshape(frames, H, NS)
     state_query = key_query[:, H * NS :].reshape(frames, H, NS)
     keys_wide = state_keys.astype(jnp.float32)
@@ -262,10 +555,7 @@
         "shn,shp->hnp", keys_wide * tail_dev.T[:, :, None], vals_wide, precision=PRECISE
     )
     carry_dev = jnp.where(segments[-1] == seg_before, jnp.exp(total_log[:, -1]), 0.0)
-    identity = (jnp.ones((H,), jnp.float32), jnp.zeros((H, NS, P_SIZE), jnp.float32))
-    entry_scale, entry_state = entering_2(
-        (carry_dev, local_state), "tm", chain_states, identity, False
-    )
+    entry_state, all_scales = entry_of(local_state, carry_dev, None)
     count_blocks = frames // BLK
     saved_blocks = []
     outputs = []
@@ -336,14 +626,11 @@
     normed_d, unit_d, inverse_d = layer_norm(conv_sum, norm_gains[3], norm_shifts[3])
     low_d = (normed_d * jax.nn.sigmoid(normed_d)).astype(jnp.bfloat16)
     after_c = after_b + product(low_d, w_project)
-    after_e, kept_e = ffn_forward(after_c, up_second, down_second, norm_gains[4], norm_shifts[4])
-    final_out, unit_f, inverse_f = layer_norm(after_e, norm_gains[5], norm_shifts[5])
-    output = final_out.astype(jnp.bfloat16)[None]
-    grad_out = cotangent[0].astype(jnp.float32)
-    grad_e, gain_f, shift_f = norm_grad(grad_out, unit_f, inverse_f, norm_gains[5])
-    grad_c, grad_up_e, grad_down_e, gain_e, shift_e = ffn_backward(
-        grad_e, kept_e, up_second, down_second, norm_gains[4]
-    )
+    output, grad_c, tile_grads_e, vec_e = ffn_second(
+        after_c, cotangent[0], gathered, vector_master, own_rows
+    )
+    output = output[None]
+    gain_e, shift_e, gain_f, shift_f = vec_e[0], vec_e[1], vec_e[2], vec_e[3]
     project_in = grad_c.astype(jnp.bfloat16)
     grad_project = weight_grad(low_d, project_in)
     grad_swish = input_grad(project_in, w_project) * swish_slope(normed_d)
@@ -388,7 +675,7 @@
     local_back = jnp.einsum(
         "thn,thp->hnp", query_wide * entering_dev.T[:, :, None], grad_y_wide, precision=PRECISE
     )
-    exit_scale, exit_grad = entering_2((carry_dev, local_back), "tm", chain_states, identity, True)
+    exit_grad, _ = entry_of(local_back, carry_dev, all_scales)
     incoming = exit_grad
     vals_parts = []
     keys_parts = []
@@ -446,8 +733,10 @@
         ],
         axis=1,
     ).astype(jnp.bfloat16)
+    low_b = layer_norm(after_a, norm_gains[1], norm_shifts[1])[0].astype(jnp.bfloat16)
     grad_w_values = weight_grad(low_b, grad_v_low)
     grad_w_states = weight_grad(low_b, grad_kq_low)
+    _, unit_b, inverse_b = layer_norm(after_a, norm_gains[1], norm_shifts[1])
     grad_in_b, gain_b, shift_b = norm_grad(
         input_grad(grad_v_low, w_values) + input_grad(grad_kq_low, w_states),
         unit_b,
@@ -455,42 +744,11 @@
         norm_gains[1],
     )
     grad_a = grad_b + grad_in_b
-    grad_start, grad_up_a, grad_down_a, gain_a, shift_a = ffn_backward(
-        grad_a, kept_a, up_first, down_first, norm_gains[0]
-    )
-    blocks_ff = FF // D
+    grad_start, tile_grads_a, vec_a = ffn_back(
+        inputs[0], grad_a, gathered, vector_master, own_rows
+    )
+    gain_a, shift_a = vec_a[0], vec_a[1]
     count = lax.axis_size("tm")
-
-    def reduce_tiles(parts):
-        stacked = jnp.concatenate(parts, axis=0).astype(jnp.bfloat16)
-        stacked = stacked.reshape(stacked.shape[0], count, own_rows, D).transpose(1, 0, 2, 3)
-        return halving_sum(stacked, "tm")
-
-    middle = reduce_tiles([jnp.stack([grad_w_output, grad_w_linear, grad_w_gate])])
-    late = reduce_tiles(
-        [
-            grad_project[None],
-            column_tiles(grad_up_e),
-            grad_down_e.reshape(blocks_ff, D, D),
-        ]
-    )
-    early = reduce_tiles(
-        [
-            column_tiles(grad_up_a),
-            grad_down_a.reshape(blocks_ff, D, D),
-            jnp.stack([grad_w_values, grad_w_states]),
-        ]
-    )
-    shards = jnp.concatenate([early, middle, late, jnp.zeros((1, own_rows, D), jnp.bfloat16)], axis=0)
-    tiles = tile_slots.shape[0]
-    tile_of = (
-        jnp.full((owners_count * capacity,), tiles, jnp.int32)
-        .at[tile_slots]
-        .set(jnp.arange(tiles, dtype=jnp.int32))
-    )
-    placed = shards[tile_of].reshape(owners_count, capacity, own_rows, D)
-    reduced = lax.psum_scatter(placed, "utt", scatter_dimension=0)
-    reduced = reduced.astype(jnp.float32).transpose(1, 0, 2)
     vector_grad = jnp.concatenate(
         [
             jnp.stack(
@@ -513,7 +771,46 @@
         ],
         axis=0,
     )
-    vector_total = lax.psum(vector_grad, ("utt", "tm"))
+    mixers = jnp.stack(
+        [grad_w_values, grad_w_states, grad_w_output, grad_w_linear, grad_w_gate, grad_project]
+    ).astype(jnp.bfloat16)
+    mixers = mixers.reshape(6, count, own_rows, D).transpose(1, 0, 2, 3)
+    tail = jnp.zeros((VEC_ROWS - vector_grad.shape[0], D), jnp.float32)
+    vectors = jnp.concatenate([vector_grad, tail], axis=0).astype(jnp.bfloat16)
+    shards_e = halving_sum(tile_grads_e.reshape(count, 8 * own_rows, D), "tm")
+    shards_m = halving_sum(mixers.reshape(count, 6 * own_rows, D), "tm")
+    shards_a = halving_sum(
+        jnp.concatenate(
+            [
+                tile_grads_a.reshape(count, 8 * own_rows, D),
+                jnp.broadcast_to(vectors[None], (count, VEC_ROWS, D)),
+            ],
+            axis=1,
+        ),
+        "tm",
+    )
+    shards = jnp.concatenate(
+        [
+            shards_a[: 8 * own_rows].reshape(8, own_rows, D),
+            shards_m.reshape(6, own_rows, D),
+            shards_e.reshape(8, own_rows, D),
+            jnp.zeros((1, own_rows, D), jnp.bfloat16),
+        ],
+        axis=0,
+    )
+    tiles = tile_slots.shape[0]
+    tile_of = (
+        jnp.full((owners_count * capacity,), tiles, jnp.int32)
+        .at[tile_slots]
+        .set(jnp.arange(tiles, dtype=jnp.int32))
+    )
+    placed = shards[tile_of].reshape(owners_count, capacity * own_rows, D)
+    shared = jnp.broadcast_to(shards_a[None, 8 * own_rows :], (owners_count, VEC_ROWS, D))
+    reduced = lax.psum_scatter(
+        jnp.concatenate([placed, shared], axis=1), "utt", scatter_dimension=0
+    ).astype(jnp.float32)
+    vector_total = reduced[capacity * own_rows :][: vector_grad.shape[0]]
+    reduced = reduced[: capacity * own_rows].reshape(capacity, own_rows, D).transpose(1, 0, 2)
     tile_new, first_new, second_new = adam_step(
         master_weight_tiles, tile_first, tile_second, reduced, RATE_TILES, DECAY_TILES
     )

time: 570 us -> 529 us (0.928)
  Pallas kernels: 0 us -> 151 us
  matrix products: 122 us -> 64 us
  blocking collectives: 77.7 us -> 21.5 us
  waiting for transfers between devices: 124 us -> 78.4 us
  local copies, waits for them, and re-layouts: 112 us -> 75.2 us
    pallas_call x0 -> x4, Pallas kernels: none -> 151 us  [the longest x1 93.4 us: gather_tiles(): pl.pallas_call(functools.partial(gather_kernel, owners, count), out_shape...]
    all_gather x3 -> x0, waiting for transfers between devices: 78.4 us -> none  [the longest x1 48.1 us: local(): by_slot = lax.all_gather(low_master, 'utt', axis=0, tiled=True)]
    reduce_scatter x1, waiting for transfers between devices: 0.01 us -> 43.7 us  [local(): lax.psum_scatter(jnp.concatenate([placed, shared], axis=1), 'utt', scatte...]
    psum x1 -> x0, blocking collectives: 39.9 us -> none  [local(): vector_total = lax.psum(vector_grad, ('utt', 'tm'))]
    unnamed x510 -> x304, local copies, waits for them, and re-layouts: 43.8 us -> 18.3 us
    dot_general x10 -> x6, matrix products: 35 us -> 10.5 us  [input_grad(): lax.dot_general(gradients, weights, (((1,), (1,)), ((), ())), preferred_e...]
    dot_general x10 -> x4, matrix products: 22.1 us -> 4.83 us  [product(): return jnp.dot(matrix_a, matrix_b, preferred_element_type=jnp.float32)]
    dot_general x10 -> x6, matrix products: 25 us -> 10.2 us  [weight_grad(): lax.dot_general(activations, gradients, (((0,), (0,)), ((), ())), preferr...]
  transfers between devices with their start and end apart: 23 -> 20, of which waited for: 10 -> 8; matrix products, arithmetic and copies ran while one was open for 35% -> 7% of each run, Pallas kernels for 0% -> 4%
where the time goes in v2:
time: 529 us; the launch traced here: 522 us
  Pallas kernels  151 us (29%)
  other arithmetic  92.4 us (17%)
  waiting for transfers between devices  78.4 us (15%)
  local copies, waits for them, and re-layouts  75.2 us (14%)
  matrix products  64 us (12%)
  starting transfers between devices  21.8 us (4%)
  blocking collectives  21.5 us (4%)
  between operations  18.1 us (3%)
    pallas_call x1, Pallas kernels, gather_tiles(): pl.pallas_call(functools.partial(gather_kernel, owners, count), out_shape...  93.4 us
    pallas_call x2, Pallas kernels, ffn_back_call(): pl.pallas_call(functools.partial(back_kernel, steps, last, 4 if last else...  44.4 us
    reduce_scatter x1, waiting for transfers between devices, local(): lax.psum_scatter(jnp.concatenate([placed, shared], axis=1), 'utt', scatte...  43.7 us
    ppermute x15, waiting for transfers between devices, exchange_bit(): got = lax.ppermute(sent, axis, [(i, i ^ 1 << bit) for i in range(count)])  34.6 us
    reduce_sum x2, other arithmetic, layer_norm(): centered = values - jnp.mean(values, axis=-1, keepdims=True)  22.5 us
    all_gather x2, blocking collectives, entry_of(): arrived = lax.all_gather(sent, 'tm')  21.5 us
    unnamed x304, local copies, waits for them, and re-layouts  18.3 us
    reduce_sum x3, other arithmetic, local(): jnp.sum(grad_conv_wide * padded[kernel_offset:kernel_offset + frames].ast...  15.5 us
  transfers between devices with their start and end apart: 20, of which 8 were waited for; matrix products, arithmetic and copies ran while one was open for 7% of the time, Pallas kernels for 4%

profile of v2, /device:TPU:0, one launch (start us, length us, event | category | flops | bytes accessed | tf_op | source)
XLA Modules:
  0.0 521.8 jit_solution(12378857311257553153)
XLA Ops:
  12.5 93.4 %shard_map.187.ffn_ref.mix_ref = bf16[8,24,64,512]{3,2,1,0:T(8,128)(2,1)S(1)} custom-call(s32[22]{0:T(128)S(1)} %copy-done.4, bf16[8,64,512]{2,1,0:T(8,128)(2,1)S(1)} %bitcast.338), custom_call_target="tpu_custom_call" | custom-call | tf_op jit(solution)/shard_map/pallas_call | solution.py:299
  105.9 4.5 copy-done
  110.4 12.7 %shard_map.188 = (f32[1024,512]{1,0:T(8,128)S(1)}, bf16[1024,512]{1,0:T(8,128)(2,1)S(1)}, bf16[1024,512]{1,0:T(8,128)(2,1)S(1)}) custom-call(bf16[1024,512]{1,0:T(8,128)(2,1)S(1)} %bitcast.336, bf16[8,24,64,512]{3,2,1,0:T(8,128)(2,1)} %copy-done, bf16[8,24,64,512]{3,2,1,0:T(8,128)(2,1)} %copy-done, f32[27,512]{1,0:T(8,128)S(1)} %copy-done.2), custom_call_target="tpu_custom_call" | custom-call | tf_op jit(solution)/shard_map/pallas_call | solution.py:379
  126.9 2.3 copy.223
  129.1 2.2 fusion.214
  131.4 3.5 fusion.204
  139.0 2.3 reduce-window.25
  141.8 2.5 copy.220
  145.0 2.5 convolution_convert_fusion.8
  147.6 10.5 %all-gather = bf16[64,33,64]{2,0,1:T(8,128)(2,1)S(1)} all-gather(bf16[8,33,64]{2,0,1:T(8,128)(2,1)S(1)} %copy.224), channel_id=2, replica_groups=mesh['utt'=4,'tm'=8] {'tm'}, dimensions={0}, use_global_device_ids=true | all-gather | bytes 304128 | tf_op jit(solution)/shard_map/all_gather | solution.py:125
  159.2 1.8 broadcast_compare_fusion.2
  164.5 1.8 copy.218
  166.3 1.8 copy.219
  168.1 2.1 copy.217
  170.2 2.9 fusion.209
  173.1 2.0 copy.225
  175.6 2.0 copy.230
  178.5 1.8 copy.228
  182.1 2.0 copy.227
  184.2 2.0 copy.232
  186.2 3.9 multiply_convert_fusion.3
  192.2 3.0 multiply_convert_fusion.2
  203.6 2.1 multiply_convert_fusion.8
  207.2 2.9 collective-permute-start
  218.0 2.5 copy.234
  221.8 2.1 copy.235
  223.9 22.3 %fusion.202 = (f32[1024]{0:T(1024)S(1)}, f32[1024,512]{1,0:T(8,128)S(1)}) fusion(f32[1024]{0:T(1024)} %get-tuple-element.172, bf16[7,512]{1,0:T(8,128)(2,1)} %collective-permute-done.1, bf16[1024,512]{1,0:T(8,128)(2,1)} %copy-done.8, f32[512]{0:T(512)} %bitcast.435, f32[1024]{0:T(1024)} %get-tuple-element.171, f32[512]{0:T(512)} %bitcast.437, ...), kind=kLoop, calls=%fused_computation.465 | loop fusion | flops 53476352 | bytes 3256320 | tf_op jit(solution)/shard_map/reduce_sum | solution.py:64
  247.8 24.6 %shard_map.189 = (bf16[1024,512]{1,0:T(8,128)(2,1)}, f32[1024,512]{1,0:T(8,128)S(1)}, bf16[8,8,64,512]{3,2,1,0:T(8,128)(2,1)}, f32[8,512]{1,0:T(8,128)S(1)}) custom-call(f32[1024,512]{1,0:T(8,128)S(1)} %convolution_add_fusion.2.x_ref, bf16[1024,512]{1,0:T(8,128)(2,1)S(1)} %bitcast.339, bf16[8,24,64,512]{3,2,1,0:T(8,128)(2,1)} %copy-done, f32[27,512]{1,0:T(8,128)S(1)} %copy-done.2), custom_call_target="tpu_custom_call" | custom-call | tf_op jit(solution)/shard_map/pallas_call | solution.py:478
  272.5 2.3 multiply_reduce_fusion
  274.9 8.3 %fusion.76 = (bf16[512]{0:T(512)(128)(2,1)}, bf16[512]{0:T(512)(128)(2,1)}, bf16[512]{0:T(512)(128)(2,1)}, bf16[512]{0:T(512)(128)(2,1)}, bf16[512]{0:T(512)(128...) fusion(bf16[7,512]{1,0:T(8,128)(2,1)} %collective-permute-done.1, bf16[1024,512]{1,0:T(8,128)(2,1)S(1)} %copy-done.9, ...), kind=kLoop, calls=%fused_computation.147 | loop fusion | flops 26735616 | bytes 6347776 | tf_op jit(solution)/shard_map/reduce_sum | solution.py:652
  284.5 3.7 collective-permute-start.3
  288.2 4.6 fusion.60
  293.0 2.1 convolution_convert_fusion.1
  295.3 7.5 %multiply_convert_fusion.5 = (bf16[1024,512]{1,0:T(8,128)(2,1)S(1)}, f32[1024,512]{1,0:T(8,128)S(1)}) fusion(f32[1024,512]{1,0:T(8,128)S(1)} %copy-done.14, f32[1024]{0:T(1024)S(1)} %copy-done.99, bf16[1024,512]{1,0:T(8,128)(2,1)S(1)} %get-tuple-element.65, bf16[7,512]{1,0:T(8,128)(2,1)S(1)} %collective-permute-done.3, f32[512]{0:T(512)S(1)} %bitcast.436, ...), kind=kLoop, calls=%fused_computation.161 | loop fusion | flops 54001664 | bytes 6397952 | tf_op jit(solution)/shard_map/convert_element_type | solution.py:659
  304.9 1.9 multiply_reduce_fusion.1
  309.5 2.8 multiply_convert_fusion.1
  312.7 3.0 multiply_convert_fusion
  318.3 1.8 fusion.226
  324.2 11.0 %all-gather.1 = bf16[64,32,64]{2,1,0:T(8,128)(2,1)S(1)} all-gather(bf16[8,32,64]{2,1,0:T(8,128)(2,1)S(1)} %convolution_convert_fusion.7), channel_id=3, replica_groups=mesh['utt'=4,'tm'=8] {'tm'}, dimensions={0}, use_global_device_ids=true | all-gather | bytes 294912 | tf_op jit(solution)/shard_map/all_gather | solution.py:125
  338.0 2.0 fusion.94
  341.5 2.0 fusion.93
  343.6 2.0 convolution_add_fusion.5
  345.6 2.5 copy.236
  348.1 3.4 convolution_add_fusion.4
  351.5 2.6 copy.237
  356.4 1.9 fusion.195
  358.3 3.1 multiply_reduce_fusion.2
  362.9 2.3 copy.240
  365.2 2.8 fusion.82
  373.3 2.5 fusion.74
  379.5 19.8 %shard_map.190 = (f32[1024,512]{1,0:T(8,128)}, bf16[8,8,64,512]{3,2,1,0:T(8,128)(2,1)}, f32[8,512]{1,0:T(8,128)S(1)}) custom-call(bf16[1024,512]{1,0:T(8,128)(2,1)S(1)} %bitcast.337, f32[1024,512]{1,0:T(8,128)S(1)} %multiply_add_fusion.grad_ref, bf16[8,24,64,512]{3,2,1,0:T(8,128)(2,1)} %copy-done, f32[27,512]{1,0:T(8,128)S(1)} %copy-done.2), custom_call_target="tpu_custom_call" | custom-call | tf_op jit(solution)/shard_map/pallas_call | solution.py:478
  399.5 2.3 fusion.78
  406.9 6.6 %collective-permute-done.10 = bf16[2,1,192,512]{3,2,0,1:T(8,128)(2,1)S(1)} collective-permute-done((bf16[2,1,192,512]{3,2,0,1:T(8,128)(2,1)S(1)}, bf16[2,1,192,512]{3,2,0,1:T(8,128)(2,1)S(1)}, u32[]{:S(2)}, u32[]{:S(2)}) %collective-permute-start.10) | collective-permute-done | bytes 393248 | tf_op jit(solution)/shard_map/ppermute | solution.py:168
  414.4 3.7 collective-permute-done.12
  419.0 2.8 fusion.37
  425.1 2.3 fusion.7
  429.9 7.0 %collective-permute-done.15 = bf16[2,1,256,512]{3,2,1,0:T(8,128)(2,1)S(1)} collective-permute-done((bf16[2,1,256,512]{3,2,1,0:T(8,128)(2,1)S(1)}, bf16[2,1,256,512]{3,2,1,0:T(8,128)(2,1)S(1)}, u32[]{:S(2)}, u32[]{:S(2)}) %collective-permute-start.15) | collective-permute-done | bytes 524320 | tf_op jit(solution)/shard_map/ppermute | solution.py:168
  439.4 9.4 %collective-permute-done.5 = bf16[2,1,272,512]{3,2,1,0:T(8,128)(2,1)S(1)} collective-permute-done((bf16[2,1,272,512]{3,2,1,0:T(8,128)(2,1)S(1)}, bf16[2,1,272,512]{3,2,1,0:T(8,128)(2,1)S(1)}, u32[]{:S(2)}, u32[]{:S(2)}) %collective-permute-start.5) | collective-permute-done | bytes 557088 | tf_op jit(solution)/shard_map/ppermute | solution.py:168
  451.4 4.5 collective-permute-done.16
  456.1 2.7 collective-permute-done.8
  459.2 2.0 gather_fusion
  461.2 3.1 pad_maximum_fusion
  464.3 43.7 %reduce-scatter.2.cloned.1.call-done = bf16[1,544,512]{2,1,0:T(8,128)(2,1)} async-done(((bf16[4,544,512]{2,1,0:T(8,128)(2,1)}), bf16[1,544,512]{2,1,0:T(8,128)(2,1)}) %reduce-scatter.2.cloned.1.call-update) | async-done | bytes 557072 | tf_op jit(solution)/shard_map/reduce_scatter | solution.py:809
  509.3 4.6 fusion.198
  (515 shorter events, 93.1 us)
Async XLA Ops:
  7.2 500.9 %reduce-scatter.2.cloned.1.call-start = ((), (), s32[]{:S(2)}) async-start(), calls=%async_computation.1 | async-start | bytes 2785280 | tf_op jit(solution)/shard_map/reduce_scatter | solution.py:809
  7.2 151.0 %copy-start.145 = (pred[8]{0:T(512)(128)(4,1)}, pred[8]{0:T(512)(128)(4,1)S(1)}, u32[]{:S(2)}) copy-start(pred[8]{0:T(512)(128)(4,1)S(1)} %iota_compare_fusion.3) | copy-start | bytes 28
  12.5 97.9 %copy-start.1 = (bf16[1,1024,512]{2,1,0:T(8,128)(2,1)S(1)}, bf16[1,1024,512]{2,1,0:T(8,128)(2,1)}, u32[]{:S(2)}) copy-start(bf16[1,1024,512]{2,1,0:T(8,128)(2,1)} %param.12) | copy-start | bytes 3145732
  12.5 97.9 %copy-start.2 = (f32[27,512]{1,0:T(8,128)S(1)}, f32[27,512]{1,0:T(8,128)}, u32[]{:S(2)}) copy-start(f32[27,512]{1,0:T(8,128)} %vec_ref.5) | copy-start | bytes 165892
  131.4 7.6 %copy-start.104 = (f32[1,8,1024]{2,1,0:T(8,128)S(1)}, f32[1,8,1024]{2,1,0:T(8,128)}, u32[]{:S(2)}) copy-start(f32[1,8,1024]{2,1,0:T(8,128)} %param.16) | copy-start | bytes 98308
  175.2 16.9 %copy-start.76 = (f32[8,512]{1,0:T(8,128)}, f32[8,512]{1,0:T(8,128)S(1)}, u32[]{:S(2)}) copy-start(f32[8,512]{1,0:T(8,128)S(1)} %get-tuple-element.188) | copy-start | bytes 49156
  175.2 36.2 %copy-start.73 = (f32[8,512]{1,0:T(8,128)}, f32[8,512]{1,0:T(8,128)S(1)}, u32[]{:S(2)}) copy-start(f32[8,512]{1,0:T(8,128)S(1)} %get-tuple-element.71) | copy-start | bytes 49156
  205.7 6.6 %copy-start.5 = (s32[22]{0:T(128)S(1)}, s32[22]{0:T(128)}, u32[]{:S(2)}) copy-start(s32[22]{0:T(128)} %slots_ref.1) | copy-start | bytes 268
  207.2 16.6 %collective-permute-start = (bf16[7,512]{1,0:T(8,128)(2,1)}, bf16[7,512]{1,0:T(8,128)(2,1)}, u32[]{:S(2)}, u32[]{:S(2)}) collective-permute-start(bf16[7,512]{1,0:T(8,128)(2,1)} %get-tuple-element.93), channel_id=1, source_target_pairs={{0,1},{1,2},{2,3},{3,4},{4,5},{5,6},{6,7},{8,9},{9,10},{10,11},{11... | collective-permute-start | bytes 21512 | tf_op jit(solution)/shard_map/ppermute | solution.py:38
  210.1 13.7 %collective-permute-start.1 = (bf16[7,512]{1,0:T(8,128)(2,1)}, bf16[7,512]{1,0:T(8,128)(2,1)}, u32[]{:S(2)}, u32[]{:S(2)}) collective-permute-start(bf16[7,512]{1,0:T(8,128)(2,1)} %get-tuple-element.94), channel_id=1, source_target_pairs={{1,0},{2,1},{3,2},{4,3},{5,4},{6,5},{7,6},{9,8},{10,9},{11,10},{12... | collective-permute-start | bytes 21512 | tf_op jit(solution)/shard_map/ppermute | solution.py:40
  223.8 22.7 %copy-start.7 = (f32[1024,512]{1,0:T(8,128)S(1)}, f32[1024,512]{1,0:T(8,128)}, u32[]{:S(2)}) copy-start(f32[1024,512]{1,0:T(8,128)} %copy-done.6) | copy-start | bytes 6291460
  223.8 22.7 %copy-start.62 = (bf16[8,1,64,512]{3,2,1,0:T(8,128)(2,1)S(1)}, bf16[8,1,64,512]{3,2,1,0:T(8,128)(2,1)}, u32[]{:S(2)}) copy-start(bf16[8,1,64,512]{3,2,1,0:T(8,128)(2,1)} %get-tuple-element.76) | copy-start | bytes 1572868
  223.8 22.7 %copy-start.125 = (f32[1,512]{1,0:T(1,128)S(1)}, f32[1,512]{1,0:T(1,128)}, u32[]{:S(2)}) copy-start(f32[1,512]{1,0:T(1,128)} %get-tuple-element.108) | copy-start | bytes 6148
  223.8 22.7 %copy-start.144 = (f32[1,512]{1,0:T(1,128)S(1)}, f32[1,512]{1,0:T(1,128)}, u32[]{:S(2)}) copy-start(f32[1,512]{1,0:T(1,128)} %get-tuple-element.107) | copy-start | bytes 6148
  274.8 13.3 %copy-start.88 = (f32[1024]{0:T(1024)S(1)}, f32[1024]{0:T(1024)}, u32[]{:S(2)}) copy-start(f32[1024]{0:T(1024)} %get-tuple-element.159) | copy-start | bytes 12292
  274.8 13.3 %copy-start.89 = (f32[1024]{0:T(1024)S(1)}, f32[1024]{0:T(1024)}, u32[]{:S(2)}) copy-start(f32[1024]{0:T(1024)} %get-tuple-element.160) | copy-start | bytes 12292
  274.9 13.3 %copy-start.90 = (f32[1024]{0:T(1024)S(1)}, f32[1024]{0:T(1024)}, u32[]{:S(2)}) copy-start(f32[1024]{0:T(1024)} %get-tuple-element.162) | copy-start | bytes 12292
  274.9 13.3 %copy-start.91 = (f32[1024]{0:T(1024)S(1)}, f32[1024]{0:T(1024)}, u32[]{:S(2)}) copy-start(f32[1024]{0:T(1024)} %get-tuple-element.163) | copy-start | bytes 12292
  274.9 13.3 %copy-start.92 = (f32[1024]{0:T(1024)S(1)}, f32[1024]{0:T(1024)}, u32[]{:S(2)}) copy-start(f32[1024]{0:T(1024)} %get-tuple-element.164) | copy-start | bytes 12292
  274.9 13.3 %copy-start.99 = (f32[1024]{0:T(1024)S(1)}, f32[1024]{0:T(1024)}, u32[]{:S(2)}) copy-start(f32[1024]{0:T(1024)} %get-tuple-element.173) | copy-start | bytes 12292
  283.2 11.9 %copy-start.15 = (bf16[1024,512]{1,0:T(8,128)(2,1)}, bf16[1024,512]{1,0:T(8,128)(2,1)S(1)}, u32[]{:S(2)}) copy-start(bf16[1024,512]{1,0:T(8,128)(2,1)S(1)} %get-tuple-element.65) | copy-start | bytes 3145732
  283.2 11.9 %collective-permute-start.2 = (bf16[7,512]{1,0:T(8,128)(2,1)S(1)}, bf16[7,512]{1,0:T(8,128)(2,1)S(1)}, u32[]{:S(2)}, u32[]{:S(2)}) collective-permute-start(bf16[7,512]{1,0:T(8,128)(2,1)S(1)} %get-tuple-element.91), channel_id=1, source_target_pairs={{1,0},{2,1},{3,2},{4,3},{5,4},{6,5},{7,6},{9,8},{10,9},{11,10},{12... | collective-permute-start | bytes 21512 | tf_op jit(solution)/shard_map/ppermute | solution.py:40
  284.5 10.6 %collective-permute-start.3 = (bf16[7,512]{1,0:T(8,128)(2,1)S(1)}, bf16[7,512]{1,0:T(8,128)(2,1)S(1)}, u32[]{:S(2)}, u32[]{:S(2)}) collective-permute-start(bf16[7,512]{1,0:T(8,128)(2,1)S(1)} %get-tuple-element.92), channel_id=1, source_target_pairs={{0,1},{1,2},{2,3},{3,4},{4,5},{5,6},{6,7},{8,9},{9,10},{10,11},{11... | collective-permute-start | bytes 21512 | tf_op jit(solution)/shard_map/ppermute | solution.py:38
  295.1 7.7 %copy-start.24 = (f32[1024,512]{1,0:T(8,128)S(1)}, f32[1024,512]{1,0:T(8,128)}, u32[]{:S(2)}) copy-start(f32[1024,512]{1,0:T(8,128)} %get-tuple-element.183) | copy-start | bytes 6291460
  323.2 11.9 %copy-start.122 = (f32[8,8]{1,0:T(8,128)S(1)}, f32[8,8]{1,0:T(8,128)}, u32[]{:S(2)}) copy-start(f32[8,8]{1,0:T(8,128)} %broadcast_select_fusion) | copy-start | bytes 772
  323.2 12.2 %copy-start.30 = (f32[512,256]{0,1:T(8,128)S(1)}, f32[512,256]{0,1:T(8,128)}, u32[]{:S(2)}) copy-start(f32[512,256]{0,1:T(8,128)} %copy.232) | copy-start | bytes 1572868
  323.2 12.2 %copy-start.142 = (f32[8]{0:T(128)S(1)}, f32[8]{0:T(128)}, u32[]{:S(2)}) copy-start(f32[8]{0:T(128)} %slice_reduce_fusion.4) | copy-start | bytes 100
  351.5 4.8 copy-start.123
  369.5 6.7 %copy-start.38 = (bf16[8,8,64,512]{3,2,1,0:T(8,128)(2,1)S(1)}, bf16[8,8,64,512]{3,2,1,0:T(8,128)(2,1)}, u32[]{:S(2)}) copy-start(bf16[8,8,64,512]{3,2,1,0:T(8,128)(2,1)} %get-tuple-element.28) | copy-start | bytes 12582916
  369.9 6.0 %copy-start.23 = (bf16[8,6,64,512]{3,2,1,0:T(8,128)(2,1)}, bf16[8,6,64,512]{3,2,1,0:T(8,128)(2,1)S(1)}, u32[]{:S(2)}) copy-start(bf16[8,6,64,512]{3,2,1,0:T(8,128)(2,1)S(1)} %copy.241) | copy-start | bytes 9437188
  369.9 6.0 %copy-start.132 = (bf16[512]{0:T(512)(128)(2,1)S(1)}, bf16[512]{0:T(512)(128)(2,1)}, u32[]{:S(2)}) copy-start(bf16[512]{0:T(512)(128)(2,1)} %get-tuple-element.44) | copy-start | bytes 3076
  369.9 6.0 %copy-start.131 = (bf16[512]{0:T(512)(128)(2,1)S(1)}, bf16[512]{0:T(512)(128)(2,1)}, u32[]{:S(2)}) copy-start(bf16[512]{0:T(512)(128)(2,1)} %get-tuple-element.46) | copy-start | bytes 3076
  369.9 6.0 %copy-start.130 = (bf16[512]{0:T(512)(128)(2,1)S(1)}, bf16[512]{0:T(512)(128)(2,1)}, u32[]{:S(2)}) copy-start(bf16[512]{0:T(512)(128)(2,1)} %get-tuple-element.45) | copy-start | bytes 3076
  369.9 6.0 %copy-start.129 = (bf16[512]{0:T(512)(128)(2,1)S(1)}, bf16[512]{0:T(512)(128)(2,1)}, u32[]{:S(2)}) copy-start(bf16[512]{0:T(512)(128)(2,1)} %get-tuple-element.42) | copy-start | bytes 3076
  370.0 6.0 %copy-start.128 = (bf16[512]{0:T(512)(128)(2,1)S(1)}, bf16[512]{0:T(512)(128)(2,1)}, u32[]{:S(2)}) copy-start(bf16[512]{0:T(512)(128)(2,1)} %get-tuple-element.43) | copy-start | bytes 3076
  370.0 6.0 %copy-start.127 = (bf16[512]{0:T(512)(128)(2,1)S(1)}, bf16[512]{0:T(512)(128)(2,1)}, u32[]{:S(2)}) copy-start(bf16[512]{0:T(512)(128)(2,1)} %get-tuple-element.41) | copy-start | bytes 3076
  370.0 6.1 %copy-start.138 = (bf16[512]{0:T(512)(128)(2,1)S(1)}, bf16[512]{0:T(512)(128)(2,1)}, u32[]{:S(2)}) copy-start(bf16[512]{0:T(512)(128)(2,1)} %get-tuple-element.36) | copy-start | bytes 3076
  370.0 6.1 %copy-start.137 = (bf16[512]{0:T(512)(128)(2,1)S(1)}, bf16[512]{0:T(512)(128)(2,1)}, u32[]{:S(2)}) copy-start(bf16[512]{0:T(512)(128)(2,1)} %get-tuple-element.37) | copy-start | bytes 3076
  370.0 6.1 %copy-start.136 = (bf16[512]{0:T(512)(128)(2,1)S(1)}, bf16[512]{0:T(512)(128)(2,1)}, u32[]{:S(2)}) copy-start(bf16[512]{0:T(512)(128)(2,1)} %get-tuple-element.38) | copy-start | bytes 3076
  370.0 6.1 %copy-start.135 = (bf16[512]{0:T(512)(128)(2,1)S(1)}, bf16[512]{0:T(512)(128)(2,1)}, u32[]{:S(2)}) copy-start(bf16[512]{0:T(512)(128)(2,1)} %get-tuple-element.39) | copy-start | bytes 3076
  370.0 6.1 %copy-start.134 = (bf16[512]{0:T(512)(128)(2,1)S(1)}, bf16[512]{0:T(512)(128)(2,1)}, u32[]{:S(2)}) copy-start(bf16[512]{0:T(512)(128)(2,1)} %get-tuple-element.40) | copy-start | bytes 3076
  370.0 6.1 %copy-start.133 = (bf16[512]{0:T(512)(128)(2,1)S(1)}, bf16[512]{0:T(512)(128)(2,1)}, u32[]{:S(2)}) copy-start(bf16[512]{0:T(512)(128)(2,1)} %get-tuple-element.35) | copy-start | bytes 3076
  370.0 6.1 %copy-start.147 = (bf16[512]{0:T(512)(128)(2,1)S(1)}, bf16[512]{0:T(512)(128)(2,1)}, u32[]{:S(2)}) copy-start(bf16[512]{0:T(512)(128)(2,1)} %get-tuple-element.29) | copy-start | bytes 3076
  370.0 6.1 %copy-start.146 = (bf16[512]{0:T(512)(128)(2,1)S(1)}, bf16[512]{0:T(512)(128)(2,1)}, u32[]{:S(2)}) copy-start(bf16[512]{0:T(512)(128)(2,1)} %get-tuple-element.53) | copy-start | bytes 3076
  371.3 28.2 %collective-permute-start.9 = (bf16[4,1,384,512]{3,2,0,1:T(8,128)(2,1)}, bf16[4,1,384,512]{3,2,0,1:T(8,128)(2,1)}, u32[]{:S(2)}, u32[]{:S(2)}) collective-permute-start(bf16[4,1,384,512]{3,2,0,1:T(8,128)(2,1)} %dynamic-slice_bitcast_fusion.1), channel_id=1, source_target_pairs={{0,1},{1,0},{2,3},{3,2},{4,5},{5,4},{6,7},{7,6},{8,9},{9,8},{10,11... | collective-permute-start | bytes 4718600 | tf_op jit(solution)/shard_map/ppermute | solution.py:168
  377.7 41.3 %collective-permute-start.14 = (bf16[4,1,512,512]{3,2,0,1:T(8,128)(2,1)}, bf16[4,1,512,512]{3,2,0,1:T(8,128)(2,1)}, u32[]{:S(2)}, u32[]{:S(2)}) collective-permute-start(bf16[4,1,512,512]{3,2,0,1:T(8,128)(2,1)} %dynamic-slice_bitcast_fusion), channel_id=1, source_target_pairs={{0,1},{1,0},{2,3},{3,2},{4,5},{5,4},{6,7},{7,6},{8,9},{9,8},{10,11... | collective-permute-start | bytes 6291464 | tf_op jit(solution)/shard_map/ppermute | solution.py:168
  379.5 19.9 %copy-start.140 = (bf16[512]{0:T(512)(128)(2,1)S(1)}, bf16[512]{0:T(512)(128)(2,1)}, u32[]{:S(2)}) copy-start(bf16[512]{0:T(512)(128)(2,1)} %get-tuple-element.31) | copy-start | bytes 3076
  379.5 19.9 %copy-start.139 = (bf16[512]{0:T(512)(128)(2,1)S(1)}, bf16[512]{0:T(512)(128)(2,1)}, u32[]{:S(2)}) copy-start(bf16[512]{0:T(512)(128)(2,1)} %get-tuple-element.54) | copy-start | bytes 3076
  402.1 11.4 %collective-permute-start.10 = (bf16[2,1,192,512]{3,2,0,1:T(8,128)(2,1)S(1)}, bf16[2,1,192,512]{3,2,0,1:T(8,128)(2,1)S(1)}, u32[]{:S(2)}, u32[]{:S(2)}) collective-permute-start(bf16[2,1,192,512]{3,2,0,1:T(8,128)(2,1)S(1)} %dynamic-slice_bitcast_fusion.7), channel_id=1, source_target_pairs={{0,2},{1,3},{2,0},{3,1},{4,6},{5,7},{6,4},{7,5},{8,10},{9,11},{10,... | collective-permute-start | bytes 1179656 | tf_op jit(solution)/shard_map/ppermute | solution.py:168
  405.6 19.5 %collective-permute-start.4 = (bf16[4,1,544,512]{3,2,0,1:T(8,128)(2,1)}, bf16[4,1,544,512]{3,2,0,1:T(8,128)(2,1)}, u32[]{:S(2)}, u32[]{:S(2)}) collective-permute-start(bf16[4,1,544,512]{3,2,0,1:T(8,128)(2,1)} %fusion.4), channel_id=1, source_target_pairs={{0,1},{1,0},{2,3},{3,2},{4,5},{5,4},{6,7},{7,6},{8,9},{9,8},{10,11... | collective-permute-start | bytes 6684680 | tf_op jit(solution)/shard_map/ppermute | solution.py:168
  406.0 12.1 %collective-permute-start.12 = (bf16[1,2,192,512]{3,2,1,0:T(8,128)(2,1)S(1)}, bf16[1,2,192,512]{3,2,1,0:T(8,128)(2,1)S(1)}, u32[]{:S(2)}, u32[]{:S(2)}) collective-permute-start(bf16[1,2,192,512]{3,2,1,0:T(8,128)(2,1)S(1)} %dynamic-slice_bitcast_fusion.6), channel_id=1, source_target_pairs={{0,4},{1,5},{2,6},{3,7},{4,0},{5,1},{6,2},{7,3},{8,12},{9,13},{10,... | collective-permute-start | bytes 1179656 | tf_op jit(solution)/shard_map/ppermute | solution.py:168
  413.6 10.6 %collective-permute-start.11 = (bf16[1,1,192,512]{3,2,0,1:T(8,128)(2,1)S(1)}, bf16[1,1,192,512]{3,2,0,1:T(8,128)(2,1)S(1)}, u32[]{:S(2)}, u32[]{:S(2)}) collective-permute-start(bf16[1,1,192,512]{3,2,0,1:T(8,128)(2,1)S(1)} %constant_dynamic-slice_fusion.3), channel_id=1, source_target_pairs={{0,4},{1,5},{2,6},{3,7},{4,0},{5,1},{6,2},{7,3},{8,12},{9,13},{10,... | collective-permute-start | bytes 589832 | tf_op jit(solution)/shard_map/ppermute | solution.py:168
  418.2 6.8 %collective-permute-start.13 = (bf16[1,1,192,512]{3,2,1,0:T(8,128)(2,1)S(1)}, bf16[1,1,192,512]{3,2,1,0:T(8,128)(2,1)S(1)}, u32[]{:S(2)}, u32[]{:S(2)}) collective-permute-start(bf16[1,1,192,512]{3,2,1,0:T(8,128)(2,1)S(1)} %constant_dynamic-slice_fusion.2), channel_id=1, source_target_pairs={{0,2},{1,3},{2,0},{3,1},{4,6},{5,7},{6,4},{7,5},{8,10},{9,11},{10,... | collective-permute-start | bytes 589832 | tf_op jit(solution)/shard_map/ppermute | solution.py:168
  422.0 14.9 %collective-permute-start.15 = (bf16[2,1,256,512]{3,2,1,0:T(8,128)(2,1)S(1)}, bf16[2,1,256,512]{3,2,1,0:T(8,128)(2,1)S(1)}, u32[]{:S(2)}, u32[]{:S(2)}) collective-permute-start(bf16[2,1,256,512]{3,2,1,0:T(8,128)(2,1)S(1)} %dynamic-slice_bitcast_fusion.5), channel_id=1, source_target_pairs={{0,2},{1,3},{2,0},{3,1},{4,6},{5,7},{6,4},{7,5},{8,10},{9,11},{10,... | collective-permute-start | bytes 1572872 | tf_op jit(solution)/shard_map/ppermute | solution.py:168
  423.5 15.0 %collective-permute-start.17 = (bf16[1,2,256,512]{3,2,1,0:T(8,128)(2,1)S(1)}, bf16[1,2,256,512]{3,2,1,0:T(8,128)(2,1)S(1)}, u32[]{:S(2)}, u32[]{:S(2)}) collective-permute-start(bf16[1,2,256,512]{3,2,1,0:T(8,128)(2,1)S(1)} %dynamic-slice_bitcast_fusion.4), channel_id=1, source_target_pairs={{0,4},{1,5},{2,6},{3,7},{4,0},{5,1},{6,2},{7,3},{8,12},{9,13},{10,... | collective-permute-start | bytes 1572872 | tf_op jit(solution)/shard_map/ppermute | solution.py:168
  427.7 21.2 %collective-permute-start.5 = (bf16[2,1,272,512]{3,2,1,0:T(8,128)(2,1)S(1)}, bf16[2,1,272,512]{3,2,1,0:T(8,128)(2,1)S(1)}, u32[]{:S(2)}, u32[]{:S(2)}) collective-permute-start(bf16[2,1,272,512]{3,2,1,0:T(8,128)(2,1)S(1)} %dynamic-slice_bitcast_fusion.3), channel_id=1, source_target_pairs={{0,2},{1,3},{2,0},{3,1},{4,6},{5,7},{6,4},{7,5},{8,10},{9,11},{10,... | collective-permute-start | bytes 1671176 | tf_op jit(solution)/shard_map/ppermute | solution.py:168
  428.4 22.0 %collective-permute-start.7 = (bf16[1,2,272,512]{3,2,1,0:T(8,128)(2,1)S(1)}, bf16[1,2,272,512]{3,2,1,0:T(8,128)(2,1)S(1)}, u32[]{:S(2)}, u32[]{:S(2)}) collective-permute-start(bf16[1,2,272,512]{3,2,1,0:T(8,128)(2,1)S(1)} %dynamic-slice_bitcast_fusion.2), channel_id=1, source_target_pairs={{0,4},{1,5},{2,6},{3,7},{4,0},{5,1},{6,2},{7,3},{8,12},{9,13},{10,... | collective-permute-start | bytes 1671176 | tf_op jit(solution)/shard_map/ppermute | solution.py:168
  437.1 18.8 %collective-permute-start.16 = (bf16[1,1,256,512]{3,2,1,0:T(8,128)(2,1)S(1)}, bf16[1,1,256,512]{3,2,1,0:T(8,128)(2,1)S(1)}, u32[]{:S(2)}, u32[]{:S(2)}) collective-permute-start(bf16[1,1,256,512]{3,2,1,0:T(8,128)(2,1)S(1)} %constant_dynamic-slice_fusion.1), channel_id=1, source_target_pairs={{0,4},{1,5},{2,6},{3,7},{4,0},{5,1},{6,2},{7,3},{8,12},{9,13},{10,... | collective-permute-start | bytes 786440 | tf_op jit(solution)/shard_map/ppermute | solution.py:168
  438.7 17.3 %collective-permute-start.18 = (bf16[1,1,256,512]{3,2,1,0:T(8,128)(2,1)S(1)}, bf16[1,1,256,512]{3,2,1,0:T(8,128)(2,1)S(1)}, u32[]{:S(2)}, u32[]{:S(2)}) collective-permute-start(bf16[1,1,256,512]{3,2,1,0:T(8,128)(2,1)S(1)} %constant_dynamic-slice_fusion), channel_id=1, source_target_pairs={{0,2},{1,3},{2,0},{3,1},{4,6},{5,7},{6,4},{7,5},{8,10},{9,11},{10,... | collective-permute-start | bytes 786440 | tf_op jit(solution)/shard_map/ppermute | solution.py:168
  449.0 9.8 %collective-permute-start.6 = (bf16[1,1,272,512]{3,2,1,0:T(8,128)(2,1)S(1)}, bf16[1,1,272,512]{3,2,1,0:T(8,128)(2,1)S(1)}, u32[]{:S(2)}, u32[]{:S(2)}) collective-permute-start(bf16[1,1,272,512]{3,2,1,0:T(8,128)(2,1)S(1)} %constant_dynamic-slice_fusion.5), channel_id=1, source_target_pairs={{0,4},{1,5},{2,6},{3,7},{4,0},{5,1},{6,2},{7,3},{8,12},{9,13},{10,... | collective-permute-start | bytes 835592 | tf_op jit(solution)/shard_map/ppermute | solution.py:168
  450.6 8.1 %collective-permute-start.8 = (bf16[1,1,272,512]{3,2,1,0:T(8,128)(2,1)S(1)}, bf16[1,1,272,512]{3,2,1,0:T(8,128)(2,1)S(1)}, u32[]{:S(2)}, u32[]{:S(2)}) collective-permute-start(bf16[1,1,272,512]{3,2,1,0:T(8,128)(2,1)S(1)} %constant_dynamic-slice_fusion.4), channel_id=1, source_target_pairs={{0,2},{1,3},{2,0},{3,1},{4,6},{5,7},{6,4},{7,5},{8,10},{9,11},{10,... | collective-permute-start | bytes 835592 | tf_op jit(solution)/shard_map/ppermute | solution.py:168
  464.3 44.9 %copy-start.39 = (f32[64,8,512]{2,1,0:T(8,128)S(1)}, f32[64,8,512]{2,1,0:T(8,128)}, u32[]{:S(2)}) copy-start(f32[64,8,512]{2,1,0:T(8,128)} %param.18) | copy-start | bytes 3145732
  509.3 4.8 copy-start.80
  509.3 4.8 copy-start.81
  (105 other events, 222.9 us)
Sparse Core Ops, SparseCore 0:
  464.5 43.5 reduce-scatter.1

commit v3 on v2

--- a/solution.py
+++ b/solution.py
@@ -82,21 +82,6 @@
     return sigmoid_of * (1.0 + pre_act * (1.0 - sigmoid_of))
 
 
-def block_weights(log_piece, seg_piece, seg_prior):
-    cumulative = jnp.cumsum(log_piece, axis=1)
-    row_index = jnp.arange(seg_piece.shape[0], dtype=jnp.int32)
-    allowed = (seg_piece[:, None] == seg_piece[None, :]) & (
-        row_index[:, None] >= row_index[None, :]
-    )
-    exponent = jnp.where(allowed[None], cumulative[:, :, None] - cumulative[:, None, :], 0.0)
-    within = jnp.where(allowed[None], jnp.exp(exponent), 0.0)
-    entering = jnp.where((seg_piece == seg_prior)[None, :], jnp.exp(cumulative), 0.0)
-    leaving = jnp.where(
-        (seg_piece == seg_piece[-1])[None, :], jnp.exp(cumulative[:, -1:] - cumulative), 0.0
-    )
-    return (within, entering, leaving)
-
-
 def adam_step(master, first_old, second, gradient, step_rate, decay_rate):
     first_new = BETA_ONE * first_old + (1.0 - BETA_ONE) * gradient
     second_new = BETA_TWO * second + (1.0 - BETA_TWO) * gradient * gradient
@@ -112,32 +97,6 @@
 ROW_STEP = 256
 ORDER = tuple(range(8)) + tuple(range(14, 22)) + tuple(range(8, 14))
 MESH = pl.DeviceIdType.MESH
-
-
-def entry_of(local_state, carry, scales):
-    count = lax.axis_size("tm")
-    place = lax.axis_index("tm")
-    backward = scales is not None
-    sent = local_state.astype(jnp.bfloat16)
-    if not backward:
-        row = jnp.broadcast_to(carry[:, None, None], (H, 1, P_SIZE)).astype(jnp.bfloat16)
-        sent = jnp.concatenate([sent, row], axis=1)
-    arrived = lax.all_gather(sent, "tm")
-    if not backward:
-        scales = arrived[:, :, NS, 0].astype(jnp.float32)
-        arrived = arrived[:, :, :NS]
-    source = jnp.arange(count)[:, None]
-    between = jnp.arange(count)[None, :]
-    if backward:
-        passed = (between < source) & (between > place)
-        ahead = source > place
-    else:
-        passed = (between > source) & (between < place)
-        ahead = source < place
-    weights = jnp.prod(jnp.where(passed[:, :, None], scales[None], 1.0), axis=1)
-    weights = jnp.where(ahead, weights, 0.0)
-    state = jnp.sum(weights[:, :, None, None] * arrived.astype(jnp.float32), axis=0)
-    return state, scales
 
 
 def halving_sum(cells, axis):
@@ -504,6 +463,305 @@
     return ffn_back_call(values, grad, gathered, vectors, own_rows, False)
 
 
+def scan_lanes(values):
+    lane = lax.broadcasted_iota(jnp.int32, values.shape, 1)
+    shift = 1
+    while shift < values.shape[1]:
+        values = values + jnp.where(lane >= shift, pltpu.roll(values, shift, 1), 0.0)
+        shift *= 2
+    return values
+
+
+def segment_in(starts_ref, positions):
+    found = jnp.full_like(positions, -1)
+    for number in range(starts_ref.shape[0] - 1):
+        found = found + (starts_ref[number] <= positions).astype(jnp.int32)
+    return found
+
+
+def segment_at(starts_ref, position):
+    found = jnp.int32(-1)
+    for number in range(starts_ref.shape[0] - 1):
+        found = found + jnp.where(starts_ref[number] <= position, 1, 0)
+    return found
+
+
+def block_parts(starts_ref, decay_ref, block):
+    base = starts_ref[starts_ref.shape[0] - 1] + block * BLK
+    cumulative = scan_lanes(jnp.log(decay_ref[...]))
+    row = segment_in(starts_ref, base + lax.broadcasted_iota(jnp.int32, (1, BLK), 1))
+    prior = segment_at(starts_ref, base - 1)
+    final = segment_at(starts_ref, base + BLK - 1)
+    entering = jnp.where(row == prior, jnp.exp(cumulative), 0.0)
+    leaving = jnp.where(row == final, jnp.exp(cumulative[:, BLK - 1 :] - cumulative), 0.0)
+    return base, cumulative, row, entering, leaving
+
+
+def per_lane(values, width):
+    shape = (H, H * width)
+    chosen = lax.broadcasted_iota(jnp.int32, shape, 0) == (
+        lax.broadcasted_iota(jnp.int32, shape, 1) // width
+    )
+    return weight_grad(values.astype(jnp.bfloat16), chosen.astype(jnp.bfloat16))
+
+
+def own_heads(values):
+    shape = (H * NS, H * P_SIZE)
+    same = (lax.broadcasted_iota(jnp.int32, shape, 0) // NS) == (
+        lax.broadcasted_iota(jnp.int32, shape, 1) // P_SIZE
+    )
+    return jnp.where(same, values, 0.0)
+
+
+def pack_state(state):
+    folded = state[:, 0:128] + state[:, 128:256] + state[:, 256:384] + state[:, 384:512]
+    folded = folded + pltpu.roll(folded, 64, 1)
+    lane = lax.broadcasted_iota(jnp.int32, (128, 128), 1)
+    return jnp.where(lane < 64, folded[0:128], folded[128:256])
+
+
+def unpack_state(packed):
+    turned = pltpu.roll(packed, 64, 1)
+    lane = lax.broadcasted_iota(jnp.int32, (128, 128), 1)
+    both = jnp.concatenate(
+        [jnp.where(lane < 64, packed, turned), jnp.where(lane < 64, turned, packed)], axis=0
+    )
+    return own_heads(jnp.concatenate([both] * 4, axis=1))
+
+
+def lanes_of(values, head, width):
+    first = head * width // 128 * 128
+    whole = values[:, first : first + 128]
+    lane = lax.broadcasted_iota(jnp.int32, whole.shape, 1) + first
+    return whole, jnp.where(lane // width == head, whole, jnp.zeros_like(whole))
+
+
+def fill_bias(starts_ref, bias_s, base, row):
+    column = segment_in(starts_ref, base + lax.broadcasted_iota(jnp.int32, (BLK, 1), 0))
+    shape = (BLK, BLK)
+    later = lax.broadcasted_iota(jnp.int32, shape, 0) >= lax.broadcasted_iota(jnp.int32, shape, 1)
+    bias_s[...] = jnp.where((column == row) & later, 0.0, -1e30)
+
+
+def advance(keys, values, weights, state):
+    spread = per_lane(weights[0], P_SIZE)
+    added = weight_grad(keys, (values.astype(jnp.float32) * spread).astype(jnp.bfloat16))
+    return own_heads(added) + weights[1] * state
+
+
+def summary_kernel(backward, starts_ref, decay_ref, kq_ref, vals_ref, out_ref, state_s, carry_s):
+    step = pl.program_id(0)
+    blocks = pl.num_programs(0)
+
+    @pl.when(step == 0)
+    def _():
+        state_s[...] = jnp.zeros_like(state_s)
+        carry_s[...] = jnp.ones_like(carry_s)
+
+    block = blocks - 1 - step if backward else step
+    _, _, _, entering, leaving = block_parts(starts_ref, decay_ref, block)
+    spread_last = per_lane(entering, P_SIZE)[BLK - 1 :]
+    if backward:
+        keys, weights = kq_ref[:, H * NS :], entering
+    else:
+        keys, weights = kq_ref[:, : H * NS], leaving
+    state_s[...] = advance(keys, vals_ref[...], (weights, spread_last), state_s[...])
+    carry_s[...] = carry_s[...] * entering[:, BLK - 1 :]
+
+    @pl.when(step == blocks - 1)
+    def _():
+        rest = jnp.concatenate([carry_s[...], jnp.zeros_like(carry_s)], axis=0)
+        out_ref[...] = jnp.concatenate([pack_state(state_s[...]), rest], axis=0).astype(
+            jnp.bfloat16
+        )
+
+
+def mixing_kernel(starts_ref, decay_ref, kq_ref, vals_ref, entry_ref, y_ref, saved_ref, state_s, bias_s):
+    step = pl.program_id(0)
+
+    @pl.when(step == 0)
+    def _():
+        state_s[...] = unpack_state(entry_ref[...])
+
+    base, cumulative, row, entering, leaving = block_parts(starts_ref, decay_ref, step)
+    fill_bias(starts_ref, bias_s, base, row)
+    columns = cumulative.T
+    keys, queries, values = kq_ref[:, : H * NS], kq_ref[:, H * NS :], vals_ref[...]
+    spread = per_lane(entering, P_SIZE)
+    low_state = state_s[...].astype(jnp.bfloat16)
+    saved_ref[0] = low_state
+    carried = product(queries, low_state) * spread
+    half = BLK // 2
+    for pair in range(H // 2):
+        sums = [carried[:half, pair * 128 : pair * 128 + 128], carried[half:, pair * 128 : pair * 128 + 128]]
+        for head in (2 * pair, 2 * pair + 1):
+            _, query = lanes_of(queries, head, NS)
+            key, _ = lanes_of(keys, head, NS)
+            _, value = lanes_of(values, head, P_SIZE)
+            for part in range(2):
+                rows = slice(part * half, part * half + half)
+                seen = (part + 1) * half
+                scores = input_grad(query[rows], key[:seen])
+                within = jnp.exp(
+                    columns[rows, head : head + 1]
+                    - cumulative[head : head + 1, :seen]
+                    + bias_s[rows, :seen]
+                )
+                mixed = (within * scores).astype(jnp.bfloat16)
+                sums[part] = sums[part] + product(mixed, value[:seen])
+        for part in range(2):
+            y_ref[part * half : part * half + half, pair * 128 : pair * 128 + 128] = sums[
+                part
+            ].astype(jnp.bfloat16)
+    state_s[...] = advance(keys, values, (leaving, spread[BLK - 1 :]), state_s[...])
+
+
+def unmixing_kernel(
+    starts_ref, decay_ref, kq_ref, vals_ref, dy_ref, saved_ref, exit_ref, dv_ref, dkq_ref,
+    state_s, bias_s, dk_s, dv_s,
+):
+    step = pl.program_id(0)
+    block = pl.num_programs(0) - 1 - step
+
+    @pl.when(step == 0)
+    def _():
+        state_s[...] = unpack_state(exit_ref[...])
+
+    base, cumulative, row, entering, leaving = block_parts(starts_ref, decay_ref, block)
+    fill_bias(starts_ref, bias_s, base, row)
+    columns = cumulative.T
+    keys, queries, values = kq_ref[:, : H * NS], kq_ref[:, H * NS :], vals_ref[...]
+    grads = dy_ref[...]
+    low_state = state_s[...].astype(jnp.bfloat16)
+    dv_s[...] = product(keys, low_state) * per_lane(leaving, P_SIZE)
+    dk_s[...] = input_grad(values, low_state) * per_lane(leaving, NS)
+    dq = input_grad(grads, saved_ref[0]) * per_lane(entering, NS)
+    half = BLK // 2
+    for quad in range(H // 4):
+        lanes = slice(quad * 128, quad * 128 + 128)
+        sums = [dq[:half, lanes], dq[half:, lanes]]
+        for head in range(4 * quad, 4 * quad + 4):
+            _, query = lanes_of(queries, head, NS)
+            key, own_key = lanes_of(keys, head, NS)
+            value, _ = lanes_of(values, head, P_SIZE)
+            _, grad = lanes_of(grads, head, P_SIZE)
+            wide = slice(head // 2 * 128, head // 2 * 128 + 128)
+            for part in range(2):
+                rows = slice(part * half, part * half + half)
+                seen = (part + 1) * half
+                within = jnp.exp(
+                    columns[rows, head : head + 1]
+                    - cumulative[head : head + 1, :seen]
+                    + bias_s[rows, :seen]
+                )
+                mixed = (within * input_grad(query[rows], key[:seen])).astype(jnp.bfloat16)
+                dscores = (within * input_grad(grad[rows], value[:seen])).astype(jnp.bfloat16)
+                sums[part] = sums[part] + product(dscores, own_key[:seen])
+                dk_s[:seen, lanes] += weight_grad(dscores, query[rows])
+                dv_s[:seen, wide] += weight_grad(mixed, grad[rows])
+        for part in range(2):
+            dkq_ref[part * half : part * half + half, H * NS + quad * 128 : H * NS + quad * 128 + 128] = (
+                sums[part].astype(jnp.bfloat16)
+            )
+    dkq_ref[:, : H * NS] = dk_s[...].astype(jnp.bfloat16)
+    dv_ref[...] = dv_s[...].astype(jnp.bfloat16)
+    spread_last = per_lane(entering, P_SIZE)[BLK - 1 :]
+    state_s[...] = advance(queries, grads, (entering, spread_last), state_s[...])
+
+
+def block_specs(blocks, backward):
+    def turn(i):
+        return blocks - 1 - i if backward else i
+
+    return (
+        pl.BlockSpec(memory_space=pltpu.SMEM),
+        pl.BlockSpec((H, BLK), lambda i: (0, turn(i))),
+        pl.BlockSpec((BLK, D), lambda i: (turn(i), 0)),
+        pl.BlockSpec((1, H * NS, H * P_SIZE), lambda i: (turn(i), 0, 0)),
+    )
+
+
+STATE = (H * NS, H * P_SIZE)
+BIG = pltpu.CompilerParams(vmem_limit_bytes=48 << 20)
+
+
+def state_summary(places, decays, key_query, values, backward):
+    blocks = key_query.shape[0] // BLK
+    scalars, heads, rows, _ = block_specs(blocks, backward)
+    return pl.pallas_call(
+        functools.partial(summary_kernel, backward),
+        grid=(blocks,),
+        out_shape=jax.ShapeDtypeStruct((144, 128), jnp.bfloat16),
+        in_specs=[scalars, heads, rows, rows],
+        out_specs=pl.BlockSpec((144, 128), lambda i: (0, 0)),
+        scratch_shapes=[pltpu.VMEM(STATE, jnp.float32), pltpu.VMEM((H, 128), jnp.float32)],
+        compiler_params=BIG,
+    )(places, decays, key_query, values)
+
+
+def mix_states(places, decays, key_query, values, entry):
+    frames = key_query.shape[0]
+    blocks = frames // BLK
+    scalars, heads, rows, states = block_specs(blocks, False)
+    return pl.pallas_call(
+        mixing_kernel,
+        grid=(blocks,),
+        out_shape=(
+            jax.ShapeDtypeStruct((frames, D), jnp.bfloat16),
+            jax.ShapeDtypeStruct((blocks, *STATE), jnp.bfloat16),
+        ),
+        in_specs=[scalars, heads, rows, rows, pl.BlockSpec((128, 128), lambda i: (0, 0))],
+        out_specs=(rows, states),
+        scratch_shapes=[pltpu.VMEM(STATE, jnp.float32), pltpu.VMEM((BLK, BLK), jnp.float32)],
+        compiler_params=BIG,
+    )(places, decays, key_query, values, entry)
+
+
+def unmix_states(places, decays, key_query, values, grad_y, saved, leaving_grad):
+    frames = key_query.shape[0]
+    blocks = frames // BLK
+    scalars, heads, rows, states = block_specs(blocks, True)
+    return pl.pallas_call(
+        unmixing_kernel,
+        grid=(blocks,),
+        out_shape=(
+            jax.ShapeDtypeStruct((frames, D), jnp.bfloat16),
+            jax.ShapeDtypeStruct((frames, D), jnp.bfloat16),
+        ),
+        in_specs=[scalars, heads, rows, rows, rows, states, pl.BlockSpec((128, 128), lambda i: (0, 0))],
+        out_specs=(rows, rows),
+        scratch_shapes=[
+            pltpu.VMEM(STATE, jnp.float32),
+            pltpu.VMEM((BLK, BLK), jnp.float32),
+            pltpu.VMEM((BLK, H * NS), jnp.float32),
+            pltpu.VMEM((BLK, D), jnp.float32),
+        ],
+        compiler_params=BIG,
+    )(places, decays, key_query, values, grad_y, saved, leaving_grad)
+
+
+def entry_of(summary, scales):
+    count = lax.axis_size("tm")
+    place = lax.axis_index("tm")
+    backward = scales is not None
+    arrived = lax.all_gather(summary, "tm")
+    if not backward:
+        scales = arrived[:, 128 : 128 + H, 0].astype(jnp.float32)
+    source = jnp.arange(count)[:, None]
+    between = jnp.arange(count)[None, :]
+    if backward:
+        passed = (between < source) & (between > place)
+        ahead = source > place
+    else:
+        passed = (between > source) & (between < place)
+        ahead = source < place
+    weights = jnp.prod(jnp.where(passed[:, :, None], scales[None], 1.0), axis=1)
+    weights = jnp.where(ahead, weights, 0.0).reshape(count, 2, H // 2)
+    weights = jnp.repeat(weights.transpose(0, 2, 1), NS, axis=1)
+    weights = jnp.repeat(weights, P_SIZE, axis=2)
+    return jnp.sum(weights * arrived[:, :128].astype(jnp.float32), axis=0), scales
+
+
 def local(
     inputs,
     cotangent,
@@ -537,67 +795,13 @@
 
     positions = first_frame + jnp.arange(frames, dtype=jnp.int32)
     segments = segment_of(positions)
-    seg_before = segment_of(jnp.reshape(first_frame - 1, (1,)))[0]
-    log_decay = jnp.log(decays[0])
     after_a, raw_vals, key_query = ffn_first(inputs[0], gathered, vector_master)
     live_mask = frame_mask[0].astype(jnp.bfloat16)[:, None]
-    state_vals = (raw_vals * live_mask).reshape(frames, H, P_SIZE)
-    state_keys = key_query[:, : H * NS].reshape(frames, H, NS)
-    state_query = key_query[:, H * NS :].reshape(frames, H, NS)
-    keys_wide = state_keys.astype(jnp.float32)
-    query_wide = state_query.astype(jnp.float32)
-    vals_wide = state_vals.astype(jnp.float32)
-    total_log = jnp.cumsum(log_decay, axis=1)
-    tail_dev = jnp.where(
-        (segments == segments[-1])[None, :], jnp.exp(total_log[:, -1:] - total_log), 0.0
-    )
-    local_state = jnp.einsum(
-        "shn,shp->hnp", keys_wide * tail_dev.T[:, :, None], vals_wide, precision=PRECISE
-    )
-    carry_dev = jnp.where(segments[-1] == seg_before, jnp.exp(total_log[:, -1]), 0.0)
-    entry_state, all_scales = entry_of(local_state, carry_dev, None)
-    count_blocks = frames // BLK
-    saved_blocks = []
-    outputs = []
-    run_state = entry_state
-    for number in range(count_blocks):
-        block_start = number * BLK
-        rows_here = slice(block_start, block_start + BLK)
-        if number == 0:
-            seg_prior = seg_before
-        else:
-            seg_prior = segments[block_start - 1]
-        within, entering, leaving = block_weights(
-            log_decay[:, rows_here], segments[rows_here], seg_prior
-        )
-        scores = jnp.einsum(
-            "thn,shn->hts",
-            state_query[rows_here],
-            state_keys[rows_here],
-            preferred_element_type=jnp.float32,
-        )
-        mixed_low = (within * scores).astype(jnp.bfloat16)
-        inner_part = jnp.einsum(
-            "hts,shp->thp", mixed_low, state_vals[rows_here], preferred_element_type=jnp.float32
-        )
-        carried = jnp.einsum(
-            "thn,hnp->thp",
-            query_wide[rows_here] * entering.T[:, :, None],
-            run_state,
-            precision=PRECISE,
-        )
-        outputs.append(inner_part + carried)
-        saved_blocks.append((within, entering, leaving, mixed_low, run_state))
-        run_state = (
-            jnp.einsum(
-                "shn,shp->hnp",
-                keys_wide[rows_here] * leaving.T[:, :, None],
-                vals_wide[rows_here],
-                precision=PRECISE,
-            )
-            + entering[:, -1][:, None, None] * run_state
-        )
-    low_y = jnp.concatenate(outputs, axis=0).reshape(frames, H * P_SIZE).astype(jnp.bfloat16)
+    state_vals = raw_vals * live_mask
+    places = jnp.concatenate([starts, jnp.reshape(first_frame, (1,))]).astype(jnp.int32)
+    summary = state_summary(places, decays[0], key_query, state_vals, False)
+    entry_state, all_scales = entry_of(summary, None)
+    low_y, saved_states = mix_states(places, decays[0], key_query, state_vals, entry_state)
     after_b = after_a + product(low_y, w_output)
     normed_c_out, unit_c, inverse_c = layer_norm(after_b, norm_gains[2], norm_shifts[2])
     low_c = normed_c_out.astype(jnp.bfloat16)
@@ -669,70 +873,13 @@
     grad_b = grad_c + grad_in_c
     output_in = grad_b.astype(jnp.bfloat16)
     grad_w_output = weight_grad(low_y, output_in)
-    grad_y = input_grad(output_in, w_output).astype(jnp.bfloat16).reshape(frames, H, P_SIZE)
-    grad_y_wide = grad_y.astype(jnp.float32)
-    entering_dev = jnp.where((segments == seg_before)[None, :], jnp.exp(total_log), 0.0)
-    local_back = jnp.einsum(
-        "thn,thp->hnp", query_wide * entering_dev.T[:, :, None], grad_y_wide, precision=PRECISE
-    )
-    exit_grad, _ = entry_of(local_back, carry_dev, all_scales)
-    incoming = exit_grad
-    vals_parts = []
-    keys_parts = []
-    query_parts = []
-    for number in reversed(range(count_blocks)):
-        block_start = number * BLK
-        rows_here = slice(block_start, block_start + BLK)
-        within, entering, leaving, mixed_low, prior_state = saved_blocks[number]
-        grad_blk = grad_y[rows_here]
-        grad_blk_wide = grad_y_wide[rows_here]
-        grad_mixed = jnp.einsum(
-            "thp,shp->hts", grad_blk, state_vals[rows_here], preferred_element_type=jnp.float32
-        )
-        grad_vals = jnp.einsum(
-            "hts,thp->shp", mixed_low, grad_blk, preferred_element_type=jnp.float32
-        )
-        grad_scores = (within * grad_mixed).astype(jnp.bfloat16)
-        grad_query = jnp.einsum(
-            "hts,shn->thn", grad_scores, state_keys[rows_here], preferred_element_type=jnp.float32
-        )
-        grad_keys = jnp.einsum(
-            "hts,thn->shn", grad_scores, state_query[rows_here], preferred_element_type=jnp.float32
-        )
-        grad_query = grad_query + entering.T[:, :, None] * jnp.einsum(
-            "thp,hnp->thn", grad_blk_wide, prior_state, precision=PRECISE
-        )
-        grad_vals = grad_vals + jnp.einsum(
-            "shn,hnp->shp",
-            keys_wide[rows_here] * leaving.T[:, :, None],
-            incoming,
-            precision=PRECISE,
-        )
-        grad_keys = grad_keys + leaving.T[:, :, None] * jnp.einsum(
-            "shp,hnp->shn", vals_wide[rows_here], incoming, precision=PRECISE
-        )
-        incoming = (
-            jnp.einsum(
-                "thn,thp->hnp",
-                query_wide[rows_here] * entering.T[:, :, None],
-                grad_blk_wide,
-                precision=PRECISE,
-            )
-            + entering[:, -1][:, None, None] * incoming
-        )
-        vals_parts.insert(0, grad_vals)
-        keys_parts.insert(0, grad_keys)
-        query_parts.insert(0, grad_query)
-    grad_v_low = (
-        jnp.concatenate(vals_parts, axis=0).reshape(frames, D) * live_mask.astype(jnp.float32)
-    ).astype(jnp.bfloat16)
-    grad_kq_low = jnp.concatenate(
-        [
-            jnp.concatenate(keys_parts, axis=0).reshape(frames, H * NS),
-            jnp.concatenate(query_parts, axis=0).reshape(frames, H * NS),
-        ],
-        axis=1,
-    ).astype(jnp.bfloat16)
+    grad_y = input_grad(output_in, w_output).astype(jnp.bfloat16)
+    summary = state_summary(places, decays[0], key_query, grad_y, True)
+    exit_grad, _ = entry_of(summary, all_scales)
+    grad_v_low, grad_kq_low = unmix_states(
+        places, decays[0], key_query, state_vals, grad_y, saved_states, exit_grad
+    )
+    grad_v_low = grad_v_low * live_mask
     low_b = layer_norm(after_a, norm_gains[1], norm_shifts[1])[0].astype(jnp.bfloat16)
     grad_w_values = weight_grad(low_b, grad_v_low)
     grad_w_states = weight_grad(low_b, grad_kq_low)
@@ -744,11 +891,13 @@
         norm_gains[1],
     )
     grad_a = grad_b + grad_in_b
+    count = lax.axis_size("tm")
+    shards_e = halving_sum(tile_grads_e.reshape(count, 8 * own_rows, D), "tm")
+    grad_a, shards_e = lax.optimization_barrier((grad_a, shards_e))
     grad_start, tile_grads_a, vec_a = ffn_back(
         inputs[0], grad_a, gathered, vector_master, own_rows
     )
     gain_a, shift_a = vec_a[0], vec_a[1]
-    count = lax.axis_size("tm")
     vector_grad = jnp.concatenate(
         [
             jnp.stack(
@@ -777,7 +926,6 @@
     mixers = mixers.reshape(6, count, own_rows, D).transpose(1, 0, 2, 3)
     tail = jnp.zeros((VEC_ROWS - vector_grad.shape[0], D), jnp.float32)
     vectors = jnp.concatenate([vector_grad, tail], axis=0).astype(jnp.bfloat16)
-    shards_e = halving_sum(tile_grads_e.reshape(count, 8 * own_rows, D), "tm")
     shards_m = halving_sum(mixers.reshape(count, 6 * own_rows, D), "tm")
     shards_a = halving_sum(
         jnp.concatenate(

time: 529 us -> 478 us (0.904)
  matrix products: 64 us -> 19.7 us
  Pallas kernels: 151 us -> 182 us
  local copies, waits for them, and re-layouts: 75.2 us -> 49.3 us
  other arithmetic: 92.4 us -> 67.9 us
  waiting for transfers between devices: 78.4 us -> 85.7 us
  starting transfers between devices: 21.8 us -> 27.2 us
    dot_general x24 -> x0, matrix products: 38.4 us -> none  [the longest x2 6.86 us: local(): jnp.einsum('thn,shn->hts', state_query[rows_here], state_keys[rows_here],...]
    pallas_call x0 -> x4, Pallas kernels: none -> 31.5 us  [the longest x1 16.9 us: unmix_states(): pl.pallas_call(unmixing_kernel, grid=(blocks,), out_shape=(jax.ShapeDtype...]
    slice x22 -> x3, local copies, waits for them, and re-layouts: 28.3 us -> 1.45 us  [the longest x2 1.45 us: entry_of(): arrived[:, :128].astype(jnp.float32)]
    concatenate x22, local copies, waits for them, and re-layouts: 0.24 us -> 9.02 us  [local(): vectors = jnp.concatenate([vector_grad, tail], axis=0).astype(jnp.bfloat16)]
    ppermute x15, waiting for transfers between devices: 34.6 us -> 41.9 us  [exchange_bit(): got = lax.ppermute(sent, axis, [(i, i ^ 1 << bit) for i in range(count)])]
    unnamed x304 -> x213, local copies, waits for them, and re-layouts: 18.3 us -> 24.2 us
    reduce_sum x3, other arithmetic: 15.5 us -> 9.69 us  [local(): jnp.sum(grad_conv_wide * padded[kernel_offset:kernel_offset + frames].ast...]
  transfers between devices with their start and end apart: 20 -> 20, of which waited for: 8 -> 11; matrix products, arithmetic and copies ran while one was open for 7% -> 12% of each run, Pallas kernels for 4% -> 8%
where the time goes in v3:
time: 478 us; the launch traced here: 469 us
  Pallas kernels  182 us (38%)
  waiting for transfers between devices  85.7 us (18%)
  other arithmetic  67.9 us (14%)
  local copies, waits for them, and re-layouts  49.3 us (10%)
  starting transfers between devices  27.2 us (6%)
  blocking collectives  21 us (4%)
  matrix products  19.7 us (4%)
  between operations  16.1 us (3%)
    pallas_call x1, Pallas kernels, gather_tiles(): pl.pallas_call(functools.partial(gather_kernel, owners, count), out_shape...  93.4 us
    pallas_call x2, Pallas kernels, ffn_back_call(): pl.pallas_call(functools.partial(back_kernel, steps, last, 4 if last else...  44.6 us
    reduce_scatter x1, waiting for transfers between devices, local(): lax.psum_scatter(jnp.concatenate([placed, shared], axis=1), 'utt', scatte...  43.8 us
    ppermute x15, waiting for transfers between devices, exchange_bit(): got = lax.ppermute(sent, axis, [(i, i ^ 1 << bit) for i in range(count)])  41.9 us
    unnamed x213, local copies, waits for them, and re-layouts  24.2 us
    reduce_sum x2, other arithmetic, layer_norm(): centered = values - jnp.mean(values, axis=-1, keepdims=True)  21.1 us
    all_gather x2, blocking collectives, entry_of(): arrived = lax.all_gather(summary, 'tm')  21 us
    pallas_call x1, Pallas kernels, unmix_states(): pl.pallas_call(unmixing_kernel, grid=(blocks,), out_shape=(jax.ShapeDtype...  16.9 us
  transfers between devices with their start and end apart: 20, of which 11 were waited for; matrix products, arithmetic and copies ran while one was open for 12% of the time, Pallas kernels for 8%

profile of v3, /device:TPU:0, one launch (start us, length us, event | category | flops | bytes accessed | tf_op | source)
XLA Modules:
  0.0 468.9 jit_solution(15576766256013833800)
XLA Ops:
  7.2 1.3 fusion.162
  8.5 1.8 fusion.161
  12.5 1.8 copy.96
  15.0 93.4 %shard_map.187.ffn_ref.mix_ref = bf16[8,24,64,512]{3,2,1,0:T(8,128)(2,1)S(1)} custom-call(s32[22]{0:T(128)S(1)} %copy-done.15, bf16[8,64,512]{2,1,0:T(8,128)(2,1)S(1)} %bitcast.217), custom_call_target="tpu_custom_call" | custom-call | tf_op jit(solution)/shard_map/pallas_call | solution.py:258
  108.4 4.5 copy-done
  112.9 1.7 fusion.155
  114.8 12.7 %shard_map.188 = (f32[1024,512]{1,0:T(8,128)S(1)}, bf16[1024,512]{1,0:T(8,128)(2,1)S(1)}, bf16[1024,512]{1,0:T(8,128)(2,1)S(1)}) custom-call(bf16[1024,512]{1,0:T(8,128)(2,1)S(1)} %bitcast.215, bf16[8,24,64,512]{3,2,1,0:T(8,128)(2,1)} %copy-done, bf16[8,24,64,512]{3,2,1,0:T(8,128)(2,1)} %copy-done, f32[27,512]{1,0:T(8,128)S(1)} %copy-done.10), custom_call_target="tpu_custom_call" | custom-call | tf_op jit(solution)/shard_map/pallas_call | solution.py:338
  128.2 3.1 shard_map.189
  132.3 9.4 %all-gather = bf16[1152,128]{1,0:T(8,128)(2,1)S(1)} all-gather(bf16[144,128]{1,0:T(8,128)(2,1)S(1)} %shard_map.189), channel_id=2, replica_groups=mesh['utt'=4,'tm'=8] {'tm'}, dimensions={0}, use_global_device_ids=true | all-gather | bytes 331776 | tf_op jit(solution)/shard_map/all_gather | solution.py:747
  142.6 1.1 copy.85
  146.5 1.2 copy-done.2
  147.7 8.6 %shard_map.190 = (bf16[1024,512]{1,0:T(8,128)(2,1)S(1)}, bf16[2,256,512]{2,1,0:T(8,128)(2,1)S(1)}) custom-call(s32[5]{0:T(128)S(1)} %pad_add_fusion.starts_ref, f32[8,1024]{1,0:T(8,128)S(1)} %bitcast.220, bf16[1024,512]{1,0:T(8,128)(2,1)S(1)} %get-tuple-element.26.kq_ref, bf16[1024,512]{1,0:T(8,128)(2,1)S(1)} %copy-done.2, f32[128,128]{1,0:T(8,128)S(1)} %copy.68.entry_ref), custom_call_target="tpu_custom_call" | custom-call | tf_op jit(solution)/shard_map/pallas_call | solution.py:706
  160.2 2.1 multiply_convert_fusion.4
  163.3 2.3 collective-permute-start
  165.6 1.5 collective-permute-start.1
  168.8 20.9 %fusion.153 = (f32[1024]{0:T(1024)S(1)}, f32[1024,512]{1,0:T(8,128)S(1)}) fusion(f32[1024]{0:T(1024)S(1)} %get-tuple-element.120, bf16[7,512]{1,0:T(8,128)(2,1)S(1)} %collective-permute-done.1, bf16[1024,512]{1,0:T(8,128)(2,1)} %copy-done.21, f32[512]{0:T(512)S(1)} %bitcast.273, f32[1024]{0:T(1024)S(1)} %get-tuple-element.121, f32[512]{0:T(512)S(1)} %bitcast.275, ...), kind=kLoop, calls=%fused_computation.362 | loop fusion | flops 53476352 | bytes 3256320 | tf_op jit(solution)/shard_map/reduce_sum | solution.py:64
  191.4 24.8 %shard_map.191 = (bf16[1024,512]{1,0:T(8,128)(2,1)}, f32[1024,512]{1,0:T(8,128)S(1)}, bf16[8,8,64,512]{3,2,1,0:T(8,128)(2,1)}, f32[8,512]{1,0:T(8,128)S(1)}) custom-call(f32[1024,512]{1,0:T(8,128)S(1)} %convolution_add_fusion.2.x_ref, bf16[1024,512]{1,0:T(8,128)(2,1)S(1)} %bitcast.218, bf16[8,24,64,512]{3,2,1,0:T(8,128)(2,1)} %copy-done, ...), custom_call_target="tpu_custom_call" | custom-call | tf_op jit(solution)/shard_map/pallas_call | solution.py:437
  216.2 2.1 convolution_convert_fusion.1
  218.3 1.8 multiply_reduce_fusion
  220.7 5.1 %fusion.76 = (bf16[512]{0:T(512)(128)(2,1)S(1)}, bf16[512]{0:T(512)(128)(2,1)S(1)}, bf16[512]{0:T(512)(128)(2,1)S(1)}, bf16[512]{0:T(512)(128)(2,1)S(1)}, bf16[5...) fusion(bf16[7,512]{1,0:T(8,128)(2,1)S(1)} %collective-permute-done.1, ...), kind=kLoop, calls=%fused_computation.141 | loop fusion | flops 26735616 | bytes 6347776 | tf_op jit(solution)/shard_map/reduce_sum | solution.py:856
  225.9 1.3 collective-permute-start.2
  227.2 5.2 %collective-permute-start.3 = (bf16[7,512]{1,0:T(8,128)(2,1)S(1)}, bf16[7,512]{1,0:T(8,128)(2,1)S(1)}, u32[]{:S(2)}, u32[]{:S(2)}) collective-permute-start(bf16[7,512]{1,0:T(8,128)(2,1)S(1)} %get-tuple-element.95), channel_id=1, source_target_pairs={{0,1},{1,2},{2,3},{3,4},{4,5},{5,6},{6,7},{8,9},{9,10},{10,11},{11... | collective-permute-start | bytes 21512 | tf_op jit(solution)/shard_map/ppermute | solution.py:38
  232.4 1.9 fusion.74
  234.3 2.7 fusion.60
  237.0 1.5 dynamic-slice_bitcast_fusion
  247.3 1.7 collective-permute-start.4
  249.1 7.5 %multiply_convert_fusion.1 = (bf16[1024,512]{1,0:T(8,128)(2,1)S(1)}, f32[1024,512]{1,0:T(8,128)S(1)}) fusion(f32[1024,512]{1,0:T(8,128)S(1)} %copy-done.24, f32[1024]{0:T(1024)S(1)} %get-tuple-element.119, bf16[1024,512]{1,0:T(8,128)(2,1)S(1)} %get-tuple-element.77, bf16[7,512]{1,0:T(8,128)(2,1)S(1)} %collective-permute-done.3, f32[512]{0:T(512)S(1)} %bitcast.274, ...), kind=kLoop, calls=%fused_computation.153 | loop fusion | flops 54001664 | bytes 6397952 | tf_op jit(solution)/shard_map/convert_element_type | solution.py:863
  259.4 2.0 multiply_reduce_fusion.1
  262.7 1.5 convolution_convert_fusion.4
  265.0 2.9 shard_map.192
  268.8 11.6 %all-gather.1 = bf16[1152,128]{1,0:T(8,128)(2,1)S(1)} all-gather(bf16[144,128]{1,0:T(8,128)(2,1)S(1)} %shard_map.192), channel_id=3, replica_groups=mesh['utt'=4,'tm'=8] {'tm'}, dimensions={0}, use_global_device_ids=true | all-gather | bytes 331776 | tf_op jit(solution)/shard_map/all_gather | solution.py:747
  281.1 1.1 copy.86
  283.9 1.2 copy-done.3
  285.1 1.2 copy-done.5
  286.3 1.0 copy-done.14
  287.4 16.9 %shard_map.193 = (bf16[1024,512]{1,0:T(8,128)(2,1)S(1)}, bf16[1024,512]{1,0:T(8,128)(2,1)S(1)}) custom-call(s32[5]{0:T(128)S(1)} %pad_add_fusion.starts_ref, f32[8,1024]{1,0:T(8,128)S(1)} %bitcast.222, bf16[1024,512]{1,0:T(8,128)(2,1)S(1)} %get-tuple-element.26.kq_ref, bf16[1024,512]{1,0:T(8,128)(2,1)S(1)} %copy-done.3, bf16[1024,512]{1,0:T(8,128)(2,1)S(1)} %copy-done.5, ...), custom_call_target="tpu_custom_call" | custom-call | tf_op jit(solution)/shard_map/pallas_call | solution.py:724
  304.3 1.2 convolution_convert_fusion.6
  305.5 1.1 convolution_convert_fusion.5
  310.5 1.3 dynamic-slice_bitcast_fusion.1
  313.2 1.5 multiply_reduce_fusion.2
  315.4 2.3 fusion.37
  318.0 2.1 collective-permute-start.7
  320.0 12.0 %collective-permute-done.5 = bf16[2,1,256,512]{3,2,1,0:T(8,128)(2,1)S(1)} collective-permute-done((bf16[2,1,256,512]{3,2,1,0:T(8,128)(2,1)S(1)}, bf16[2,1,256,512]{3,2,1,0:T(8,128)(2,1)S(1)}, u32[]{:S(2)}, u32[]{:S(2)}) %collective-permute-start.5) | collective-permute-done | bytes 524320 | tf_op jit(solution)/shard_map/ppermute | solution.py:127
  332.8 1.8 collective-permute-start.8
  335.6 4.4 collective-permute-done.6
  341.6 19.8 %shard_map.194 = (f32[1024,512]{1,0:T(8,128)}, bf16[8,8,64,512]{3,2,1,0:T(8,128)(2,1)}, f32[8,512]{1,0:T(8,128)S(1)}) custom-call(bf16[1024,512]{1,0:T(8,128)(2,1)S(1)} %bitcast.216, f32[1024,512]{1,0:T(8,128)S(1)} %multiply_add_fusion.grad_ref, bf16[8,24,64,512]{3,2,1,0:T(8,128)(2,1)} %copy-done, f32[27,512]{1,0:T(8,128)S(1)} %copy-done.10), custom_call_target="tpu_custom_call" | custom-call | tf_op jit(solution)/shard_map/pallas_call | solution.py:437
  361.8 3.1 fusion.4
  365.8 2.3 fusion.77
  368.3 1.5 collective-permute-start.15
  370.6 9.3 %collective-permute-done.15 = bf16[2,1,192,512]{3,2,0,1:T(8,128)(2,1)S(1)} collective-permute-done((bf16[2,1,192,512]{3,2,0,1:T(8,128)(2,1)S(1)}, bf16[2,1,192,512]{3,2,0,1:T(8,128)(2,1)S(1)}, u32[]{:S(2)}, u32[]{:S(2)}) %collective-permute-start.15) | collective-permute-done | bytes 393248 | tf_op jit(solution)/shard_map/ppermute | solution.py:127
  380.0 1.5 collective-permute-start.16
  382.4 2.2 fusion.7
  384.8 1.5 collective-permute-start.12
  386.7 1.6 collective-permute-start.10
  388.4 10.1 %collective-permute-done.12 = bf16[1,2,272,512]{3,2,1,0:T(8,128)(2,1)S(1)} collective-permute-done((bf16[1,2,272,512]{3,2,1,0:T(8,128)(2,1)S(1)}, bf16[1,2,272,512]{3,2,1,0:T(8,128)(2,1)S(1)}, u32[]{:S(2)}, u32[]{:S(2)}) %collective-permute-start.12) | collective-permute-done | bytes 557088 | tf_op jit(solution)/shard_map/ppermute | solution.py:127
  398.7 1.5 collective-permute-start.13
  400.7 1.5 collective-permute-start.11
  402.2 3.8 collective-permute-done.13
  406.1 1.2 collective-permute-done.11
  407.6 2.0 gather_fusion
  409.7 3.1 pad_maximum_fusion
  412.8 43.8 %reduce-scatter.2.cloned.1.call-done = bf16[1,544,512]{2,1,0:T(8,128)(2,1)} async-done(((bf16[4,544,512]{2,1,0:T(8,128)(2,1)}), bf16[1,544,512]{2,1,0:T(8,128)(2,1)}) %reduce-scatter.2.cloned.1.call-update) | async-done | bytes 557072 | tf_op jit(solution)/shard_map/reduce_scatter | solution.py:957
  456.6 1.3 convert_element_type.597
  458.8 3.0 fusion.149
  (360 shorter events, 48.6 us)
Async XLA Ops:
  7.2 449.4 %reduce-scatter.2.cloned.1.call-start = ((), (), s32[]{:S(2)}) async-start(), calls=%async_computation.1 | async-start | bytes 2785280 | tf_op jit(solution)/shard_map/reduce_scatter | solution.py:957
  10.3 132.2 %copy-start.97 = (pred[8]{0:T(512)(128)(4,1)}, pred[8]{0:T(512)(128)(4,1)S(1)}, u32[]{:S(2)}) copy-start(pred[8]{0:T(512)(128)(4,1)S(1)} %get-tuple-element.147) | copy-start | bytes 28
  11.2 97.2 %copy-start.100 = (s32[4,1]{0,1:T(1,128)}, s32[4,1]{0,1:T(1,128)S(1)}, u32[]{:S(2)}) copy-start(s32[4,1]{0,1:T(1,128)S(1)} %reduce-window.4) | copy-start | bytes 52
  12.5 115.0 %copy-start.55 = (bf16[1024]{0:T(1024)(128)(2,1)}, bf16[1024]{0:T(1024)(128)(2,1)S(1)}, u32[]{:S(2)}) copy-start(bf16[1024]{0:T(1024)(128)(2,1)S(1)} %convert_reduce_fusion.2) | copy-start | bytes 6148
  108.4 4.5 copy-start
  147.7 8.6 %copy-start.27 = (bf16[8,1,64,512]{3,2,1,0:T(8,128)(2,1)S(1)}, bf16[8,1,64,512]{3,2,1,0:T(8,128)(2,1)}, u32[]{:S(2)}) copy-start(bf16[8,1,64,512]{3,2,1,0:T(8,128)(2,1)} %get-tuple-element.87) | copy-start | bytes 1572868
  160.2 6.8 %copy-start.99 = (s32[1,4]{1,0:T(1,128)S(1)}, s32[1,4]{1,0:T(1,128)}, u32[]{:S(2)}) copy-start(s32[1,4]{1,0:T(1,128)} %param.15) | copy-start | bytes 52
  160.2 6.8 %copy-start.101 = (s32[4,1]{0,1:T(1,128)S(1)}, s32[4,1]{0,1:T(1,128)}, u32[]{:S(2)}) copy-start(s32[4,1]{0,1:T(1,128)} %copy-done.100) | copy-start | bytes 52
  163.3 5.3 %collective-permute-start = (bf16[7,512]{1,0:T(8,128)(2,1)S(1)}, bf16[7,512]{1,0:T(8,128)(2,1)S(1)}, u32[]{:S(2)}, u32[]{:S(2)}) collective-permute-start(bf16[7,512]{1,0:T(8,128)(2,1)S(1)} %get-tuple-element.96), channel_id=1, source_target_pairs={{0,1},{1,2},{2,3},{3,4},{4,5},{5,6},{6,7},{8,9},{9,10},{10,11},{11... | collective-permute-start | bytes 21512 | tf_op jit(solution)/shard_map/ppermute | solution.py:38
  165.6 3.1 collective-permute-start.1
  168.8 21.4 %copy-start.18 = (f32[1024,512]{1,0:T(8,128)S(1)}, f32[1024,512]{1,0:T(8,128)}, u32[]{:S(2)}) copy-start(f32[1024,512]{1,0:T(8,128)} %copy-done.17) | copy-start | bytes 6291460
  168.8 21.4 %copy-start.50 = (bf16[8,1,64,512]{3,2,1,0:T(8,128)(2,1)S(1)}, bf16[8,1,64,512]{3,2,1,0:T(8,128)(2,1)}, u32[]{:S(2)}) copy-start(bf16[8,1,64,512]{3,2,1,0:T(8,128)(2,1)} %get-tuple-element.84) | copy-start | bytes 1572868
  168.8 21.4 %copy-start.73 = (f32[1,512]{1,0:T(1,128)S(1)}, f32[1,512]{1,0:T(1,128)}, u32[]{:S(2)}) copy-start(f32[1,512]{1,0:T(1,128)} %get-tuple-element.101) | copy-start | bytes 6148
  168.8 21.4 %copy-start.96 = (f32[1,512]{1,0:T(1,128)S(1)}, f32[1,512]{1,0:T(1,128)}, u32[]{:S(2)}) copy-start(f32[1,512]{1,0:T(1,128)} %get-tuple-element.100) | copy-start | bytes 6148
  225.9 23.2 %collective-permute-start.2 = (bf16[7,512]{1,0:T(8,128)(2,1)S(1)}, bf16[7,512]{1,0:T(8,128)(2,1)S(1)}, u32[]{:S(2)}, u32[]{:S(2)}) collective-permute-start(bf16[7,512]{1,0:T(8,128)(2,1)S(1)} %get-tuple-element.94), channel_id=1, source_target_pairs={{1,0},{2,1},{3,2},{4,3},{5,4},{6,5},{7,6},{9,8},{10,9},{11,10},{12... | collective-permute-start | bytes 21512 | tf_op jit(solution)/shard_map/ppermute | solution.py:40
  227.2 9.8 %copy-start.35 = (bf16[8,8,64,512]{3,2,1,0:T(8,128)(2,1)S(1)}, bf16[8,8,64,512]{3,2,1,0:T(8,128)(2,1)}, u32[]{:S(2)}) copy-start(bf16[8,8,64,512]{3,2,1,0:T(8,128)(2,1)} %get-tuple-element.34) | copy-start | bytes 12582916
  227.2 21.9 %collective-permute-start.3 = (bf16[7,512]{1,0:T(8,128)(2,1)S(1)}, bf16[7,512]{1,0:T(8,128)(2,1)S(1)}, u32[]{:S(2)}, u32[]{:S(2)}) collective-permute-start(bf16[7,512]{1,0:T(8,128)(2,1)S(1)} %get-tuple-element.95), channel_id=1, source_target_pairs={{0,1},{1,2},{2,3},{3,4},{4,5},{5,6},{6,7},{8,9},{9,10},{10,11},{11... | collective-permute-start | bytes 21512 | tf_op jit(solution)/shard_map/ppermute | solution.py:38
  237.0 12.1 %copy-start.24 = (f32[1024,512]{1,0:T(8,128)S(1)}, f32[1024,512]{1,0:T(8,128)}, u32[]{:S(2)}) copy-start(f32[1024,512]{1,0:T(8,128)} %copy-done.23) | copy-start | bytes 6291460
  247.3 9.3 %copy-start.26 = (f32[1024,512]{1,0:T(8,128)S(1)}, f32[1024,512]{1,0:T(8,128)}, u32[]{:S(2)}) copy-start(f32[1024,512]{1,0:T(8,128)} %get-tuple-element.143) | copy-start | bytes 6291460
  247.3 67.3 %collective-permute-start.4 = (bf16[4,1,512,512]{3,2,0,1:T(8,128)(2,1)}, bf16[4,1,512,512]{3,2,0,1:T(8,128)(2,1)}, u32[]{:S(2)}, u32[]{:S(2)}) collective-permute-start(bf16[4,1,512,512]{3,2,0,1:T(8,128)(2,1)} %dynamic-slice_bitcast_fusion), channel_id=1, source_target_pairs={{0,1},{1,0},{2,3},{3,2},{4,5},{5,4},{6,7},{7,6},{8,9},{9,8},{10,11... | collective-permute-start | bytes 6291464 | tf_op jit(solution)/shard_map/ppermute | solution.py:127
  258.0 3.4 copy-start.33
  282.2 22.1 %copy-start.54 = (f32[1,512]{1,0:T(1,128)S(1)}, f32[1,512]{1,0:T(1,128)}, u32[]{:S(2)}) copy-start(f32[1,512]{1,0:T(1,128)} %get-tuple-element.99) | copy-start | bytes 6148
  282.2 22.1 %copy-start.56 = (bf16[1024]{0:T(1024)(128)(2,1)S(1)}, bf16[1024]{0:T(1024)(128)(2,1)}, u32[]{:S(2)}) copy-start(bf16[1024]{0:T(1024)(128)(2,1)} %copy-done.55) | copy-start | bytes 6148
  282.2 22.1 %copy-start.95 = (f32[1,512]{1,0:T(1,128)S(1)}, f32[1,512]{1,0:T(1,128)}, u32[]{:S(2)}) copy-start(f32[1,512]{1,0:T(1,128)} %get-tuple-element.98) | copy-start | bytes 6148
  311.7 54.1 %collective-permute-start.14 = (bf16[4,1,384,512]{3,2,0,1:T(8,128)(2,1)}, bf16[4,1,384,512]{3,2,0,1:T(8,128)(2,1)}, u32[]{:S(2)}, u32[]{:S(2)}) collective-permute-start(bf16[4,1,384,512]{3,2,0,1:T(8,128)(2,1)} %dynamic-slice_bitcast_fusion.1), channel_id=1, source_target_pairs={{0,1},{1,0},{2,3},{3,2},{4,5},{5,4},{6,7},{7,6},{8,9},{9,8},{10,11... | collective-permute-start | bytes 4718600 | tf_op jit(solution)/shard_map/ppermute | solution.py:127
  317.8 14.2 %collective-permute-start.5 = (bf16[2,1,256,512]{3,2,1,0:T(8,128)(2,1)S(1)}, bf16[2,1,256,512]{3,2,1,0:T(8,128)(2,1)S(1)}, u32[]{:S(2)}, u32[]{:S(2)}) collective-permute-start(bf16[2,1,256,512]{3,2,1,0:T(8,128)(2,1)S(1)} %dynamic-slice_bitcast_fusion.5), channel_id=1, source_target_pairs={{0,2},{1,3},{2,0},{3,1},{4,6},{5,7},{6,4},{7,5},{8,10},{9,11},{10,... | collective-permute-start | bytes 1572872 | tf_op jit(solution)/shard_map/ppermute | solution.py:127
  318.0 14.6 %collective-permute-start.7 = (bf16[1,2,256,512]{3,2,1,0:T(8,128)(2,1)S(1)}, bf16[1,2,256,512]{3,2,1,0:T(8,128)(2,1)S(1)}, u32[]{:S(2)}, u32[]{:S(2)}) collective-permute-start(bf16[1,2,256,512]{3,2,1,0:T(8,128)(2,1)S(1)} %dynamic-slice_bitcast_fusion.4), channel_id=1, source_target_pairs={{0,4},{1,5},{2,6},{3,7},{4,0},{5,1},{6,2},{7,3},{8,12},{9,13},{10,... | collective-permute-start | bytes 1572872 | tf_op jit(solution)/shard_map/ppermute | solution.py:127
  320.0 14.6 %copy-start.20 = (f32[1024,512]{1,0:T(8,128)S(1)}, f32[1024,512]{1,0:T(8,128)}, u32[]{:S(2)}) copy-start(f32[1024,512]{1,0:T(8,128)} %copy-done.19) | copy-start | bytes 6291460
  332.3 7.8 %collective-permute-start.6 = (bf16[1,1,256,512]{3,2,1,0:T(8,128)(2,1)S(1)}, bf16[1,1,256,512]{3,2,1,0:T(8,128)(2,1)S(1)}, u32[]{:S(2)}, u32[]{:S(2)}) collective-permute-start(bf16[1,1,256,512]{3,2,1,0:T(8,128)(2,1)S(1)} %constant_dynamic-slice_fusion.5), channel_id=1, source_target_pairs={{0,4},{1,5},{2,6},{3,7},{4,0},{5,1},{6,2},{7,3},{8,12},{9,13},{10,... | collective-permute-start | bytes 786440 | tf_op jit(solution)/shard_map/ppermute | solution.py:127
  332.8 7.7 %collective-permute-start.8 = (bf16[1,1,256,512]{3,2,1,0:T(8,128)(2,1)S(1)}, bf16[1,1,256,512]{3,2,1,0:T(8,128)(2,1)S(1)}, u32[]{:S(2)}, u32[]{:S(2)}) collective-permute-start(bf16[1,1,256,512]{3,2,1,0:T(8,128)(2,1)S(1)} %constant_dynamic-slice_fusion.4), channel_id=1, source_target_pairs={{0,2},{1,3},{2,0},{3,1},{4,6},{5,7},{6,4},{7,5},{8,10},{9,11},{10,... | collective-permute-start | bytes 786440 | tf_op jit(solution)/shard_map/ppermute | solution.py:127
  335.5 5.9 %copy-start.9 = (bf16[1,1024,512]{2,1,0:T(8,128)(2,1)S(1)}, bf16[1,1024,512]{2,1,0:T(8,128)(2,1)}, u32[]{:S(2)}) copy-start(bf16[1,1024,512]{2,1,0:T(8,128)(2,1)} %param.12) | copy-start | bytes 3145732
  341.5 20.0 %copy-start.75 = (bf16[1,512]{1,0:T(2,128)(2,1)S(1)}, bf16[1,512]{1,0:T(2,128)(2,1)}, u32[]{:S(2)}) copy-start(bf16[1,512]{1,0:T(2,128)(2,1)} %concatenate.141) | copy-start | bytes 3076
  341.5 20.0 %copy-start.76 = (bf16[1,512]{1,0:T(2,128)(2,1)S(1)}, bf16[1,512]{1,0:T(2,128)(2,1)}, u32[]{:S(2)}) copy-start(bf16[1,512]{1,0:T(2,128)(2,1)} %concatenate.140) | copy-start | bytes 3076
  341.5 20.0 %copy-start.77 = (bf16[1,512]{1,0:T(2,128)(2,1)S(1)}, bf16[1,512]{1,0:T(2,128)(2,1)}, u32[]{:S(2)}) copy-start(bf16[1,512]{1,0:T(2,128)(2,1)} %concatenate.133) | copy-start | bytes 3076
  341.5 20.0 %copy-start.78 = (bf16[1,512]{1,0:T(2,128)(2,1)S(1)}, bf16[1,512]{1,0:T(2,128)(2,1)}, u32[]{:S(2)}) copy-start(bf16[1,512]{1,0:T(2,128)(2,1)} %concatenate.135) | copy-start | bytes 3076
  341.5 20.0 %copy-start.79 = (bf16[1,512]{1,0:T(2,128)(2,1)S(1)}, bf16[1,512]{1,0:T(2,128)(2,1)}, u32[]{:S(2)}) copy-start(bf16[1,512]{1,0:T(2,128)(2,1)} %concatenate.136) | copy-start | bytes 3076
  341.5 20.0 %copy-start.80 = (bf16[1,512]{1,0:T(2,128)(2,1)S(1)}, bf16[1,512]{1,0:T(2,128)(2,1)}, u32[]{:S(2)}) copy-start(bf16[1,512]{1,0:T(2,128)(2,1)} %concatenate.137) | copy-start | bytes 3076
  341.5 20.0 %copy-start.81 = (bf16[1,512]{1,0:T(2,128)(2,1)S(1)}, bf16[1,512]{1,0:T(2,128)(2,1)}, u32[]{:S(2)}) copy-start(bf16[1,512]{1,0:T(2,128)(2,1)} %concatenate.138) | copy-start | bytes 3076
  341.5 20.0 %copy-start.82 = (bf16[1,512]{1,0:T(2,128)(2,1)S(1)}, bf16[1,512]{1,0:T(2,128)(2,1)}, u32[]{:S(2)}) copy-start(bf16[1,512]{1,0:T(2,128)(2,1)} %concatenate.139) | copy-start | bytes 3076
  341.5 20.0 %copy-start.83 = (bf16[1,512]{1,0:T(2,128)(2,1)S(1)}, bf16[1,512]{1,0:T(2,128)(2,1)}, u32[]{:S(2)}) copy-start(bf16[1,512]{1,0:T(2,128)(2,1)} %concatenate.134) | copy-start | bytes 3076
  341.5 20.0 %copy-start.84 = (bf16[1,512]{1,0:T(2,128)(2,1)S(1)}, bf16[1,512]{1,0:T(2,128)(2,1)}, u32[]{:S(2)}) copy-start(bf16[1,512]{1,0:T(2,128)(2,1)} %concatenate.130) | copy-start | bytes 3076
  341.5 20.0 %copy-start.85 = (bf16[1,512]{1,0:T(2,128)(2,1)S(1)}, bf16[1,512]{1,0:T(2,128)(2,1)}, u32[]{:S(2)}) copy-start(bf16[1,512]{1,0:T(2,128)(2,1)} %concatenate.131) | copy-start | bytes 3076
  341.5 20.0 %copy-start.86 = (bf16[1,512]{1,0:T(2,128)(2,1)S(1)}, bf16[1,512]{1,0:T(2,128)(2,1)}, u32[]{:S(2)}) copy-start(bf16[1,512]{1,0:T(2,128)(2,1)} %concatenate.132) | copy-start | bytes 3076
  341.6 20.0 %copy-start.87 = (bf16[1,512]{1,0:T(2,128)(2,1)S(1)}, bf16[1,512]{1,0:T(2,128)(2,1)}, u32[]{:S(2)}) copy-start(bf16[1,512]{1,0:T(2,128)(2,1)} %concatenate.127) | copy-start | bytes 3076
  341.6 20.0 %copy-start.88 = (bf16[1,512]{1,0:T(2,128)(2,1)S(1)}, bf16[1,512]{1,0:T(2,128)(2,1)}, u32[]{:S(2)}) copy-start(bf16[1,512]{1,0:T(2,128)(2,1)} %concatenate.129) | copy-start | bytes 3076
  341.6 20.0 %copy-start.89 = (bf16[1,512]{1,0:T(2,128)(2,1)S(1)}, bf16[1,512]{1,0:T(2,128)(2,1)}, u32[]{:S(2)}) copy-start(bf16[1,512]{1,0:T(2,128)(2,1)} %concatenate.128) | copy-start | bytes 3076
  341.6 20.0 %copy-start.90 = (bf16[1,512]{1,0:T(2,128)(2,1)S(1)}, bf16[1,512]{1,0:T(2,128)(2,1)}, u32[]{:S(2)}) copy-start(bf16[1,512]{1,0:T(2,128)(2,1)} %get-tuple-element.134) | copy-start | bytes 3076
  341.6 20.0 %copy-start.91 = (bf16[1,512]{1,0:T(2,128)(2,1)S(1)}, bf16[1,512]{1,0:T(2,128)(2,1)}, u32[]{:S(2)}) copy-start(bf16[1,512]{1,0:T(2,128)(2,1)} %get-tuple-element.135) | copy-start | bytes 3076
  341.6 20.0 %copy-start.92 = (bf16[1,512]{1,0:T(2,128)(2,1)S(1)}, bf16[1,512]{1,0:T(2,128)(2,1)}, u32[]{:S(2)}) copy-start(bf16[1,512]{1,0:T(2,128)(2,1)} %get-tuple-element.136) | copy-start | bytes 3076
  341.6 20.0 %copy-start.93 = (bf16[1,512]{1,0:T(2,128)(2,1)S(1)}, bf16[1,512]{1,0:T(2,128)(2,1)}, u32[]{:S(2)}) copy-start(bf16[1,512]{1,0:T(2,128)(2,1)} %get-tuple-element.137) | copy-start | bytes 3076
  364.9 17.4 %collective-permute-start.9 = (bf16[4,1,544,512]{3,2,0,1:T(8,128)(2,1)}, bf16[4,1,544,512]{3,2,0,1:T(8,128)(2,1)}, u32[]{:S(2)}, u32[]{:S(2)}) collective-permute-start(bf16[4,1,544,512]{3,2,0,1:T(8,128)(2,1)} %fusion.4), channel_id=1, source_target_pairs={{0,1},{1,0},{2,3},{3,2},{4,5},{5,4},{6,7},{7,6},{8,9},{9,8},{10,11... | collective-permute-start | bytes 6684680 | tf_op jit(solution)/shard_map/ppermute | solution.py:127
  368.3 14.1 %copy-start.25 = (bf16[8,8,64,512]{3,2,1,0:T(8,128)(2,1)S(1)}, bf16[8,8,64,512]{3,2,1,0:T(8,128)(2,1)}, u32[]{:S(2)}) copy-start(bf16[8,8,64,512]{3,2,1,0:T(8,128)(2,1)} %get-tuple-element.37) | copy-start | bytes 12582916
  368.3 11.6 %collective-permute-start.15 = (bf16[2,1,192,512]{3,2,0,1:T(8,128)(2,1)S(1)}, bf16[2,1,192,512]{3,2,0,1:T(8,128)(2,1)S(1)}, u32[]{:S(2)}, u32[]{:S(2)}) collective-permute-start(bf16[2,1,192,512]{3,2,0,1:T(8,128)(2,1)S(1)} %dynamic-slice_bitcast_fusion.7), channel_id=1, source_target_pairs={{0,2},{1,3},{2,0},{3,1},{4,6},{5,7},{6,4},{7,5},{8,10},{9,11},{10,... | collective-permute-start | bytes 1179656 | tf_op jit(solution)/shard_map/ppermute | solution.py:127
  369.9 11.7 %collective-permute-start.17 = (bf16[1,2,192,512]{3,2,1,0:T(8,128)(2,1)S(1)}, bf16[1,2,192,512]{3,2,1,0:T(8,128)(2,1)S(1)}, u32[]{:S(2)}, u32[]{:S(2)}) collective-permute-start(bf16[1,2,192,512]{3,2,1,0:T(8,128)(2,1)S(1)} %dynamic-slice_bitcast_fusion.6), channel_id=1, source_target_pairs={{0,4},{1,5},{2,6},{3,7},{4,0},{5,1},{6,2},{7,3},{8,12},{9,13},{10,... | collective-permute-start | bytes 1179656 | tf_op jit(solution)/shard_map/ppermute | solution.py:127
  380.0 6.6 %collective-permute-start.16 = (bf16[1,1,192,512]{3,2,0,1:T(8,128)(2,1)S(1)}, bf16[1,1,192,512]{3,2,0,1:T(8,128)(2,1)S(1)}, u32[]{:S(2)}, u32[]{:S(2)}) collective-permute-start(bf16[1,1,192,512]{3,2,0,1:T(8,128)(2,1)S(1)} %constant_dynamic-slice_fusion.1), channel_id=1, source_target_pairs={{0,4},{1,5},{2,6},{3,7},{4,0},{5,1},{6,2},{7,3},{8,12},{9,13},{10,... | collective-permute-start | bytes 589832 | tf_op jit(solution)/shard_map/ppermute | solution.py:127
  381.7 6.5 %collective-permute-start.18 = (bf16[1,1,192,512]{3,2,1,0:T(8,128)(2,1)S(1)}, bf16[1,1,192,512]{3,2,1,0:T(8,128)(2,1)S(1)}, u32[]{:S(2)}, u32[]{:S(2)}) collective-permute-start(bf16[1,1,192,512]{3,2,1,0:T(8,128)(2,1)S(1)} %constant_dynamic-slice_fusion), channel_id=1, source_target_pairs={{0,2},{1,3},{2,0},{3,1},{4,6},{5,7},{6,4},{7,5},{8,10},{9,11},{10,... | collective-permute-start | bytes 589832 | tf_op jit(solution)/shard_map/ppermute | solution.py:127
  384.8 13.7 %collective-permute-start.12 = (bf16[1,2,272,512]{3,2,1,0:T(8,128)(2,1)S(1)}, bf16[1,2,272,512]{3,2,1,0:T(8,128)(2,1)S(1)}, u32[]{:S(2)}, u32[]{:S(2)}) collective-permute-start(bf16[1,2,272,512]{3,2,1,0:T(8,128)(2,1)S(1)} %dynamic-slice_bitcast_fusion.2), channel_id=1, source_target_pairs={{0,4},{1,5},{2,6},{3,7},{4,0},{5,1},{6,2},{7,3},{8,12},{9,13},{10,... | collective-permute-start | bytes 1671176 | tf_op jit(solution)/shard_map/ppermute | solution.py:127
  386.7 13.8 %collective-permute-start.10 = (bf16[2,1,272,512]{3,2,1,0:T(8,128)(2,1)S(1)}, bf16[2,1,272,512]{3,2,1,0:T(8,128)(2,1)S(1)}, u32[]{:S(2)}, u32[]{:S(2)}) collective-permute-start(bf16[2,1,272,512]{3,2,1,0:T(8,128)(2,1)S(1)} %dynamic-slice_bitcast_fusion.3), channel_id=1, source_target_pairs={{0,2},{1,3},{2,0},{3,1},{4,6},{5,7},{6,4},{7,5},{8,10},{9,11},{10,... | collective-permute-start | bytes 1671176 | tf_op jit(solution)/shard_map/ppermute | solution.py:127
  398.7 7.3 %collective-permute-start.13 = (bf16[1,1,272,512]{3,2,1,0:T(8,128)(2,1)S(1)}, bf16[1,1,272,512]{3,2,1,0:T(8,128)(2,1)S(1)}, u32[]{:S(2)}, u32[]{:S(2)}) collective-permute-start(bf16[1,1,272,512]{3,2,1,0:T(8,128)(2,1)S(1)} %constant_dynamic-slice_fusion.2), channel_id=1, source_target_pairs={{0,2},{1,3},{2,0},{3,1},{4,6},{5,7},{6,4},{7,5},{8,10},{9,11},{10,... | collective-permute-start | bytes 835592 | tf_op jit(solution)/shard_map/ppermute | solution.py:127
  400.6 6.8 %copy-start.46 = (bf16[512,512]{1,0:T(8,128)(2,1)S(1)}, bf16[512,512]{1,0:T(8,128)(2,1)}, u32[]{:S(2)}) copy-start(bf16[512,512]{1,0:T(8,128)(2,1)} %pad_maximum_fusion.6) | copy-start | bytes 1572868
  400.7 6.6 %collective-permute-start.11 = (bf16[1,1,272,512]{3,2,1,0:T(8,128)(2,1)S(1)}, bf16[1,1,272,512]{3,2,1,0:T(8,128)(2,1)S(1)}, u32[]{:S(2)}, u32[]{:S(2)}) collective-permute-start(bf16[1,1,272,512]{3,2,1,0:T(8,128)(2,1)S(1)} %constant_dynamic-slice_fusion.3), channel_id=1, source_target_pairs={{0,4},{1,5},{2,6},{3,7},{4,0},{5,1},{6,2},{7,3},{8,12},{9,13},{10,... | collective-permute-start | bytes 835592 | tf_op jit(solution)/shard_map/ppermute | solution.py:127
  412.8 45.1 %copy-start.52 = (f32[27,512]{1,0:T(8,128)S(1)}, f32[27,512]{1,0:T(8,128)}, u32[]{:S(2)}) copy-start(f32[27,512]{1,0:T(8,128)} %param.22) | copy-start | bytes 165892
  412.8 45.2 %copy-start.53 = (f32[27,512]{1,0:T(8,128)S(1)}, f32[27,512]{1,0:T(8,128)}, u32[]{:S(2)}) copy-start(f32[27,512]{1,0:T(8,128)} %param.23) | copy-start | bytes 165892
  412.8 46.0 %copy-start.37 = (f32[64,8,512]{2,1,0:T(8,128)S(1)}, f32[64,8,512]{2,1,0:T(8,128)}, u32[]{:S(2)}) copy-start(f32[64,8,512]{2,1,0:T(8,128)} %param.18) | copy-start | bytes 3145732
  (58 other events, 81.7 us)
Sparse Core Ops, SparseCore 0:
  413.0 43.6 reduce-scatter.1
